TPU v7x, 16 devices: a whole 2x2x2 slice. The times are simulated.
16 devices in a mesh: tp: 4 (over z, y), cp: 4 (over x, core).
Axes of the slice: x: 2, y: 2, z: 2, core: 2. Of those that a mesh axis runs over, the one named last changes fastest.
Arguments:
- x_in: bfloat16 [8, 512, 1024], P(None, 'cp')
- d_y: bfloat16 [8, 512, 1024], P(None, 'cp')
- key_mask: int32 [8, 512], P(None, 'cp')
- rel_bias: float32 [32, 16], P(None, 'tp')
- g_attn: float32 [2, 1024], replicated
- g_mlp: float32 [2, 1024], replicated
- w_q: bfloat16 [2, 1024, 1024], P(None, None, 'tp')
- w_k: bfloat16 [2, 1024, 1024], P(None, None, 'tp')
- w_v: bfloat16 [2, 1024, 1024], P(None, None, 'tp')
- w_o: bfloat16 [2, 1024, 1024], P(None, 'tp')
- w_gate: bfloat16 [2, 1024, 2816], P(None, None, 'tp')
- w_lin: bfloat16 [2, 1024, 2816], P(None, None, 'tp')
- w_out: bfloat16 [2, 2816, 1024], P(None, 'tp')
Outputs:
- output 1: bfloat16 [8, 512, 1024], P(None, 'cp')
- output 2: float32 [32, 16], P(None, 'tp')
- output 3: float32 [2, 1024], replicated
- output 4: float32 [2, 1024], replicated
- output 5: bfloat16 [2, 1024, 1024], P(None, None, 'tp')
- output 6: bfloat16 [2, 1024, 1024], P(None, None, 'tp')
- output 7: bfloat16 [2, 1024, 1024], P(None, None, 'tp')
- output 8: bfloat16 [2, 1024, 1024], P(None, 'tp')
- output 9: bfloat16 [2, 1024, 2816], P(None, None, 'tp')
- output 10: bfloat16 [2, 1024, 2816], P(None, None, 'tp')
- output 11: bfloat16 [2, 2816, 1024], P(None, 'tp')
All inputs are finite; a program needn't handle non-finite values.
Results may differ from a plain program's by a relative error of at most 0.02.
Values are sent between devices in bfloat16 or wider.
A program may use at most 1 GiB of HBM per device.

v0:
```python
import jax
import jax.numpy as jnp
from jax import lax
from jax.sharding import PartitionSpec as P

NORM_EPS = 1e-6
MASK_NEG = -1e9


def rel_bucket(rel_pos):
    distance = jnp.minimum(jnp.abs(rel_pos), 128)
    distance_sq = distance * distance
    log_part = 8 + sum((distance_sq >= 64 * 2 ** power).astype(jnp.int32) for power in range(1, 8))
    return jnp.where(distance < 8, distance, log_part) + 16 * (rel_pos > 0).astype(jnp.int32)


def pair_bias(bias_table, q_block, k_block, blk_len):
    offsets = jnp.arange(blk_len)
    rel_pos = (k_block - q_block) * blk_len + offsets[None, :] - offsets[:, None]
    buckets = rel_bucket(rel_pos)
    return buckets, jnp.take(bias_table, buckets, axis=1)


def pair_scores(queries, key_blk, bias, key_add):
    scores = jnp.einsum('bqhd,bkhd->bhqk', queries, key_blk, preferred_element_type=jnp.float32)
    return scores + bias[None] + key_add[:, None, None, :]


def softmax_fold(state, queries, key_blk, val_blk, bias, key_add):
    run_max, run_sum, out_acc = state
    scores = pair_scores(queries, key_blk, bias, key_add)
    new_max = jnp.maximum(run_max, jnp.max(scores, axis=-1))
    rescale = jnp.exp(run_max - new_max)
    probs = jnp.exp(scores - new_max[..., None])
    new_sum = run_sum * rescale + jnp.sum(probs, axis=-1)
    weighted = jnp.einsum('bhqk,bkhd->bqhd', probs.astype(jnp.bfloat16), val_blk, preferred_element_type=jnp.float32)
    return new_max, new_sum, out_acc * jnp.transpose(rescale, (0, 2, 1))[..., None] + weighted


def pair_grads(queries, key_blk, val_blk, d_out, log_norm, row_dot, bias_table, key_add_all, q_block, k_block):
    batch, blk_len, heads, _ = queries.shape
    buckets, bias = pair_bias(bias_table, q_block, k_block, blk_len)
    key_add = lax.dynamic_slice_in_dim(key_add_all, k_block * blk_len, blk_len, axis=1)
    probs = jnp.exp(pair_scores(queries, key_blk, bias, key_add) - log_norm[..., None])
    d_probs = jnp.einsum('bqhd,bkhd->bhqk', d_out, val_blk, preferred_element_type=jnp.float32)
    d_scores = probs * (d_probs - row_dot[..., None])
    ds_low = d_scores.astype(jnp.bfloat16)
    dq_part = jnp.einsum('bhqk,bkhd->bqhd', ds_low, key_blk, preferred_element_type=jnp.float32)
    dk_part = jnp.einsum('bhqk,bqhd->bkhd', ds_low, queries, preferred_element_type=jnp.float32)
    dv_part = jnp.einsum('bhqk,bqhd->bkhd', probs.astype(jnp.bfloat16), d_out, preferred_element_type=jnp.float32)
    seg_ids = buckets.reshape(-1)
    n_buckets = bias_table.shape[1]
    bias_part = jax.vmap(lambda score_row: jax.ops.segment_sum(score_row, seg_ids, num_segments=n_buckets))(jnp.sum(d_scores, axis=0).reshape(heads, -1))
    return dq_part, dk_part, dv_part, bias_part


def attn_forward(queries, key_own, val_own, bias_table, key_add_all, cp_index, cp_size):
    batch, blk_len, heads, _ = queries.shape
    shift_pairs = [(device_pos, (device_pos + 1) % cp_size) for device_pos in range(cp_size)]

    def fold_from(state, key_blk, val_blk, k_block):
        _, bias = pair_bias(bias_table, cp_index, k_block, blk_len)
        key_add = lax.dynamic_slice_in_dim(key_add_all, k_block * blk_len, blk_len, axis=1)
        return softmax_fold(state, queries, key_blk, val_blk, bias, key_add)

    start_state = (jnp.full((batch, heads, blk_len), -jnp.inf, jnp.float32), jnp.zeros((batch, heads, blk_len), jnp.float32), jnp.zeros(queries.shape, jnp.float32))
    state = fold_from(start_state, key_own, val_own, cp_index)

    def step_body(step, carry):
        state, key_blk, val_blk = carry
        key_blk = lax.ppermute(key_blk, 'cp', shift_pairs)
        val_blk = lax.ppermute(val_blk, 'cp', shift_pairs)
        state = fold_from(state, key_blk, val_blk, (cp_index - step) % cp_size)
        return state, key_blk, val_blk

    state, _, _ = lax.fori_loop(1, cp_size, step_body, (state, key_own, val_own))
    run_max, run_sum, out_acc = state
    attn_out = out_acc / jnp.transpose(run_sum, (0, 2, 1))[..., None]
    return attn_out.astype(jnp.bfloat16), run_max + jnp.log(run_sum)


def attn_backward(queries, key_own, val_own, attn_out, d_out, log_norm, bias_table, key_add_all, cp_index, cp_size):
    shift_pairs = [(device_pos, (device_pos + 1) % cp_size) for device_pos in range(cp_size)]
    row_dot = jnp.einsum('bqhd,bqhd->bhq', d_out, attn_out, preferred_element_type=jnp.float32)

    def grads_from(key_blk, val_blk, k_block):
        return pair_grads(queries, key_blk, val_blk, d_out, log_norm, row_dot, bias_table, key_add_all, cp_index, k_block)

    dq_acc, dk_acc, dv_acc, bias_acc = grads_from(key_own, val_own, cp_index)

    def step_body(step, carry):
        dq_acc, bias_acc, key_blk, val_blk, dk_acc, dv_acc = carry
        key_blk = lax.ppermute(key_blk, 'cp', shift_pairs)
        val_blk = lax.ppermute(val_blk, 'cp', shift_pairs)
        dk_acc = lax.ppermute(dk_acc, 'cp', shift_pairs)
        dv_acc = lax.ppermute(dv_acc, 'cp', shift_pairs)
        dq_part, dk_part, dv_part, bias_part = grads_from(key_blk, val_blk, (cp_index - step) % cp_size)
        return dq_acc + dq_part, bias_acc + bias_part, key_blk, val_blk, dk_acc + dk_part, dv_acc + dv_part

    dq_acc, bias_acc, _, _, dk_acc, dv_acc = lax.fori_loop(1, cp_size, step_body, (dq_acc, bias_acc, key_own, val_own, dk_acc, dv_acc))
    dk_home = lax.ppermute(dk_acc, 'cp', shift_pairs)
    dv_home = lax.ppermute(dv_acc, 'cp', shift_pairs)
    return dq_acc.astype(jnp.bfloat16), dk_home.astype(jnp.bfloat16), dv_home.astype(jnp.bfloat16), bias_acc


def rms_parts(x_f, gain):
    inv_rms = lax.rsqrt(jnp.mean(x_f * x_f, axis=-1, keepdims=True) + NORM_EPS)
    return inv_rms, (x_f * inv_rms * gain).astype(jnp.bfloat16)


def rms_backward(d_norm, x_f, inv_rms, gain):
    normed = x_f * inv_rms
    d_gain = jnp.sum(d_norm * normed, axis=(0, 1))
    d_normed = d_norm * gain
    d_x = inv_rms * (d_normed - normed * jnp.mean(d_normed * normed, axis=-1, keepdims=True))
    return d_x, d_gain


def layer_forward(x_in, weights, bias_table, key_add_all, cp_index, cp_size):
    g_attn, g_mlp, w_q, w_k, w_v, w_o, w_gate, w_lin, w_out = weights
    batch, blk_len, _ = x_in.shape
    head_shape = (batch, blk_len, bias_table.shape[0], -1)
    x_f = x_in.astype(jnp.float32)
    inv_attn, h_attn = rms_parts(x_f, g_attn)
    queries = jnp.dot(h_attn, w_q, preferred_element_type=jnp.float32).astype(jnp.bfloat16).reshape(head_shape)
    key_own = jnp.dot(h_attn, w_k, preferred_element_type=jnp.float32).astype(jnp.bfloat16).reshape(head_shape)
    val_own = jnp.dot(h_attn, w_v, preferred_element_type=jnp.float32).astype(jnp.bfloat16).reshape(head_shape)
    attn_out, log_norm = attn_forward(queries, key_own, val_own, bias_table, key_add_all, cp_index, cp_size)
    attn_flat = attn_out.reshape(batch, blk_len, -1)
    after_attn = (x_f + lax.psum(jnp.dot(attn_flat, w_o, preferred_element_type=jnp.float32), 'tp')).astype(jnp.bfloat16)
    after_f = after_attn.astype(jnp.float32)
    inv_mlp, h_mlp = rms_parts(after_f, g_mlp)
    gate_pre = jnp.dot(h_mlp, w_gate, preferred_element_type=jnp.float32)
    lin_pre = jnp.dot(h_mlp, w_lin, preferred_element_type=jnp.float32)
    gated = (jax.nn.gelu(gate_pre, approximate=True) * lin_pre).astype(jnp.bfloat16)
    layer_out = (after_f + lax.psum(jnp.dot(gated, w_out, preferred_element_type=jnp.float32), 'tp')).astype(jnp.bfloat16)
    saved = (x_in, inv_attn, h_attn, queries, key_own, val_own, attn_out, log_norm, after_attn, inv_mlp, h_mlp, gate_pre, lin_pre, gated)
    return layer_out, saved


def layer_backward(d_layer, saved, weights, bias_table, key_add_all, cp_index, cp_size):
    g_attn, g_mlp, w_q, w_k, w_v, w_o, w_gate, w_lin, w_out = weights
    x_in, inv_attn, h_attn, queries, key_own, val_own, attn_out, log_norm, after_attn, inv_mlp, h_mlp, gate_pre, lin_pre, gated = saved
    batch, blk_len, _ = x_in.shape
    d_low = d_layer.astype(jnp.bfloat16)
    d_w_out = jnp.einsum('bsf,bsd->fd', gated, d_low, preferred_element_type=jnp.float32)
    d_gated = jnp.einsum('bsd,fd->bsf', d_low, w_out, preferred_element_type=jnp.float32)
    gelu_val, gelu_pull = jax.vjp(lambda gate_in: jax.nn.gelu(gate_in, approximate=True), gate_pre)
    d_lin = (d_gated * gelu_val).astype(jnp.bfloat16)
    d_gate = gelu_pull(d_gated * lin_pre)[0].astype(jnp.bfloat16)
    d_w_gate = jnp.einsum('bsd,bsf->df', h_mlp, d_gate, preferred_element_type=jnp.float32)
    d_w_lin = jnp.einsum('bsd,bsf->df', h_mlp, d_lin, preferred_element_type=jnp.float32)
    d_h_mlp = (jnp.einsum('bsf,df->bsd', d_gate, w_gate, preferred_element_type=jnp.float32)
               + jnp.einsum('bsf,df->bsd', d_lin, w_lin, preferred_element_type=jnp.float32))
    d_mid, d_g_mlp = rms_backward(lax.psum(d_h_mlp, 'tp'), after_attn.astype(jnp.float32), inv_mlp, g_mlp)
    d_mid = d_mid + d_layer
    d_mid_low = d_mid.astype(jnp.bfloat16)
    attn_flat = attn_out.reshape(batch, blk_len, -1)
    d_w_o = jnp.einsum('bsn,bsd->nd', attn_flat, d_mid_low, preferred_element_type=jnp.float32)
    d_out = jnp.einsum('bsd,nd->bsn', d_mid_low, w_o, preferred_element_type=jnp.float32).astype(jnp.bfloat16).reshape(attn_out.shape)
    d_q, d_k, d_v, d_bias = attn_backward(queries, key_own, val_own, attn_out, d_out, log_norm, bias_table, key_add_all, cp_index, cp_size)
    flat_shape = (batch, blk_len, -1)
    d_q = d_q.reshape(flat_shape)
    d_k = d_k.reshape(flat_shape)
    d_v = d_v.reshape(flat_shape)
    d_w_q = jnp.einsum('bsd,bsn->dn', h_attn, d_q, preferred_element_type=jnp.float32)
    d_w_k = jnp.einsum('bsd,bsn->dn', h_attn, d_k, preferred_element_type=jnp.float32)
    d_w_v = jnp.einsum('bsd,bsn->dn', h_attn, d_v, preferred_element_type=jnp.float32)
    d_h_attn = (jnp.einsum('bsn,dn->bsd', d_q, w_q, preferred_element_type=jnp.float32)
                + jnp.einsum('bsn,dn->bsd', d_k, w_k, preferred_element_type=jnp.float32)
                + jnp.einsum('bsn,dn->bsd', d_v, w_v, preferred_element_type=jnp.float32))
    d_x, d_g_attn = rms_backward(lax.psum(d_h_attn, 'tp'), x_in.astype(jnp.float32), inv_attn, g_attn)
    grads = (d_g_attn, d_g_mlp, d_w_q, d_w_k, d_w_v, d_w_o, d_w_gate, d_w_lin, d_w_out)
    return d_x + d_mid, grads, d_bias


def solution(mesh):
    cp_size = mesh.shape['cp']
    seq_spec = P(None, 'cp', None)
    col_spec = P(None, None, 'tp')
    row_spec = P(None, 'tp', None)
    weight_specs = (P(), P(), col_spec, col_spec, col_spec, row_spec, col_spec, col_spec, row_spec)

    def local_program(x_in, d_y, key_mask, rel_bias, g_attn, g_mlp, w_q, w_k, w_v, w_o, w_gate, w_lin, w_out):
        cp_index = lax.axis_index('cp')
        mask_all = lax.all_gather(key_mask, 'cp', axis=1, tiled=True)
        key_add_all = jnp.where(mask_all > 0, 0.0, MASK_NEG).astype(jnp.float32)
        bias_table = rel_bias.T
        stacks = (g_attn, g_mlp, w_q, w_k, w_v, w_o, w_gate, w_lin, w_out)
        layer_weights = [tuple(stack[layer] for stack in stacks) for layer in range(w_q.shape[0])]
        hidden = x_in
        saved_all = []
        for weights in layer_weights:
            hidden, saved = layer_forward(hidden, weights, bias_table, key_add_all, cp_index, cp_size)
            saved_all.append(saved)
        grad = d_y.astype(jnp.float32)
        bias_grad = jnp.zeros(bias_table.shape, jnp.float32)
        layer_grads = []
        for layer in reversed(range(len(layer_weights))):
            grad, grads, d_bias = layer_backward(grad, saved_all[layer], layer_weights[layer], bias_table, key_add_all, cp_index, cp_size)
            layer_grads.insert(0, grads)
            bias_grad = bias_grad + d_bias
        summed = [lax.psum(jnp.stack([grads[which] for grads in layer_grads]), 'cp') for which in range(len(stacks))]
        return tuple([grad.astype(jnp.bfloat16), lax.psum(bias_grad, 'cp').T, summed[0], summed[1]] + [part.astype(jnp.bfloat16) for part in summed[2:]])

    return jax.shard_map(local_program, mesh=mesh, in_specs=(seq_spec, seq_spec, P(None, 'cp'), P(None, 'tp')) + weight_specs, out_specs=(seq_spec, P(None, 'tp')) + weight_specs, check_vma=False)
```

profile of v0, /device:TPU:0, one launch (start us, length us, event | category | flops | bytes accessed | tf_op | source)
XLA Modules:
  0.0 3170.4 jit_solution(7941063508833526916)
XLA Ops:
  95.0 201.2 %while.96 = (s32[]{:T(128)}, f32[8,4,128]{2,1,0:T(4,128)S(1)}, f32[8,4,128]{2,1,0:T(4,128)S(1)}, f32[8,128,4,64]{1,3,2,0:T(8,128)S(1)}, bf16[8,128,4,64]{1,3,2,0...) while((s32[]{:T(128)}, f32[8,4,128]{2,1,0:T(4,128)S(1)}, ...), condition=%wide.region_6.8_spmd, body=%wide.region_3.0_spmd.sunk | while | flops 141734032 | bytes 19093420 | solution.py:76
  97.2 54.8 %gather_fusion = f32[16384,4]{1,0:T(8,128)} fusion(f32[4,32]{0,1:T(8,128)S(1)} %get-tuple-element.1768, s32[16384]{0:T(1024)S(1)} %bitcast_clamp_fusion.9), kind=kCustom, calls=%fused_computation.clone.clone.1 | custom fusion | bytes 589824 | tf_op jit(solution)/shard_map/while/body/eval_jaxpr/jit(_take)/gather | solution.py:21
  163.3 54.8 %gather_fusion = f32[16384,4]{1,0:T(8,128)} fusion(f32[4,32]{0,1:T(8,128)S(1)} %get-tuple-element.1768, s32[16384]{0:T(1024)S(1)} %bitcast_clamp_fusion.9), kind=kCustom, calls=%fused_computation.clone.clone.1 | custom fusion | bytes 589824 | tf_op jit(solution)/shard_map/while/body/eval_jaxpr/jit(_take)/gather | solution.py:21
  230.8 54.8 %gather_fusion = f32[16384,4]{1,0:T(8,128)} fusion(f32[4,32]{0,1:T(8,128)S(1)} %get-tuple-element.1768, s32[16384]{0:T(1024)S(1)} %bitcast_clamp_fusion.9), kind=kCustom, calls=%fused_computation.clone.clone.1 | custom fusion | bytes 589824 | tf_op jit(solution)/shard_map/while/body/eval_jaxpr/jit(_take)/gather | solution.py:21
  301.9 95.2 %all-reduce.10.cloned.1.call-done = f32[8,128,1024]{2,1,0:T(8,128)} async-done(((f32[8,128,1024]{2,1,0:T(8,128)}), f32[8,128,1024]{2,1,0:T(8,128)}) %all-reduce.10.cloned.1.call-update) | async-done | bytes 4194320 | tf_op jit(solution)/shard_map/psum | solution.py:130
  411.7 95.7 %all-reduce.12.cloned.1.call-done = f32[8,128,1024]{2,1,0:T(8,128)} async-done(((f32[8,128,1024]{2,1,0:T(8,128)}), f32[8,128,1024]{2,1,0:T(8,128)}) %all-reduce.12.cloned.1.call-update) | async-done | bytes 4194320 | tf_op jit(solution)/shard_map/psum | solution.py:136
  524.2 200.8 %while.97 = (s32[]{:T(128)}, f32[8,4,128]{2,1,0:T(4,128)S(1)}, f32[8,4,128]{2,1,0:T(4,128)S(1)}, f32[8,128,4,64]{1,3,2,0:T(8,128)S(1)}, bf16[8,128,4,64]{1,3,2,0...) while((s32[]{:T(128)}, f32[8,4,128]{2,1,0:T(4,128)S(1)}, ...), condition=%wide.region_16.18_spmd, body=%wide.region_13.17_spmd.sunk | while | flops 141734032 | bytes 19093420 | solution.py:76
  525.9 54.8 %gather_fusion.1 = f32[16384,4]{1,0:T(8,128)} fusion(f32[4,32]{0,1:T(8,128)S(1)} %get-tuple-element.1816, s32[16384]{0:T(1024)S(1)} %bitcast_clamp_fusion.10), kind=kCustom, calls=%fused_computation.1.clone.clone.1 | custom fusion | bytes 589824 | tf_op jit(solution)/shard_map/while/body/eval_jaxpr/jit(_take)/gather | solution.py:21
  592.2 54.8 %gather_fusion.1 = f32[16384,4]{1,0:T(8,128)} fusion(f32[4,32]{0,1:T(8,128)S(1)} %get-tuple-element.1816, s32[16384]{0:T(1024)S(1)} %bitcast_clamp_fusion.10), kind=kCustom, calls=%fused_computation.1.clone.clone.1 | custom fusion | bytes 589824 | tf_op jit(solution)/shard_map/while/body/eval_jaxpr/jit(_take)/gather | solution.py:21
  659.5 54.8 %gather_fusion.1 = f32[16384,4]{1,0:T(8,128)} fusion(f32[4,32]{0,1:T(8,128)S(1)} %get-tuple-element.1816, s32[16384]{0:T(1024)S(1)} %bitcast_clamp_fusion.10), kind=kCustom, calls=%fused_computation.1.clone.clone.1 | custom fusion | bytes 589824 | tf_op jit(solution)/shard_map/while/body/eval_jaxpr/jit(_take)/gather | solution.py:21
  729.6 94.4 %all-reduce.14.cloned.1.call-done = f32[8,128,1024]{2,1,0:T(8,128)} async-done(((f32[8,128,1024]{2,1,0:T(8,128)}), f32[8,128,1024]{2,1,0:T(8,128)}) %all-reduce.14.cloned.1.call-update) | async-done | bytes 4194320 | tf_op jit(solution)/shard_map/psum | solution.py:130
  845.0 94.4 %all-reduce.16.cloned.1.call-done = f32[8,128,1024]{2,1,0:T(8,128)} async-done(((f32[8,128,1024]{2,1,0:T(8,128)}), f32[8,128,1024]{2,1,0:T(8,128)}) %all-reduce.16.cloned.1.call-update) | async-done | bytes 4194320 | tf_op jit(solution)/shard_map/psum | solution.py:155
  963.9 101.5 %scatter_custom_fusion.2 = f32[4,32]{0,1:T(8,128)S(1)} fusion(s32[16384]{0:T(1024)} %bitcast.578, f32[16384,4]{1,0:T(8,128)} %copy.221, f32[]{:T(128)} %constant.635.clone.1), kind=kCustom, calls=%fused_computation.436 | custom fusion | flops 65536 | bytes 1024 | tf_op jit(solution)/shard_map/vmap()/scatter-add | solution.py:53
  1065.4 591.5 %while.98 = (s32[]{:T(128)}, f32[8,128,4,64]{1,3,2,0:T(8,128)}, f32[4,32]{0,1:T(8,128)S(1)}, bf16[8,128,4,64]{1,3,2,0:T(8,128)(2,1)}, bf16[8,128,4,64]{1,3,2,0:T...) while((s32[]{:T(128)}, f32[8,128,4,64]{1,3,2,0:T(8,128)}, ...), condition=%wide.region_26.28_spmd, body=%wide.region_23.27_spmd.sunk | while | flops 342229120 | bytes 50674372 | solution.py:100
  1068.6 54.8 %gather_fusion.2 = f32[16384,4]{1,0:T(8,128)} fusion(f32[4,32]{0,1:T(8,128)S(1)} %get-tuple-element.1873, s32[16384]{0:T(1024)S(1)} %bitcast_clamp_fusion.11), kind=kCustom, calls=%fused_computation.2.clone.clone.1 | custom fusion | bytes 589824 | tf_op jit(solution)/shard_map/while/body/eval_jaxpr/jit(_take)/gather | solution.py:21
  1137.1 113.5 %scatter_fusion = f32[4,32]{0,1:T(8,128)S(1)} fusion(f32[4,32]{0,1:T(8,128)S(1)} %get-tuple-element.1846, s32[16384]{0:T(1024)S(1)} %bitcast.528, f32[16384,4]{1,0:T(8,128)} %bitcast.505), kind=kCustom, calls=%fused_computation.5.clone.1 | custom fusion | flops 65536 | bytes 851968 | tf_op jit(solution)/shard_map/while/body/eval_jaxpr/vmap()/scatter-add | solution.py:53
  1266.4 54.8 %gather_fusion.2 = f32[16384,4]{1,0:T(8,128)} fusion(f32[4,32]{0,1:T(8,128)S(1)} %get-tuple-element.1873, s32[16384]{0:T(1024)S(1)} %bitcast_clamp_fusion.11), kind=kCustom, calls=%fused_computation.2.clone.clone.1 | custom fusion | bytes 589824 | tf_op jit(solution)/shard_map/while/body/eval_jaxpr/jit(_take)/gather | solution.py:21
  1334.9 113.5 %scatter_fusion = f32[4,32]{0,1:T(8,128)S(1)} fusion(f32[4,32]{0,1:T(8,128)S(1)} %get-tuple-element.1846, s32[16384]{0:T(1024)S(1)} %bitcast.528, f32[16384,4]{1,0:T(8,128)} %bitcast.505), kind=kCustom, calls=%fused_computation.5.clone.1 | custom fusion | flops 65536 | bytes 851968 | tf_op jit(solution)/shard_map/while/body/eval_jaxpr/vmap()/scatter-add | solution.py:53
  1464.1 54.8 %gather_fusion.2 = f32[16384,4]{1,0:T(8,128)} fusion(f32[4,32]{0,1:T(8,128)S(1)} %get-tuple-element.1873, s32[16384]{0:T(1024)S(1)} %bitcast_clamp_fusion.11), kind=kCustom, calls=%fused_computation.2.clone.clone.1 | custom fusion | bytes 589824 | tf_op jit(solution)/shard_map/while/body/eval_jaxpr/jit(_take)/gather | solution.py:21
  1532.6 111.8 %scatter_fusion = f32[4,32]{0,1:T(8,128)S(1)} fusion(f32[4,32]{0,1:T(8,128)S(1)} %get-tuple-element.1846, s32[16384]{0:T(1024)S(1)} %bitcast.528, f32[16384,4]{1,0:T(8,128)} %bitcast.505), kind=kCustom, calls=%fused_computation.5.clone.1 | custom fusion | flops 65536 | bytes 851968 | tf_op jit(solution)/shard_map/while/body/eval_jaxpr/vmap()/scatter-add | solution.py:53
  1676.5 94.5 %all-reduce.18.cloned.1.call-done = f32[8,128,1024]{2,1,0:T(8,128)} async-done(((f32[8,128,1024]{2,1,0:T(8,128)}), f32[8,128,1024]{2,1,0:T(8,128)}) %all-reduce.18.cloned.1.call-update) | async-done | bytes 4194320 | tf_op jit(solution)/shard_map/psum | solution.py:172
  1811.5 76.5 %all-reduce.20.cloned.1.call-done = f32[8,128,1024]{2,1,0:T(8,128)} async-done(((f32[8,128,1024]{2,1,0:T(8,128)}), f32[8,128,1024]{2,1,0:T(8,128)}) %all-reduce.20.cloned.1.call-update) | async-done | bytes 4194320 | tf_op jit(solution)/shard_map/psum | solution.py:155
  1912.8 101.3 %scatter_custom_fusion.3 = f32[4,32]{0,1:T(8,128)S(1)} fusion(s32[16384]{0:T(1024)} %bitcast.579, f32[16384,4]{1,0:T(8,128)} %copy.231, f32[]{:T(128)} %constant.635.clone.1), kind=kCustom, calls=%fused_computation.434 | custom fusion | flops 65536 | bytes 1024 | tf_op jit(solution)/shard_map/vmap()/scatter-add | solution.py:53
  2014.1 589.2 %while.99 = (s32[]{:T(128)}, f32[8,128,4,64]{1,3,2,0:T(8,128)}, f32[4,32]{0,1:T(8,128)S(1)}, bf16[8,128,4,64]{1,3,2,0:T(8,128)(2,1)}, bf16[8,128,4,64]{1,3,2,0:T...) while((s32[]{:T(128)}, f32[8,128,4,64]{1,3,2,0:T(8,128)}, ...), condition=%wide.region_36.38_spmd, body=%wide.region_33.37_spmd.sunk | while | flops 342229120 | bytes 44382840 | solution.py:100
  2016.8 54.8 %gather_fusion.3 = f32[16384,4]{1,0:T(8,128)} fusion(f32[4,32]{0,1:T(8,128)S(1)} %get-tuple-element.1933, s32[16384]{0:T(1024)S(1)} %bitcast_clamp_fusion.12), kind=kCustom, calls=%fused_computation.3.clone.clone.1 | custom fusion | bytes 589824 | tf_op jit(solution)/shard_map/while/body/eval_jaxpr/jit(_take)/gather | solution.py:21
  2085.2 113.5 %scatter_fusion.1 = f32[4,32]{0,1:T(8,128)S(1)} fusion(f32[4,32]{0,1:T(8,128)S(1)} %get-tuple-element.1906, s32[16384]{0:T(1024)S(1)} %bitcast.529, f32[16384,4]{1,0:T(8,128)} %bitcast.506), kind=kCustom, calls=%fused_computation.6.clone.1 | custom fusion | flops 65536 | bytes 851968 | tf_op jit(solution)/shard_map/while/body/eval_jaxpr/vmap()/scatter-add | solution.py:53
  2213.6 54.8 %gather_fusion.3 = f32[16384,4]{1,0:T(8,128)} fusion(f32[4,32]{0,1:T(8,128)S(1)} %get-tuple-element.1933, s32[16384]{0:T(1024)S(1)} %bitcast_clamp_fusion.12), kind=kCustom, calls=%fused_computation.3.clone.clone.1 | custom fusion | bytes 589824 | tf_op jit(solution)/shard_map/while/body/eval_jaxpr/jit(_take)/gather | solution.py:21
  2282.1 113.5 %scatter_fusion.1 = f32[4,32]{0,1:T(8,128)S(1)} fusion(f32[4,32]{0,1:T(8,128)S(1)} %get-tuple-element.1906, s32[16384]{0:T(1024)S(1)} %bitcast.529, f32[16384,4]{1,0:T(8,128)} %bitcast.506), kind=kCustom, calls=%fused_computation.6.clone.1 | custom fusion | flops 65536 | bytes 851968 | tf_op jit(solution)/shard_map/while/body/eval_jaxpr/vmap()/scatter-add | solution.py:53
  2410.4 54.8 %gather_fusion.3 = f32[16384,4]{1,0:T(8,128)} fusion(f32[4,32]{0,1:T(8,128)S(1)} %get-tuple-element.1933, s32[16384]{0:T(1024)S(1)} %bitcast_clamp_fusion.12), kind=kCustom, calls=%fused_computation.3.clone.clone.1 | custom fusion | bytes 589824 | tf_op jit(solution)/shard_map/while/body/eval_jaxpr/jit(_take)/gather | solution.py:21
  2478.9 111.8 %scatter_fusion.1 = f32[4,32]{0,1:T(8,128)S(1)} fusion(f32[4,32]{0,1:T(8,128)S(1)} %get-tuple-element.1906, s32[16384]{0:T(1024)S(1)} %bitcast.529, f32[16384,4]{1,0:T(8,128)} %bitcast.506), kind=kCustom, calls=%fused_computation.6.clone.1 | custom fusion | flops 65536 | bytes 851968 | tf_op jit(solution)/shard_map/while/body/eval_jaxpr/vmap()/scatter-add | solution.py:53
  2655.5 62.7 %all-reduce.22.cloned.1.call-done = f32[8,128,1024]{2,1,0:T(8,128)} async-done(((f32[8,128,1024]{2,1,0:T(8,128)}), f32[8,128,1024]{2,1,0:T(8,128)}) %all-reduce.22.cloned.1.call-update) | async-done | bytes 4194320 | tf_op jit(solution)/shard_map/psum | solution.py:172
  2721.6 436.4 %all-reduce.23 = (f32[32,4]{0,1:T(4,128)}, f32[2,1024]{1,0:T(2,128)}, f32[2,1024]{1,0:T(2,128)}, bf16[2,1024,256]{2,1,0:T(8,128)(2,1)}, bf16[2,1024,256]{2,1,0:T...) all-reduce(f32[32,4]{0,1:T(4,128)S(1)} %add_bitcast_fusion, ...), channel_id=1, replica_groups=mesh['tp'=4,'cp'=4] {'cp'}, use_global_device_ids=true, to_apply=%region_39.41 | all-reduce | flops 6426752 | bytes 38568960 | tf_op jit(solution)/shard_map/psum | solution.py:204
  (697 shorter events, 564.8 us)
Async XLA Ops:
  7.2 390.0 %all-reduce.10.cloned.1.call-start = ((), (), s32[]{:S(2)}) async-start(), calls=%async_computation | async-start | bytes 8388608 | tf_op jit(solution)/shard_map/psum | solution.py:130
  95.0 63.9 %collective-permute-start = (bf16[8,128,4,64]{1,3,2,0:T(8,128)(2,1)}, bf16[8,128,4,64]{1,3,2,0:T(8,128)(2,1)S(1)}, u32[]{:S(2)}, u32[]{:S(2)}) collective-permute-start(bf16[8,128,4,64]{1,3,2,0:T(8,128)(2,1)} %get-tuple-element.1748), channel_id=1, source_target_pairs={{0,1},{1,2},{2,3},{3,0},{4,5},{5,6},{6,7},{7,4},{8,9},{9,10},{10,1... | collective-permute-start | bytes 1572872 | tf_op jit(solution)/shard_map/while/body/eval_jaxpr/ppermute | solution.py:71
  95.4 65.7 %collective-permute-start.1 = (bf16[8,128,4,64]{1,3,2,0:T(8,128)(2,1)}, bf16[8,128,4,64]{1,3,2,0:T(8,128)(2,1)S(1)}, u32[]{:S(2)}, u32[]{:S(2)}) collective-permute-start(bf16[8,128,4,64]{1,3,2,0:T(8,128)(2,1)} %get-tuple-element.1749), channel_id=1, source_target_pairs={{0,1},{1,2},{2,3},{3,0},{4,5},{5,6},{6,7},{7,4},{8,9},{9,10},{10,1... | collective-permute-start | bytes 1572872 | tf_op jit(solution)/shard_map/while/body/eval_jaxpr/ppermute | solution.py:72
  163.1 64.0 %collective-permute-start.1 = (bf16[8,128,4,64]{1,3,2,0:T(8,128)(2,1)}, bf16[8,128,4,64]{1,3,2,0:T(8,128)(2,1)S(1)}, u32[]{:S(2)}, u32[]{:S(2)}) collective-permute-start(bf16[8,128,4,64]{1,3,2,0:T(8,128)(2,1)} %get-tuple-element.1749), channel_id=1, source_target_pairs={{0,1},{1,2},{2,3},{3,0},{4,5},{5,6},{6,7},{7,4},{8,9},{9,10},{10,1... | collective-permute-start | bytes 1572872 | tf_op jit(solution)/shard_map/while/body/eval_jaxpr/ppermute | solution.py:72
  228.9 65.7 %collective-permute-start.1 = (bf16[8,128,4,64]{1,3,2,0:T(8,128)(2,1)}, bf16[8,128,4,64]{1,3,2,0:T(8,128)(2,1)S(1)}, u32[]{:S(2)}, u32[]{:S(2)}) collective-permute-start(bf16[8,128,4,64]{1,3,2,0:T(8,128)(2,1)} %get-tuple-element.1749), channel_id=1, source_target_pairs={{0,1},{1,2},{2,3},{3,0},{4,5},{5,6},{6,7},{7,4},{8,9},{9,10},{10,1... | collective-permute-start | bytes 1572872 | tf_op jit(solution)/shard_map/while/body/eval_jaxpr/ppermute | solution.py:72
  301.3 206.2 %all-reduce.12.cloned.1.call-start = ((), (), s32[]{:S(2)}) async-start(), calls=%async_computation.1 | async-start | bytes 8388608 | tf_op jit(solution)/shard_map/psum | solution.py:136
  411.7 412.3 %all-reduce.14.cloned.1.call-start = ((), (), s32[]{:S(2)}) async-start(), calls=%async_computation.2 | async-start | bytes 8388608 | tf_op jit(solution)/shard_map/psum | solution.py:130
  524.2 65.5 %collective-permute-start.3 = (bf16[8,128,4,64]{1,3,2,0:T(8,128)(2,1)}, bf16[8,128,4,64]{1,3,2,0:T(8,128)(2,1)S(1)}, u32[]{:S(2)}, u32[]{:S(2)}) collective-permute-start(bf16[8,128,4,64]{1,3,2,0:T(8,128)(2,1)} %get-tuple-element.1797), channel_id=1, source_target_pairs={{0,1},{1,2},{2,3},{3,0},{4,5},{5,6},{6,7},{7,4},{8,9},{9,10},{10,1... | collective-permute-start | bytes 1572872 | tf_op jit(solution)/shard_map/while/body/eval_jaxpr/ppermute | solution.py:72
  591.5 64.6 %collective-permute-start.3 = (bf16[8,128,4,64]{1,3,2,0:T(8,128)(2,1)}, bf16[8,128,4,64]{1,3,2,0:T(8,128)(2,1)S(1)}, u32[]{:S(2)}, u32[]{:S(2)}) collective-permute-start(bf16[8,128,4,64]{1,3,2,0:T(8,128)(2,1)} %get-tuple-element.1797), channel_id=1, source_target_pairs={{0,1},{1,2},{2,3},{3,0},{4,5},{5,6},{6,7},{7,4},{8,9},{9,10},{10,1... | collective-permute-start | bytes 1572872 | tf_op jit(solution)/shard_map/while/body/eval_jaxpr/ppermute | solution.py:72
  657.9 65.5 %collective-permute-start.3 = (bf16[8,128,4,64]{1,3,2,0:T(8,128)(2,1)}, bf16[8,128,4,64]{1,3,2,0:T(8,128)(2,1)S(1)}, u32[]{:S(2)}, u32[]{:S(2)}) collective-permute-start(bf16[8,128,4,64]{1,3,2,0:T(8,128)(2,1)} %get-tuple-element.1797), channel_id=1, source_target_pairs={{0,1},{1,2},{2,3},{3,0},{4,5},{5,6},{6,7},{7,4},{8,9},{9,10},{10,1... | collective-permute-start | bytes 1572872 | tf_op jit(solution)/shard_map/while/body/eval_jaxpr/ppermute | solution.py:72
  729.1 210.2 %all-reduce.16.cloned.1.call-start = ((), (), s32[]{:S(2)}) async-start(), calls=%async_computation.3 | async-start | bytes 8388608 | tf_op jit(solution)/shard_map/psum | solution.py:155
  843.6 927.4 %all-reduce.18.cloned.1.call-start = ((), (), s32[]{:S(2)}) async-start(), calls=%async_computation.4 | async-start | bytes 8388608 | tf_op jit(solution)/shard_map/psum | solution.py:172
  1066.2 64.0 %collective-permute-start.5 = (bf16[8,128,4,64]{1,3,2,0:T(8,128)(2,1)}, bf16[8,128,4,64]{1,3,2,0:T(8,128)(2,1)}, u32[]{:S(2)}, u32[]{:S(2)}) collective-permute-start(bf16[8,128,4,64]{1,3,2,0:T(8,128)(2,1)} %copy-done.39), channel_id=1, source_target_pairs={{0,1},{1,2},{2,3},{3,0},{4,5},{5,6},{6,7},{7,4},{8,9},{9,10},{10,1... | collective-permute-start | bytes 1572872 | tf_op jit(solution)/shard_map/while/body/eval_jaxpr/ppermute | solution.py:94
  1067.8 189.9 %collective-permute-start.6 = (f32[8,128,4,64]{1,3,2,0:T(8,128)}, f32[8,128,4,64]{1,3,2,0:T(8,128)}, u32[]{:S(2)}, u32[]{:S(2)}) collective-permute-start(f32[8,128,4,64]{1,3,2,0:T(8,128)} %get-tuple-element.1849), channel_id=1, source_target_pairs={{0,1},{1,2},{2,3},{3,0},{4,5},{5,6},{6,7},{7,4},{8,9},{9,10},{10,1... | collective-permute-start | bytes 3145736 | tf_op jit(solution)/shard_map/while/body/eval_jaxpr/ppermute | solution.py:95
  1067.8 192.6 %collective-permute-start.7 = (f32[8,128,4,64]{1,3,2,0:T(8,128)}, f32[8,128,4,64]{1,3,2,0:T(8,128)}, u32[]{:S(2)}, u32[]{:S(2)}) collective-permute-start(f32[8,128,4,64]{1,3,2,0:T(8,128)} %get-tuple-element.1850), channel_id=1, source_target_pairs={{0,1},{1,2},{2,3},{3,0},{4,5},{5,6},{6,7},{7,4},{8,9},{9,10},{10,1... | collective-permute-start | bytes 3145736 | tf_op jit(solution)/shard_map/while/body/eval_jaxpr/ppermute | solution.py:96
  1264.0 64.0 %collective-permute-start.5 = (bf16[8,128,4,64]{1,3,2,0:T(8,128)(2,1)}, bf16[8,128,4,64]{1,3,2,0:T(8,128)(2,1)}, u32[]{:S(2)}, u32[]{:S(2)}) collective-permute-start(bf16[8,128,4,64]{1,3,2,0:T(8,128)(2,1)} %copy-done.39), channel_id=1, source_target_pairs={{0,1},{1,2},{2,3},{3,0},{4,5},{5,6},{6,7},{7,4},{8,9},{9,10},{10,1... | collective-permute-start | bytes 1572872 | tf_op jit(solution)/shard_map/while/body/eval_jaxpr/ppermute | solution.py:94
  1264.0 191.4 %collective-permute-start.6 = (f32[8,128,4,64]{1,3,2,0:T(8,128)}, f32[8,128,4,64]{1,3,2,0:T(8,128)}, u32[]{:S(2)}, u32[]{:S(2)}) collective-permute-start(f32[8,128,4,64]{1,3,2,0:T(8,128)} %get-tuple-element.1849), channel_id=1, source_target_pairs={{0,1},{1,2},{2,3},{3,0},{4,5},{5,6},{6,7},{7,4},{8,9},{9,10},{10,1... | collective-permute-start | bytes 3145736 | tf_op jit(solution)/shard_map/while/body/eval_jaxpr/ppermute | solution.py:95
  1264.0 194.1 %collective-permute-start.7 = (f32[8,128,4,64]{1,3,2,0:T(8,128)}, f32[8,128,4,64]{1,3,2,0:T(8,128)}, u32[]{:S(2)}, u32[]{:S(2)}) collective-permute-start(f32[8,128,4,64]{1,3,2,0:T(8,128)} %get-tuple-element.1850), channel_id=1, source_target_pairs={{0,1},{1,2},{2,3},{3,0},{4,5},{5,6},{6,7},{7,4},{8,9},{9,10},{10,1... | collective-permute-start | bytes 3145736 | tf_op jit(solution)/shard_map/while/body/eval_jaxpr/ppermute | solution.py:96
  1461.7 64.0 %collective-permute-start.5 = (bf16[8,128,4,64]{1,3,2,0:T(8,128)(2,1)}, bf16[8,128,4,64]{1,3,2,0:T(8,128)(2,1)}, u32[]{:S(2)}, u32[]{:S(2)}) collective-permute-start(bf16[8,128,4,64]{1,3,2,0:T(8,128)(2,1)} %copy-done.39), channel_id=1, source_target_pairs={{0,1},{1,2},{2,3},{3,0},{4,5},{5,6},{6,7},{7,4},{8,9},{9,10},{10,1... | collective-permute-start | bytes 1572872 | tf_op jit(solution)/shard_map/while/body/eval_jaxpr/ppermute | solution.py:94
  1461.8 189.6 %collective-permute-start.6 = (f32[8,128,4,64]{1,3,2,0:T(8,128)}, f32[8,128,4,64]{1,3,2,0:T(8,128)}, u32[]{:S(2)}, u32[]{:S(2)}) collective-permute-start(f32[8,128,4,64]{1,3,2,0:T(8,128)} %get-tuple-element.1849), channel_id=1, source_target_pairs={{0,1},{1,2},{2,3},{3,0},{4,5},{5,6},{6,7},{7,4},{8,9},{9,10},{10,1... | collective-permute-start | bytes 3145736 | tf_op jit(solution)/shard_map/while/body/eval_jaxpr/ppermute | solution.py:95
  1461.8 192.3 %collective-permute-start.7 = (f32[8,128,4,64]{1,3,2,0:T(8,128)}, f32[8,128,4,64]{1,3,2,0:T(8,128)}, u32[]{:S(2)}, u32[]{:S(2)}) collective-permute-start(f32[8,128,4,64]{1,3,2,0:T(8,128)} %get-tuple-element.1850), channel_id=1, source_target_pairs={{0,1},{1,2},{2,3},{3,0},{4,5},{5,6},{6,7},{7,4},{8,9},{9,10},{10,1... | collective-permute-start | bytes 3145736 | tf_op jit(solution)/shard_map/while/body/eval_jaxpr/ppermute | solution.py:96
  1676.2 211.8 %all-reduce.20.cloned.1.call-start = ((), (), s32[]{:S(2)}) async-start(), calls=%async_computation.5 | async-start | bytes 8388608 | tf_op jit(solution)/shard_map/psum | solution.py:155
  1792.2 926.0 %all-reduce.22.cloned.1.call-start = ((), (), s32[]{:S(2)}) async-start(), calls=%async_computation.6 | async-start | bytes 8388608 | tf_op jit(solution)/shard_map/psum | solution.py:172
  2014.4 64.0 %collective-permute-start.9 = (bf16[8,128,4,64]{1,3,2,0:T(8,128)(2,1)}, bf16[8,128,4,64]{1,3,2,0:T(8,128)(2,1)}, u32[]{:S(2)}, u32[]{:S(2)}) collective-permute-start(bf16[8,128,4,64]{1,3,2,0:T(8,128)(2,1)} %get-tuple-element.1908), channel_id=1, source_target_pairs={{0,1},{1,2},{2,3},{3,0},{4,5},{5,6},{6,7},{7,4},{8,9},{9,10},{10,1... | collective-permute-start | bytes 1572872 | tf_op jit(solution)/shard_map/while/body/eval_jaxpr/ppermute | solution.py:94
  2015.9 189.8 %collective-permute-start.10 = (f32[8,128,4,64]{1,3,2,0:T(8,128)}, f32[8,128,4,64]{1,3,2,0:T(8,128)}, u32[]{:S(2)}, u32[]{:S(2)}) collective-permute-start(f32[8,128,4,64]{1,3,2,0:T(8,128)} %get-tuple-element.1909), channel_id=1, source_target_pairs={{0,1},{1,2},{2,3},{3,0},{4,5},{5,6},{6,7},{7,4},{8,9},{9,10},{10,1... | collective-permute-start | bytes 3145736 | tf_op jit(solution)/shard_map/while/body/eval_jaxpr/ppermute | solution.py:95
  2016.0 192.5 %collective-permute-start.11 = (f32[8,128,4,64]{1,3,2,0:T(8,128)}, f32[8,128,4,64]{1,3,2,0:T(8,128)}, u32[]{:S(2)}, u32[]{:S(2)}) collective-permute-start(f32[8,128,4,64]{1,3,2,0:T(8,128)} %get-tuple-element.1910), channel_id=1, source_target_pairs={{0,1},{1,2},{2,3},{3,0},{4,5},{5,6},{6,7},{7,4},{8,9},{9,10},{10,1... | collective-permute-start | bytes 3145736 | tf_op jit(solution)/shard_map/while/body/eval_jaxpr/ppermute | solution.py:96
  2211.2 64.0 %collective-permute-start.9 = (bf16[8,128,4,64]{1,3,2,0:T(8,128)(2,1)}, bf16[8,128,4,64]{1,3,2,0:T(8,128)(2,1)}, u32[]{:S(2)}, u32[]{:S(2)}) collective-permute-start(bf16[8,128,4,64]{1,3,2,0:T(8,128)(2,1)} %get-tuple-element.1908), channel_id=1, source_target_pairs={{0,1},{1,2},{2,3},{3,0},{4,5},{5,6},{6,7},{7,4},{8,9},{9,10},{10,1... | collective-permute-start | bytes 1572872 | tf_op jit(solution)/shard_map/while/body/eval_jaxpr/ppermute | solution.py:94
  2211.2 191.4 %collective-permute-start.10 = (f32[8,128,4,64]{1,3,2,0:T(8,128)}, f32[8,128,4,64]{1,3,2,0:T(8,128)}, u32[]{:S(2)}, u32[]{:S(2)}) collective-permute-start(f32[8,128,4,64]{1,3,2,0:T(8,128)} %get-tuple-element.1909), channel_id=1, source_target_pairs={{0,1},{1,2},{2,3},{3,0},{4,5},{5,6},{6,7},{7,4},{8,9},{9,10},{10,1... | collective-permute-start | bytes 3145736 | tf_op jit(solution)/shard_map/while/body/eval_jaxpr/ppermute | solution.py:95
  2211.3 194.1 %collective-permute-start.11 = (f32[8,128,4,64]{1,3,2,0:T(8,128)}, f32[8,128,4,64]{1,3,2,0:T(8,128)}, u32[]{:S(2)}, u32[]{:S(2)}) collective-permute-start(f32[8,128,4,64]{1,3,2,0:T(8,128)} %get-tuple-element.1910), channel_id=1, source_target_pairs={{0,1},{1,2},{2,3},{3,0},{4,5},{5,6},{6,7},{7,4},{8,9},{9,10},{10,1... | collective-permute-start | bytes 3145736 | tf_op jit(solution)/shard_map/while/body/eval_jaxpr/ppermute | solution.py:96
  2408.1 64.0 %collective-permute-start.9 = (bf16[8,128,4,64]{1,3,2,0:T(8,128)(2,1)}, bf16[8,128,4,64]{1,3,2,0:T(8,128)(2,1)}, u32[]{:S(2)}, u32[]{:S(2)}) collective-permute-start(bf16[8,128,4,64]{1,3,2,0:T(8,128)(2,1)} %get-tuple-element.1908), channel_id=1, source_target_pairs={{0,1},{1,2},{2,3},{3,0},{4,5},{5,6},{6,7},{7,4},{8,9},{9,10},{10,1... | collective-permute-start | bytes 1572872 | tf_op jit(solution)/shard_map/while/body/eval_jaxpr/ppermute | solution.py:94
  2408.1 189.6 %collective-permute-start.10 = (f32[8,128,4,64]{1,3,2,0:T(8,128)}, f32[8,128,4,64]{1,3,2,0:T(8,128)}, u32[]{:S(2)}, u32[]{:S(2)}) collective-permute-start(f32[8,128,4,64]{1,3,2,0:T(8,128)} %get-tuple-element.1909), channel_id=1, source_target_pairs={{0,1},{1,2},{2,3},{3,0},{4,5},{5,6},{6,7},{7,4},{8,9},{9,10},{10,1... | collective-permute-start | bytes 3145736 | tf_op jit(solution)/shard_map/while/body/eval_jaxpr/ppermute | solution.py:95
  2408.2 192.3 %collective-permute-start.11 = (f32[8,128,4,64]{1,3,2,0:T(8,128)}, f32[8,128,4,64]{1,3,2,0:T(8,128)}, u32[]{:S(2)}, u32[]{:S(2)}) collective-permute-start(f32[8,128,4,64]{1,3,2,0:T(8,128)} %get-tuple-element.1910), channel_id=1, source_target_pairs={{0,1},{1,2},{2,3},{3,0},{4,5},{5,6},{6,7},{7,4},{8,9},{9,10},{10,1... | collective-permute-start | bytes 3145736 | tf_op jit(solution)/shard_map/while/body/eval_jaxpr/ppermute | solution.py:96
  (158 other events, 3645.1 us)
Sparse Core Ops, SparseCore 0:
  301.4 95.7 all-reduce.9
  411.8 95.5 all-reduce.11
  729.3 94.6 all-reduce.13
  843.7 95.5 all-reduce.15
  1676.3 94.6 all-reduce.17
  1792.3 95.5 all-reduce.19
  2622.8 95.4 all-reduce.21
where the time goes:
time: 3180 us; the launch traced here: 3170 us
  other arithmetic  953 us (30%)
  local copies, waits for them, and re-layouts  904 us (28%)
  waiting for transfers between devices  631 us (20%)
  blocking collectives  443 us (14%)
  matrix products  197 us (6%)
    scatter-add x8, other arithmetic, pair_grads(): jax.ops.segment_sum(score_row, seg_ids, num_segments=n_buckets)  880 us
    gather x26, local copies, waits for them, and re-layouts, pair_bias(): return (buckets, jnp.take(bias_table, buckets, axis=1))  790 us
    psum x1, blocking collectives, local_program(): lax.psum(bias_grad, 'cp')  436 us
    psum x2, waiting for transfers between devices, layer_forward(): lax.psum(jnp.dot(attn_flat, w_o, preferred_element_type=jnp.float32), 'tp')  190 us
    psum x2, waiting for transfers between devices, layer_backward(): lax.psum(d_h_mlp, 'tp')  171 us
    psum x2, waiting for transfers between devices, layer_backward(): lax.psum(d_h_attn, 'tp')  157 us
    psum x1, waiting for transfers between devices, layer_forward(): lax.psum(jnp.dot(gated, w_out, preferred_element_type=jnp.float32), 'tp')  95.7 us
  transfers between devices with their start and end apart: 47, of which 11 were waited for; matrix products, arithmetic and copies ran while one was open for 50% of the time, Pallas kernels for 0%

commit v1 on v0

v1 whole, which is shorter than its diff:
```python
import functools
import jax
import jax.numpy as jnp
from jax import lax
from jax.experimental import pallas as pl
from jax.experimental.pallas import tpu as pltpu
from jax.sharding import PartitionSpec as P

NORM_EPS = 1e-6
MASK_NEG = -1e9
HEAD = 64
F32 = jnp.float32
BF16 = jnp.bfloat16
NT = (((1,), (1,)), ((), ()))
TN = (((0,), (0,)), ((), ()))


def rel_bucket(rel_pos):
    distance = jnp.minimum(jnp.abs(rel_pos), 128)
    distance_sq = distance * distance
    log_part = 8 + sum((distance_sq >= 64 * 2 ** power).astype(jnp.int32) for power in range(1, 8))
    return jnp.where(distance < 8, distance, log_part) + 16 * (rel_pos > 0).astype(jnp.int32)


def bucket_onehot(seq):
    rel = jnp.arange(2 * seq) - seq
    return (rel_bucket(rel)[None, :] == jnp.arange(32)[:, None]) & (jnp.arange(2 * seq) > 0)[None, :]


def dot(a, b, dims=(((1,), (0,)), ((), ()))):
    return lax.dot_general(a, b, dims, preferred_element_type=F32)


def toeplitz(row, seq):
    base = pltpu.roll(row, seq, 1)
    rows = jnp.concatenate([base if i == 0 else pltpu.roll(base, i, 1) for i in range(8)], axis=0)
    size = 8
    while size < seq:
        rows = jnp.concatenate([rows, pltpu.roll(rows, size, 1)], axis=0)
        size *= 2
    return rows[:, :seq]


def diag_sums(mat, seq):
    wide = jnp.concatenate([mat, jnp.zeros_like(mat)], axis=1)
    size = seq
    while size > 1:
        half = size // 2
        wide = wide[:half] + pltpu.roll(wide[half:size], 2 * seq - half, 1)
        size = half
    return pltpu.roll(wide, seq, 1)


def attn_fwd_kernel(seq, batch, heads, x_ref, g_ref, wq_ref, wk_ref, wv_ref, t_ref, add_ref, h_ref, q_ref, k_ref, v_ref, o_ref, bias_ref):
    for blk in range(batch * seq // 256):
        rows = pl.ds(blk * 256, 256)
        xf = x_ref[rows, :].astype(F32)
        inv = lax.rsqrt(jnp.mean(xf * xf, axis=-1, keepdims=True) + NORM_EPS)
        h = (xf * inv * g_ref[...]).astype(BF16)
        h_ref[rows, :] = h
        q_ref[rows, :] = dot(h, wq_ref[...]).astype(BF16)
        k_ref[rows, :] = dot(h, wk_ref[...]).astype(BF16)
        v_ref[rows, :] = dot(h, wv_ref[...]).astype(BF16)
    for head in range(heads):
        bias_ref[...] = toeplitz(t_ref[head:head + 1, :], seq)
        cols = pl.ds(head * HEAD, HEAD)
        for b in range(batch):
            rows = pl.ds(b * seq, seq)
            s = dot(q_ref[rows, cols], k_ref[rows, cols], NT) + bias_ref[...] + add_ref[b:b + 1, :]
            e = jnp.exp(s - jnp.max(s, axis=-1, keepdims=True))
            total = jnp.sum(e, axis=-1, keepdims=True)
            o_ref[rows, cols] = (dot(e.astype(BF16), v_ref[rows, cols]) / total).astype(BF16)


def attn_bwd_kernel(seq, batch, heads, dm_ref, wo_ref, q_ref, k_ref, v_ref, o_ref, t_ref, add_ref, dq_ref, dk_ref, dv_ref, dt_ref, bias_ref, dout_ref, acc_ref):
    for blk in range(batch * seq // 256):
        rows = pl.ds(blk * 256, 256)
        dout_ref[rows, :] = dot(dm_ref[rows, :], wo_ref[...], NT).astype(BF16)
    dt_ref[...] = jnp.zeros_like(dt_ref)
    for head in range(heads):
        bias_ref[...] = toeplitz(t_ref[head:head + 1, :], seq)
        cols = pl.ds(head * HEAD, HEAD)
        for b in range(batch):
            rows = pl.ds(b * seq, seq)
            q, k, v, do = q_ref[rows, cols], k_ref[rows, cols], v_ref[rows, cols], dout_ref[rows, cols]
            s = dot(q, k, NT) + bias_ref[...] + add_ref[b:b + 1, :]
            e = jnp.exp(s - jnp.max(s, axis=-1, keepdims=True))
            p = e * (1.0 / jnp.sum(e, axis=-1, keepdims=True))
            row_dot = jnp.sum(do.astype(F32) * o_ref[rows, cols].astype(F32), axis=-1, keepdims=True)
            ds = p * (dot(do, v, NT) - row_dot)
            if b == 0:
                acc_ref[...] = ds
            else:
                acc_ref[...] += ds
            dsl = ds.astype(BF16)
            dq_ref[rows, cols] = dot(dsl, k).astype(BF16)
            dk_ref[rows, cols] = dot(dsl, q, TN).astype(BF16)
            dv_ref[rows, cols] = dot(p.astype(BF16), do, TN).astype(BF16)
        dt_ref[head:head + 1, :] = diag_sums(acc_ref[...], seq)


def vmem_specs(n):
    return [pl.BlockSpec(memory_space=pltpu.VMEM)] * n


def attn_fwd(x, gain, w_q, w_k, w_v, table, key_add, seq):
    rows, width = x.shape
    cols = w_q.shape[1]
    batch, heads = rows // seq, cols // HEAD
    flops = 2 * rows * width * cols * 3 + 4 * rows * seq * cols
    return pl.pallas_call(
        functools.partial(attn_fwd_kernel, seq, batch, heads),
        out_shape=[jax.ShapeDtypeStruct(x.shape, BF16)] + [jax.ShapeDtypeStruct((rows, cols), BF16)] * 4,
        in_specs=vmem_specs(7), out_specs=vmem_specs(5),
        scratch_shapes=[pltpu.VMEM((seq, seq), F32)],
        compiler_params=pltpu.CompilerParams(vmem_limit_bytes=48 * 1024 * 1024),
        cost_estimate=pl.CostEstimate(flops=flops, bytes_accessed=8 << 20, transcendentals=0),
        name="attn_fwd",
    )(x, gain[None, :], w_q, w_k, w_v, table, key_add)


def attn_bwd(d_mid, w_o, q, k, v, o, table, key_add, seq):
    rows, cols = q.shape
    batch, heads = rows // seq, cols // HEAD
    flops = 2 * rows * d_mid.shape[1] * cols + 10 * rows * seq * cols
    return pl.pallas_call(
        functools.partial(attn_bwd_kernel, seq, batch, heads),
        out_shape=[jax.ShapeDtypeStruct((rows, cols), BF16)] * 3 + [jax.ShapeDtypeStruct(table.shape, F32)],
        in_specs=vmem_specs(8), out_specs=vmem_specs(4),
        scratch_shapes=[pltpu.VMEM((seq, seq), F32), pltpu.VMEM((rows, cols), BF16), pltpu.VMEM((seq, seq), F32)],
        compiler_params=pltpu.CompilerParams(vmem_limit_bytes=48 * 1024 * 1024),
        cost_estimate=pl.CostEstimate(flops=flops, bytes_accessed=8 << 20, transcendentals=0),
        name="attn_bwd",
    )(d_mid, w_o, q, k, v, o, table, key_add)


def rms(x, gain):
    xf = x.astype(F32)
    inv = lax.rsqrt(jnp.mean(xf * xf, axis=-1, keepdims=True) + NORM_EPS)
    return (xf * inv * gain).astype(BF16)


def scatter_sum(partial):
    return lax.psum_scatter(partial, 'tp', scatter_dimension=0, tiled=True)


def gather_rows(own):
    return lax.all_gather(own, 'tp', axis=0, tiled=True)


def own_rows(full, rows):
    return lax.dynamic_slice_in_dim(full, lax.axis_index('tp') * rows, rows, axis=0)


def fwd_sum(partial, residual):
    total = scatter_sum(partial)
    return gather_rows((own_rows(residual, total.shape[0]).astype(F32) + total).astype(BF16))


def bwd_sum(partial, x, gain, d_res):
    total = scatter_sum(partial)
    xf = own_rows(x, total.shape[0]).astype(F32)
    inv = lax.rsqrt(jnp.mean(xf * xf, axis=-1, keepdims=True) + NORM_EPS)
    normed = xf * inv
    d_gain = jnp.sum(total * normed, axis=0)
    d_normed = total * gain
    d_x = inv * (d_normed - normed * jnp.mean(d_normed * normed, axis=-1, keepdims=True))
    return gather_rows((d_x + own_rows(d_res, total.shape[0]).astype(F32)).astype(BF16)), d_gain


def mlp_up(x1, gain, w_gate, w_lin):
    h2 = rms(x1, gain)
    gate_pre, lin_pre = dot(h2, w_gate), dot(h2, w_lin)
    gated = (jax.nn.gelu(gate_pre, approximate=True) * lin_pre).astype(BF16)
    return h2, gate_pre, lin_pre, gated


def cp_sum(part):
    own = lax.psum_scatter(part, 'cp', scatter_dimension=0, tiled=True).astype(BF16)
    return lax.all_gather(own, 'cp', axis=0, tiled=True)


def solution(mesh):
    seq_spec = P(None, 'cp', None)
    col_spec = P(None, None, 'tp')
    row_spec = P(None, 'tp', None)
    weight_specs = (P(), P(), col_spec, col_spec, col_spec, row_spec, col_spec, col_spec, row_spec)
    cp_size = mesh.shape['cp']

    def local_program(x_in, d_y, key_mask, rel_bias, g_attn, g_mlp, w_q, w_k, w_v, w_o, w_gate, w_lin, w_out):
        batch, blk, width = x_in.shape
        seq = blk * cp_size
        layers = w_q.shape[0]
        own_batch = batch // cp_size

        def to_batch(arr):
            return lax.all_to_all(arr, 'cp', split_axis=0, concat_axis=1, tiled=True).reshape(own_batch * seq, width)

        x = to_batch(x_in)
        dy = to_batch(d_y)
        mask_all = lax.all_gather(key_mask, 'cp', axis=1, tiled=True)
        mask = lax.dynamic_slice_in_dim(mask_all, lax.axis_index('cp') * own_batch, own_batch, axis=0)
        key_add = jnp.where(mask > 0, 0.0, MASK_NEG).astype(F32)
        onehot = bucket_onehot(seq)
        table = jnp.sum(jnp.where(onehot[None], rel_bias.T[:, :, None], 0.0), axis=1)

        saved = []
        for l in range(layers):
            h, q, k, v, o = attn_fwd(x, g_attn[l], w_q[l], w_k[l], w_v[l], table, key_add, seq)
            x1 = fwd_sum(dot(o, w_o[l]), x)
            h2, gate_pre, lin_pre, gated = mlp_up(x1, g_mlp[l], w_gate[l], w_lin[l])
            saved.append((x, h, q, k, v, o, x1, h2, gate_pre, lin_pre, gated))
            if l < layers - 1:
                x = fwd_sum(dot(gated, w_out[l]), x1)

        grads = [None] * layers
        d_table = jnp.zeros_like(table)
        for l in reversed(range(layers)):
            x, h, q, k, v, o, x1, h2, gate_pre, lin_pre, gated = saved[l]
            d_gated = dot(dy, w_out[l], NT)
            gelu_val, gelu_pull = jax.vjp(lambda gate_in: jax.nn.gelu(gate_in, approximate=True), gate_pre)
            d_lin = (d_gated * gelu_val).astype(BF16)
            d_gate = gelu_pull(d_gated * lin_pre)[0].astype(BF16)
            d_mid, d_gm = bwd_sum(dot(d_gate, w_gate[l], NT) + dot(d_lin, w_lin[l], NT), x1, g_mlp[l], dy)
            d_wout = cp_sum(dot(gated, dy, TN))
            d_wgate = cp_sum(dot(h2, d_gate, TN))
            d_wlin = cp_sum(dot(h2, d_lin, TN))
            dq, dk, dv, dt = attn_bwd(d_mid, w_o[l], q, k, v, o, table, key_add, seq)
            d_table = d_table + dt
            part = dot(dq, w_q[l], NT) + dot(dk, w_k[l], NT) + dot(dv, w_v[l], NT)
            d_x, d_ga = bwd_sum(part, x, g_attn[l], d_mid)
            d_wo = cp_sum(dot(o, d_mid, TN))
            d_wq = cp_sum(dot(h, dq, TN))
            d_wk = cp_sum(dot(h, dk, TN))
            d_wv = cp_sum(dot(h, dv, TN))
            grads[l] = (d_ga, d_gm, d_wq, d_wk, d_wv, d_wo, d_wgate, d_wlin, d_wout)
            dy = d_x
        stacked = [jnp.stack([g[i] for g in grads]) for i in range(9)]
        d_bias = jnp.sum(jnp.where(onehot[None], d_table[:, None, :], 0.0), axis=2)
        d_bias = lax.psum(d_bias, 'cp').T
        d_gains = lax.psum(jnp.stack(stacked[:2]), ('tp', 'cp'))
        d_x = lax.all_to_all(dy.reshape(own_batch, seq, width), 'cp', split_axis=1, concat_axis=0, tiled=True)
        return (d_x, d_bias, d_gains[0], d_gains[1]) + tuple(stacked[2:])

    return jax.shard_map(local_program, mesh=mesh, in_specs=(seq_spec, seq_spec, P(None, 'cp'), P(None, 'tp')) + weight_specs, out_specs=(seq_spec, P(None, 'tp')) + weight_specs, check_vma=False)
```

time: 3180 us -> 1350 us (0.42)
  other arithmetic: 953 us -> 66.9 us
  local copies, waits for them, and re-layouts: 904 us -> 33.7 us
  blocking collectives: 443 us -> 176 us
  waiting for transfers between devices: 631 us -> 880 us
  matrix products: 197 us -> 115 us
  Pallas kernels: 0 us -> 43.6 us
    scatter-add x8 -> x0, other arithmetic: 880 us -> none  [pair_grads(): jax.ops.segment_sum(score_row, seg_ids, num_segments=n_buckets)]
    gather x26 -> x0, local copies, waits for them, and re-layouts: 790 us -> none  [pair_bias(): return (buckets, jnp.take(bias_table, buckets, axis=1))]
    reduce_scatter x0 -> x21, waiting for transfers between devices: none -> 656 us  [the longest x14 328 us: cp_sum(): lax.psum_scatter(part, 'cp', scatter_dimension=0, tiled=True).astype(BF16)]
    psum x7 -> x0, waiting for transfers between devices: 614 us -> none  [the longest x2 190 us: layer_forward(): lax.psum(jnp.dot(attn_flat, w_o, preferred_element_type=jnp.float32), 'tp')]
    psum x1 -> x2, blocking collectives: 436 us -> 38.4 us  [the longest x1 32 us: local_program(): d_gains = lax.psum(jnp.stack(stacked[:2]), ('tp', 'cp'))]
    all_gather x0 -> x13, waiting for transfers between devices: none -> 223 us  [the longest x7 149 us: gather_rows(): return lax.all_gather(own, 'tp', axis=0, tiled=True)]
    dot_general x95 -> x33, matrix products: 197 us -> 115 us  [dot(): return lax.dot_general(a, b, dims, preferred_element_type=F32)]
    all_gather x0 -> x8, blocking collectives: none -> 81.3 us  [cp_sum(): return lax.all_gather(own, 'cp', axis=0, tiled=True)]
  transfers between devices with their start and end apart: 47 -> 36, of which waited for: 11 -> 31; matrix products, arithmetic and copies ran while one was open for 50% -> 8% of each run, Pallas kernels for 0% -> 1%
where the time goes in v1:
time: 1350 us; the launch traced here: 1340 us
  waiting for transfers between devices  880 us (65%)
  blocking collectives  176 us (13%)
  matrix products  115 us (9%)
  other arithmetic  66.9 us (5%)
  Pallas kernels  43.6 us (3%)
  local copies, waits for them, and re-layouts  33.7 us (2%)
  between operations  15.8 us (1%)
    reduce_scatter x14, waiting for transfers between devices, cp_sum(): lax.psum_scatter(part, 'cp', scatter_dimension=0, tiled=True).astype(BF16)  328 us
    reduce_scatter x7, waiting for transfers between devices, scatter_sum(): return lax.psum_scatter(partial, 'tp', scatter_dimension=0, tiled=True)  328 us
    all_gather x7, waiting for transfers between devices, gather_rows(): return lax.all_gather(own, 'tp', axis=0, tiled=True)  149 us
    dot_general x33, matrix products, dot(): return lax.dot_general(a, b, dims, preferred_element_type=F32)  115 us
    all_gather x8, blocking collectives, cp_sum(): return lax.all_gather(own, 'cp', axis=0, tiled=True)  81.3 us
    all_gather x6, waiting for transfers between devices, cp_sum(): return lax.all_gather(own, 'cp', axis=0, tiled=True)  74.3 us
    psum x1, blocking collectives, local_program(): d_gains = lax.psum(jnp.stack(stacked[:2]), ('tp', 'cp'))  32 us
    all_to_all x1, blocking collectives, to_batch(): lax.all_to_all(arr, 'cp', split_axis=0, concat_axis=1, tiled=True)  29 us
  transfers between devices with their start and end apart: 36, of which 31 were waited for; matrix products, arithmetic and copies ran while one was open for 8% of the time, Pallas kernels for 1%

profile of v1, /device:TPU:0, one launch (start us, length us, event | category | flops | bytes accessed | tf_op | source)
XLA Modules:
  0.0 1341.8 jit_solution(7789056551075549831)
XLA Ops:
  11.9 27.3 %all_gather.66 = s32[8,512]{1,0:T(8,128)S(1)} all-gather(s32[8,128]{1,0:T(8,128)S(1)} %copy-done.39), channel_id=1, replica_groups=mesh['tp'=4,'cp'=4] {'cp'}, dimensions={1}, use_global_device_ids=true | all-gather | bytes 20480 | tf_op jit(solution)/shard_map/all_gather | solution.py:201
  58.8 49.7 %reduce-scatter.22.cloned.1.call-done = f32[256,1024]{1,0:T(8,128)} async-done(((f32[1024,1024]{1,0:T(8,128)}), f32[256,1024]{1,0:T(8,128)}) %reduce-scatter.22.cloned.1.call-update) | async-done | bytes 1048592 | tf_op jit(solution)/shard_map/reduce_scatter | solution.py:144
  111.1 31.0 %all-gather.14.cloned.1.call-done = bf16[1024,1024]{1,0:T(8,128)(2,1)} async-done(((bf16[256,1024]{1,0:T(8,128)(2,1)}), bf16[1024,1024]{1,0:T(8,128)(2,1)}) %all-gather.14.cloned.1.call-update) | async-done | bytes 2097168 | tf_op jit(solution)/shard_map/all_gather | solution.py:148
  157.2 48.8 %reduce-scatter.24.cloned.1.call-done = f32[256,1024]{1,0:T(8,128)} async-done(((f32[1024,1024]{1,0:T(8,128)}), f32[256,1024]{1,0:T(8,128)}) %reduce-scatter.24.cloned.1.call-update) | async-done | bytes 1048592 | tf_op jit(solution)/shard_map/reduce_scatter | solution.py:144
  208.4 31.2 %all-gather.16.cloned.1.call-done.x_ref = bf16[1024,1024]{1,0:T(8,128)(2,1)} async-done(((bf16[256,1024]{1,0:T(8,128)(2,1)}), bf16[1024,1024]{1,0:T(8,128)(2,1)}) %all-gather.16.cloned.1.call-update) | async-done | bytes 2097168 | tf_op jit(solution)/shard_map/all_gather | solution.py:148
  253.7 48.4 %reduce-scatter.26.cloned.1.call-done = f32[256,1024]{1,0:T(8,128)} async-done(((f32[1024,1024]{1,0:T(8,128)}), f32[256,1024]{1,0:T(8,128)}) %reduce-scatter.26.cloned.1.call-update) | async-done | bytes 1048592 | tf_op jit(solution)/shard_map/reduce_scatter | solution.py:144
  304.5 29.0 %all_to_all.48 = bf16[8,128,1024]{2,1,0:T(8,128)(2,1)S(1)} all-to-all(bf16[8,128,1024]{2,1,0:T(8,128)(2,1)} %param.14), channel_id=1, replica_groups=mesh['tp'=4,'cp'=4] {'cp'}, dimensions={0} | all-to-all | bytes 4194304 | tf_op jit(solution)/shard_map/all_to_all | solution.py:197
  357.4 47.4 %reduce-scatter.28.cloned.1.call-done = f32[256,1024]{1,0:T(8,128)} async-done(((f32[1024,1024]{1,0:T(8,128)}), f32[256,1024]{1,0:T(8,128)}) %reduce-scatter.28.cloned.1.call-update) | async-done | bytes 1048592 | tf_op jit(solution)/shard_map/reduce_scatter | solution.py:144
  410.4 30.2 %all-gather.20.cloned.1.call-done.dm_ref = bf16[1024,1024]{1,0:T(8,128)(2,1)} async-done(((bf16[256,1024]{1,0:T(8,128)(2,1)}), bf16[1024,1024]{1,0:T(8,128)(2,1)}) %all-gather.20.cloned.1.call-update) | async-done | bytes 2097168 | tf_op jit(solution)/shard_map/all_gather | solution.py:148
  461.9 48.7 %reduce-scatter.30.cloned.1.call-done = f32[256,1024]{1,0:T(8,128)} async-done(((f32[1024,1024]{1,0:T(8,128)}), f32[256,1024]{1,0:T(8,128)}) %reduce-scatter.30.cloned.1.call-update) | async-done | bytes 1048592 | tf_op jit(solution)/shard_map/reduce_scatter | solution.py:144
  515.2 31.2 %all-gather.22.cloned.1.call-done = bf16[1024,1024]{1,0:T(8,128)(2,1)} async-done(((bf16[256,1024]{1,0:T(8,128)(2,1)}), bf16[1024,1024]{1,0:T(8,128)(2,1)}) %all-gather.22.cloned.1.call-update) | async-done | bytes 2097168 | tf_op jit(solution)/shard_map/all_gather | solution.py:148
  560.8 48.7 %reduce-scatter.32.cloned.1.call-done = f32[256,1024]{1,0:T(8,128)} async-done(((f32[1024,1024]{1,0:T(8,128)}), f32[256,1024]{1,0:T(8,128)}) %reduce-scatter.32.cloned.1.call-update) | async-done | bytes 1048592 | tf_op jit(solution)/shard_map/reduce_scatter | solution.py:144
  687.4 27.1 %reduce-scatter.60.cloned.1.call-done = f32[176,1024]{1,0:T(8,128)} async-done(((f32[704,1024]{1,0:T(8,128)}), f32[176,1024]{1,0:T(8,128)}) %reduce-scatter.60.cloned.1.call-update) | async-done | bytes 720912 | tf_op jit(solution)/shard_map/reduce_scatter | solution.py:179
  716.5 33.1 %reduce-scatter.58.cloned.1.call-done = f32[256,704]{0,1:T(8,128)} async-done(((f32[1024,704]{0,1:T(8,128)}), f32[256,704]{0,1:T(8,128)}) %reduce-scatter.58.cloned.1.call-update) | async-done | bytes 720912 | tf_op jit(solution)/shard_map/reduce_scatter | solution.py:179
  751.5 32.6 %reduce-scatter.56.cloned.1.call-done = f32[256,704]{0,1:T(8,128)} async-done(((f32[1024,704]{0,1:T(8,128)}), f32[256,704]{0,1:T(8,128)}) %reduce-scatter.56.cloned.1.call-update) | async-done | bytes 720912 | tf_op jit(solution)/shard_map/reduce_scatter | solution.py:179
  786.1 33.1 %reduce-scatter.54.cloned.1.call-done = f32[256,704]{0,1:T(8,128)} async-done(((f32[1024,704]{0,1:T(8,128)}), f32[256,704]{0,1:T(8,128)}) %reduce-scatter.54.cloned.1.call-update) | async-done | bytes 720912 | tf_op jit(solution)/shard_map/reduce_scatter | solution.py:179
  821.1 33.1 %reduce-scatter.52.cloned.1.call-done = f32[256,704]{0,1:T(8,128)} async-done(((f32[1024,704]{0,1:T(8,128)}), f32[256,704]{0,1:T(8,128)}) %reduce-scatter.52.cloned.1.call-update) | async-done | bytes 720912 | tf_op jit(solution)/shard_map/reduce_scatter | solution.py:179
  869.9 36.0 %reduce-scatter.34.cloned.1.call-done = f32[256,1024]{1,0:T(8,128)} async-done(((f32[1024,1024]{1,0:T(8,128)}), f32[256,1024]{1,0:T(8,128)}) %reduce-scatter.34.cloned.1.call-update) | async-done | bytes 1048592 | tf_op jit(solution)/shard_map/reduce_scatter | solution.py:144
  910.4 18.9 %reduce-scatter.50.cloned.1.call-done = f32[64,1024]{1,0:T(8,128)} async-done(((f32[256,1024]{1,0:T(8,128)}), f32[64,1024]{1,0:T(8,128)}) %reduce-scatter.50.cloned.1.call-update) | async-done | bytes 262160 | tf_op jit(solution)/shard_map/reduce_scatter | solution.py:179
  930.2 23.1 %reduce-scatter.38.cloned.1.call-done = f32[256,256]{1,0:T(8,128)} async-done(((f32[1024,256]{1,0:T(8,128)}), f32[256,256]{1,0:T(8,128)}) %reduce-scatter.38.cloned.1.call-update) | async-done | bytes 262160 | tf_op jit(solution)/shard_map/reduce_scatter | solution.py:179
  954.3 22.5 %reduce-scatter.46.cloned.1.call-done = f32[256,256]{1,0:T(8,128)} async-done(((f32[1024,256]{1,0:T(8,128)}), f32[256,256]{1,0:T(8,128)}) %reduce-scatter.46.cloned.1.call-update) | async-done | bytes 262160 | tf_op jit(solution)/shard_map/reduce_scatter | solution.py:179
  977.8 23.1 %reduce-scatter.42.cloned.1.call-done = f32[256,256]{1,0:T(8,128)} async-done(((f32[1024,256]{1,0:T(8,128)}), f32[256,256]{1,0:T(8,128)}) %reduce-scatter.42.cloned.1.call-update) | async-done | bytes 262160 | tf_op jit(solution)/shard_map/reduce_scatter | solution.py:179
  1045.2 15.3 %all-gather.34.cloned.1.call-done = bf16[1024,704]{0,1:T(8,128)(2,1)} async-done(((bf16[256,704]{0,1:T(8,128)(2,1)}), bf16[1024,704]{0,1:T(8,128)(2,1)}) %all-gather.34.cloned.1.call-update) | async-done | bytes 1441808 | tf_op jit(solution)/shard_map/all_gather | solution.py:180
  1060.6 18.4 %all-gather.32.cloned.1.call-done = bf16[1024,704]{0,1:T(8,128)(2,1)} async-done(((bf16[256,704]{0,1:T(8,128)(2,1)}), bf16[1024,704]{0,1:T(8,128)(2,1)}) %all-gather.32.cloned.1.call-update) | async-done | bytes 1441808 | tf_op jit(solution)/shard_map/all_gather | solution.py:180
  1082.6 15.5 %all-gather.30.cloned.1.call-done = bf16[1024,704]{0,1:T(8,128)(2,1)} async-done(((bf16[256,704]{0,1:T(8,128)(2,1)}), bf16[1024,704]{0,1:T(8,128)(2,1)}) %all-gather.30.cloned.1.call-update) | async-done | bytes 1441808 | tf_op jit(solution)/shard_map/all_gather | solution.py:180
  1098.1 18.6 %all-gather.28.cloned.1.call-done = bf16[1024,704]{0,1:T(8,128)(2,1)} async-done(((bf16[256,704]{0,1:T(8,128)(2,1)}), bf16[1024,704]{0,1:T(8,128)(2,1)}) %all-gather.28.cloned.1.call-update) | async-done | bytes 1441808 | tf_op jit(solution)/shard_map/all_gather | solution.py:180
  1141.0 23.1 %reduce-scatter.36.cloned.1.call-done = f32[256,256]{1,0:T(8,128)} async-done(((f32[1024,256]{1,0:T(8,128)}), f32[256,256]{1,0:T(8,128)}) %reduce-scatter.36.cloned.1.call-update) | async-done | bytes 262160 | tf_op jit(solution)/shard_map/reduce_scatter | solution.py:179
  1165.0 22.5 %reduce-scatter.44.cloned.1.call-done = f32[256,256]{1,0:T(8,128)} async-done(((f32[1024,256]{1,0:T(8,128)}), f32[256,256]{1,0:T(8,128)}) %reduce-scatter.44.cloned.1.call-update) | async-done | bytes 262160 | tf_op jit(solution)/shard_map/reduce_scatter | solution.py:179
  1188.6 23.0 %reduce-scatter.40.cloned.1.call-done = f32[256,256]{1,0:T(8,128)} async-done(((f32[1024,256]{1,0:T(8,128)}), f32[256,256]{1,0:T(8,128)}) %reduce-scatter.40.cloned.1.call-update) | async-done | bytes 262160 | tf_op jit(solution)/shard_map/reduce_scatter | solution.py:179
  1219.9 24.6 %all-gather.26.cloned.1.call-done = bf16[1024,1024]{1,0:T(8,128)(2,1)} async-done(((bf16[256,1024]{1,0:T(8,128)(2,1)}), bf16[1024,1024]{1,0:T(8,128)(2,1)}) %all-gather.26.cloned.1.call-update) | async-done | bytes 2097168 | tf_op jit(solution)/shard_map/all_gather | solution.py:148
  1255.5 26.7 %all_gather.74 = bf16[1024,256]{1,0:T(8,128)(2,1)S(1)} all-gather(bf16[256,256]{1,0:T(8,128)(2,1)S(1)} %convert_element_type.215), channel_id=1, replica_groups=mesh['tp'=4,'cp'=4] {'cp'}, dimensions={0}, use_global_device_ids=true | all-gather | bytes 655360 | tf_op jit(solution)/shard_map/all_gather | solution.py:180
  1300.0 32.0 %psum.15 = f32[2,2,1024]{2,1,0:T(2,128)S(1)} all-reduce(f32[2,2,1024]{2,1,0:T(2,128)S(1)} %pad_maximum_fusion.7), channel_id=1, replica_groups=mesh['tp'=4,'cp'=4] {'tp','cp'}, use_global_device_ids=true, to_apply=%region_24.25 | all-reduce | flops 4096 | bytes 32768 | tf_op jit(solution)/shard_map/psum | solution.py:241
  (300 shorter events, 351.9 us)
Async XLA Ops:
  11.9 96.6 %reduce-scatter.22.cloned.1.call-start = ((), (), s32[]{:S(2)}) async-start(), calls=%async_computation.24 | async-start | bytes 5242880 | tf_op jit(solution)/shard_map/reduce_scatter | solution.py:144
  58.7 83.4 %all-gather.14.cloned.1.call-start = ((), (), s32[]{:S(2)}) async-start(), calls=%async_computation.25 | async-start | bytes 2621440 | tf_op jit(solution)/shard_map/all_gather | solution.py:148
  110.8 95.2 %reduce-scatter.24.cloned.1.call-start = ((), (), s32[]{:S(2)}) async-start(), calls=%async_computation.26 | async-start | bytes 5242880 | tf_op jit(solution)/shard_map/reduce_scatter | solution.py:144
  208.4 93.7 %reduce-scatter.26.cloned.1.call-start = ((), (), s32[]{:S(2)}) async-start(), calls=%async_computation.28 | async-start | bytes 5242880 | tf_op jit(solution)/shard_map/reduce_scatter | solution.py:144
  304.4 100.4 %reduce-scatter.28.cloned.1.call-start = ((), (), s32[]{:S(2)}) async-start(), calls=%async_computation.30 | async-start | bytes 5242880 | tf_op jit(solution)/shard_map/reduce_scatter | solution.py:144
  356.0 84.6 %all-gather.20.cloned.1.call-start = ((), (), s32[]{:S(2)}) async-start(), calls=%async_computation.31 | async-start | bytes 2621440 | tf_op jit(solution)/shard_map/all_gather | solution.py:148
  409.3 101.3 %reduce-scatter.30.cloned.1.call-start = ((), (), s32[]{:S(2)}) async-start(), calls=%async_computation.32 | async-start | bytes 5242880 | tf_op jit(solution)/shard_map/reduce_scatter | solution.py:144
  461.8 84.6 %all-gather.22.cloned.1.call-start = ((), (), s32[]{:S(2)}) async-start(), calls=%async_computation.33 | async-start | bytes 2621440 | tf_op jit(solution)/shard_map/all_gather | solution.py:148
  515.1 94.3 %reduce-scatter.32.cloned.1.call-start = ((), (), s32[]{:S(2)}) async-start(), calls=%async_computation.34 | async-start | bytes 5242880 | tf_op jit(solution)/shard_map/reduce_scatter | solution.py:144
  560.7 87.8 %all-gather.24.cloned.1.call-start = ((), (), s32[]{:S(2)}) async-start(), calls=%async_computation.35 | async-start | bytes 2621440 | tf_op jit(solution)/shard_map/all_gather | solution.py:148
  621.0 93.4 %reduce-scatter.60.cloned.1.call-start = ((), (), s32[]{:S(2)}) async-start(), calls=%async_computation.54 | async-start | bytes 3604480 | tf_op jit(solution)/shard_map/reduce_scatter | solution.py:179
  626.5 123.1 %reduce-scatter.58.cloned.1.call-start = ((), (), s32[]{:S(2)}) async-start(), calls=%async_computation.52 | async-start | bytes 3604480 | tf_op jit(solution)/shard_map/reduce_scatter | solution.py:179
  632.0 152.1 %reduce-scatter.56.cloned.1.call-start = ((), (), s32[]{:S(2)}) async-start(), calls=%async_computation.50 | async-start | bytes 3604480 | tf_op jit(solution)/shard_map/reduce_scatter | solution.py:179
  637.4 181.8 %reduce-scatter.54.cloned.1.call-start = ((), (), s32[]{:S(2)}) async-start(), calls=%async_computation.48 | async-start | bytes 3604480 | tf_op jit(solution)/shard_map/reduce_scatter | solution.py:179
  642.8 211.4 %reduce-scatter.52.cloned.1.call-start = ((), (), s32[]{:S(2)}) async-start(), calls=%async_computation.46 | async-start | bytes 3604480 | tf_op jit(solution)/shard_map/reduce_scatter | solution.py:179
  648.3 257.6 %reduce-scatter.34.cloned.1.call-start = ((), (), s32[]{:S(2)}) async-start(), calls=%async_computation.36 | async-start | bytes 5242880 | tf_op jit(solution)/shard_map/reduce_scatter | solution.py:144
  671.6 257.6 %reduce-scatter.50.cloned.1.call-start = ((), (), s32[]{:S(2)}) async-start(), calls=%async_computation.45 | async-start | bytes 1310720 | tf_op jit(solution)/shard_map/reduce_scatter | solution.py:179
  675.0 278.3 %reduce-scatter.38.cloned.1.call-start = ((), (), s32[]{:S(2)}) async-start(), calls=%async_computation.39 | async-start | bytes 1310720 | tf_op jit(solution)/shard_map/reduce_scatter | solution.py:179
  678.5 298.3 %reduce-scatter.46.cloned.1.call-start = ((), (), s32[]{:S(2)}) async-start(), calls=%async_computation.43 | async-start | bytes 1310720 | tf_op jit(solution)/shard_map/reduce_scatter | solution.py:179
  681.9 319.0 %reduce-scatter.42.cloned.1.call-start = ((), (), s32[]{:S(2)}) async-start(), calls=%async_computation.41 | async-start | bytes 1310720 | tf_op jit(solution)/shard_map/reduce_scatter | solution.py:179
  685.3 349.8 %all-gather.38.cloned.1.call-start = ((), (), s32[]{:S(2)}) async-start(), calls=%async_computation.57 | async-start | bytes 1802240 | tf_op jit(solution)/shard_map/all_gather | solution.py:180
  687.3 354.3 %all-gather.36.cloned.1.call-start = ((), (), s32[]{:S(2)}) async-start(), calls=%async_computation.55 | async-start | bytes 1802240 | tf_op jit(solution)/shard_map/all_gather | solution.py:180
  716.4 344.2 %all-gather.34.cloned.1.call-start = ((), (), s32[]{:S(2)}) async-start(), calls=%async_computation.53 | async-start | bytes 1802240 | tf_op jit(solution)/shard_map/all_gather | solution.py:180
  751.5 327.5 %all-gather.32.cloned.1.call-start = ((), (), s32[]{:S(2)}) async-start(), calls=%async_computation.51 | async-start | bytes 1802240 | tf_op jit(solution)/shard_map/all_gather | solution.py:180
  786.0 312.1 %all-gather.30.cloned.1.call-start = ((), (), s32[]{:S(2)}) async-start(), calls=%async_computation.49 | async-start | bytes 1802240 | tf_op jit(solution)/shard_map/all_gather | solution.py:180
  821.1 295.6 %all-gather.28.cloned.1.call-start = ((), (), s32[]{:S(2)}) async-start(), calls=%async_computation.47 | async-start | bytes 1802240 | tf_op jit(solution)/shard_map/all_gather | solution.py:180
  856.2 283.8 %reduce-scatter.48.cloned.1.call-start = ((), (), s32[]{:S(2)}) async-start(), calls=%async_computation.44 | async-start | bytes 1310720 | tf_op jit(solution)/shard_map/reduce_scatter | solution.py:179
  859.6 304.5 %reduce-scatter.36.cloned.1.call-start = ((), (), s32[]{:S(2)}) async-start(), calls=%async_computation.38 | async-start | bytes 1310720 | tf_op jit(solution)/shard_map/reduce_scatter | solution.py:179
  863.0 324.6 %reduce-scatter.44.cloned.1.call-start = ((), (), s32[]{:S(2)}) async-start(), calls=%async_computation.42 | async-start | bytes 1310720 | tf_op jit(solution)/shard_map/reduce_scatter | solution.py:179
  866.4 345.1 %reduce-scatter.40.cloned.1.call-start = ((), (), s32[]{:S(2)}) async-start(), calls=%async_computation.40 | async-start | bytes 1310720 | tf_op jit(solution)/shard_map/reduce_scatter | solution.py:179
  869.8 374.7 %all-gather.26.cloned.1.call-start = ((), (), s32[]{:S(2)}) async-start(), calls=%async_computation.37 | async-start | bytes 2621440 | tf_op jit(solution)/shard_map/all_gather | solution.py:148
  1249.6 83.0 %all-to-all-start.2 = ((bf16[2,512,1024]{2,0,1:T(2,128)(2,1)}), bf16[2,512,1024]{2,0,1:T(2,128)(2,1)S(1)}, u32[]{:S(2)}, u32[]{:S(2)}) async-start(bf16[2,512,1024]{2,0,1:T(2,128)(2,1)} %copy.33), calls=%async_computation.9 | async-start | bytes 4194304 | tf_op jit(solution)/shard_map/all_to_all | solution.py:242
  (60 other events, 745.6 us)
Sparse Core Ops, SparseCore 0:
  58.8 49.5 reduce-scatter.21
  111.0 31.1 all-gather.13
  157.3 48.6 reduce-scatter.23
  208.5 31.1 all-gather.15
  253.4 48.6 reduce-scatter.25
  304.5 31.1 all-gather.17
  356.1 48.6 reduce-scatter.27
  409.4 31.1 all-gather.19
  461.9 48.6 reduce-scatter.29
  515.2 31.1 all-gather.21
  560.8 48.6 reduce-scatter.31
  614.1 31.1 all-gather.23
  647.8 32.1 reduce-scatter.61
  682.3 32.1 reduce-scatter.59
  717.4 32.1 reduce-scatter.57
  751.9 32.1 reduce-scatter.55
  787.0 32.1 reduce-scatter.53
  822.1 32.1 reduce-scatter.51
  857.2 48.6 reduce-scatter.33
  908.2 20.9 reduce-scatter.49
  932.3 20.9 reduce-scatter.37
  955.8 20.9 reduce-scatter.45
  979.9 20.9 reduce-scatter.41
  1002.3 19.6 all-gather.37
  1023.5 18.0 all-gather.35
  1043.0 17.5 all-gather.33
  1062.0 16.9 all-gather.31
  1119.0 20.9 reduce-scatter.47
  1143.1 20.9 reduce-scatter.35
  1166.6 20.9 reduce-scatter.43
  1190.5 20.9 reduce-scatter.39
  1213.3 31.1 all-gather.25
  (2 shorter events, 33.8 us)

commit v2 on v1

--- a/solution.py
+++ b/solution.py
@@ -140,32 +140,192 @@
     return (xf * inv * gain).astype(BF16)
 
 
-def scatter_sum(partial):
-    return lax.psum_scatter(partial, 'tp', scatter_dimension=0, tiled=True)
-
-
-def gather_rows(own):
-    return lax.all_gather(own, 'tp', axis=0, tiled=True)
-
-
-def own_rows(full, rows):
-    return lax.dynamic_slice_in_dim(full, lax.axis_index('tp') * rows, rows, axis=0)
-
-
-def fwd_sum(partial, residual):
-    total = scatter_sum(partial)
-    return gather_rows((own_rows(residual, total.shape[0]).astype(F32) + total).astype(BF16))
-
-
-def bwd_sum(partial, x, gain, d_res):
-    total = scatter_sum(partial)
-    xf = own_rows(x, total.shape[0]).astype(F32)
-    inv = lax.rsqrt(jnp.mean(xf * xf, axis=-1, keepdims=True) + NORM_EPS)
-    normed = xf * inv
-    d_gain = jnp.sum(total * normed, axis=0)
-    d_normed = total * gain
-    d_x = inv * (d_normed - normed * jnp.mean(d_normed * normed, axis=-1, keepdims=True))
-    return gather_rows((d_x + own_rows(d_res, total.shape[0]).astype(F32)).astype(BF16)), d_gain
+class Stream:
+    def __init__(self, part, near, far, out, send, recv, first, second, a, b, index):
+        self.part, self.near, self.far, self.out = part, near, far, out
+        self.send, self.recv = send, recv
+        self.first, self.second = first, second
+        self.own, self.pass_on = index(a, b), index(a, 1 - b)
+        self.away_far, self.away = index(1 - a, 1 - b), index(1 - a, b)
+        self.copies = [None] * 6
+
+    def start(self, slot, src, dst, target):
+        self.copies[slot] = pltpu.make_async_remote_copy(
+            src_ref=src, dst_ref=dst, send_sem=self.send.at[slot], recv_sem=self.recv.at[slot],
+            device_id=target, device_id_type=pl.DeviceIdType.MESH)
+        self.copies[slot].start()
+
+    def send_away(self, slot):
+        quarter = self.away_far if slot == 0 else self.away
+        self.start(slot, self.part(quarter), self.near.at[slot], self.first)
+
+    def forward(self):
+        self.copies[0].wait_recv()
+        ref = self.part(self.pass_on)
+        ref[...] += self.near[0]
+        self.start(2, ref, self.far, self.second)
+
+    def finish(self, epilogue):
+        self.copies[1].wait_recv()
+        self.copies[2].wait_recv()
+        out = self.out(self.own)
+        out[...] = epilogue(self.part(self.own)[...] + self.near[1] + self.far[...])
+        self.start(3, out, out, self.first)
+        self.start(4, out, out, self.second)
+
+    def gather(self):
+        self.copies[4].wait_recv()
+        out = self.out(self.pass_on)
+        self.start(5, out, out, self.first)
+
+    def close(self):
+        self.copies[3].wait_recv()
+        self.copies[5].wait_recv()
+        for copy in self.copies:
+            copy.wait_send()
+
+
+def sum_kernel(kind, transposed, n_pairs, n_grads, *refs):
+    refs = list(refs)
+    lhs = [refs.pop(0) for _ in range(n_pairs)]
+    rhs = [refs.pop(0) for _ in range(n_pairs)]
+    res_ref = refs.pop(0)
+    if kind == 'bwd':
+        x_ref, gain_ref = refs.pop(0), refs.pop(0)
+    grad_in = [(refs.pop(0), refs.pop(0)) for _ in range(n_grads)]
+    out_ref = refs.pop(0)
+    if kind == 'bwd':
+        d_gain_ref = refs.pop(0)
+    grad_out = [refs.pop(0) for _ in range(n_grads)]
+    part, near, far, send, recv = [refs.pop(0) for _ in range(5)]
+    grad_scratch = [[refs.pop(0) for _ in range(3)] for _ in range(n_grads)]
+
+    tp, cp = lax.axis_index('tp'), lax.axis_index('cp')
+    z, y = tp // 2, tp % 2
+    x, core = cp // 2, cp % 2
+    z_peer = {'tp': (1 - z) * 2 + y, 'cp': cp}
+    y_peer = {'tp': z * 2 + 1 - y, 'cp': cp}
+    x_peer = {'tp': tp, 'cp': (1 - x) * 2 + core}
+    core_peer = {'tp': tp, 'cp': x * 2 + 1 - core}
+    peers = [z_peer, y_peer] + ([core_peer, x_peer] if n_grads else [])
+    barrier = pltpu.get_barrier_semaphore()
+    for peer in peers:
+        pl.semaphore_signal(barrier, inc=1, device_id=peer, device_id_type=pl.DeviceIdType.MESH)
+    pl.semaphore_wait(barrier, len(peers))
+
+    def colour(c, first, second, a, b, index):
+        return Stream(lambda q: part.at[q, c], near.at[c], far.at[c], lambda q: out_ref.at[q, c],
+                      send.at[c], recv.at[c], first, second, a, b, index)
+
+    zy = colour(0, z_peer, y_peer, z, y, lambda a, b: a * 2 + b)
+    yz = colour(1, y_peer, z_peer, y, z, lambda a, b: b * 2 + a)
+    streams = [zy, yz]
+    grads = []
+    for i in range(n_grads):
+        g_part, g_near, g_far = grad_scratch[i]
+        grads.append(Stream(lambda q, r=g_part: r.at[q], g_near, g_far, lambda q, r=grad_out[i]: r.at[q],
+                            send.at[2 + i], recv.at[2 + i], core_peer, x_peer, core, x, lambda a, b: b * 2 + a))
+
+    def compute(q):
+        total = sum(dot(l[q], r[...], NT) if transposed else dot(l[q], r[...]) for l, r in zip(lhs, rhs))
+        half = total.shape[0] // 2
+        part[q, 0] = total[:half]
+        part[q, 1] = total[half:]
+
+    def compute_grad(i):
+        a_ref, b_ref = grad_in[i]
+        g_part = grad_scratch[i][0]
+        quarter = g_part.shape[1]
+        width = b_ref.shape[1]
+        for lo in range(0, width, 256):
+            hi = min(lo + 256, width)
+            block = dot(a_ref[...], b_ref[:, lo:hi], TN)
+            for q in range(4):
+                g_part[q, :, lo:hi] = block[q * quarter:(q + 1) * quarter]
+        grads[i].send_away(0)
+        grads[i].send_away(1)
+
+    compute(zy.away_far)
+    zy.send_away(0)
+    yz.send_away(0)
+    compute(zy.away)
+    zy.send_away(1)
+    compute(yz.away)
+    yz.send_away(1)
+    compute(zy.own)
+    if n_grads:
+        compute_grad(0)
+    for s in streams:
+        s.forward()
+    for i in range(1, n_grads):
+        compute_grad(i)
+    for g in grads:
+        g.forward()
+
+    if kind == 'bwd':
+        d_gain = []
+
+    def epilogue(c):
+        def run(total):
+            res = res_ref[zy.own, c].astype(F32)
+            if kind == 'fwd':
+                return (res + total).astype(BF16)
+            xf = x_ref[zy.own, c].astype(F32)
+            inv = lax.rsqrt(jnp.mean(xf * xf, axis=-1, keepdims=True) + NORM_EPS)
+            normed = xf * inv
+            d_gain.append(jnp.sum(total * normed, axis=0, keepdims=True))
+            d_normed = total * gain_ref[...]
+            d_x = inv * (d_normed - normed * jnp.mean(d_normed * normed, axis=-1, keepdims=True))
+            return (d_x + res).astype(BF16)
+        return run
+
+    zy.finish(epilogue(0))
+    yz.finish(epilogue(1))
+    if kind == 'bwd':
+        d_gain_ref[...] = d_gain[0] + d_gain[1]
+    for g in grads[:1]:
+        g.finish(lambda total: total.astype(BF16))
+    for s in streams:
+        s.gather()
+    for g in grads[1:]:
+        g.finish(lambda total: total.astype(BF16))
+    for g in grads:
+        g.gather()
+    for s in streams + grads:
+        s.close()
+
+
+def tp_sum(kind, collective_id, pairs, residual, transposed=False, x=None, gain=None, grads=()):
+    rows, width = residual.shape
+    quarter = rows // 4
+    halves = (4, 2, quarter // 2, width)
+    operands = [l.reshape(4, quarter, l.shape[1]) for l, _ in pairs] + [r for _, r in pairs] + [residual.reshape(halves)]
+    out_shape = [jax.ShapeDtypeStruct(halves, BF16)]
+    if kind == 'bwd':
+        operands += [x.reshape(halves), gain[None, :]]
+        out_shape.append(jax.ShapeDtypeStruct((1, width), F32))
+    scratch = [pltpu.VMEM(halves, F32), pltpu.VMEM((2, 2) + halves[2:], F32), pltpu.VMEM((2,) + halves[2:], F32),
+               pltpu.SemaphoreType.DMA((2 + len(grads), 6)), pltpu.SemaphoreType.DMA((2 + len(grads), 6))]
+    flops = sum(2 * rows * l.shape[1] * width for l, _ in pairs)
+    for a, b in grads:
+        operands += [a, b]
+        block = (a.shape[1] // 4, b.shape[1])
+        out_shape.append(jax.ShapeDtypeStruct((4,) + block, BF16))
+        scratch += [pltpu.VMEM((4,) + block, F32), pltpu.VMEM((2,) + block, F32), pltpu.VMEM(block, F32)]
+        flops += 2 * rows * a.shape[1] * b.shape[1]
+    outs = pl.pallas_call(
+        functools.partial(sum_kernel, kind, transposed, len(pairs), len(grads)),
+        out_shape=out_shape,
+        in_specs=vmem_specs(len(operands)), out_specs=vmem_specs(len(out_shape)),
+        scratch_shapes=scratch,
+        compiler_params=pltpu.CompilerParams(collective_id=collective_id, has_side_effects=True, vmem_limit_bytes=62 * 1024 * 1024),
+        cost_estimate=pl.CostEstimate(flops=flops, bytes_accessed=16 << 20, transcendentals=0),
+        name=f"tp_sum_{collective_id}",
+    )(*operands)
+    total = outs[0].reshape(rows, width)
+    d_gain = outs[1][0] if kind == 'bwd' else None
+    grad_outs = [o.reshape(a.shape[1], b.shape[1]) for o, (a, b) in zip(outs[len(outs) - len(grads):], grads)]
+    return total, d_gain, grad_outs
 
 
 def mlp_up(x1, gain, w_gate, w_lin):
@@ -207,39 +367,47 @@
         saved = []
         for l in range(layers):
             h, q, k, v, o = attn_fwd(x, g_attn[l], w_q[l], w_k[l], w_v[l], table, key_add, seq)
-            x1 = fwd_sum(dot(o, w_o[l]), x)
+            x1 = tp_sum('fwd', 0, [(o, w_o[l])], x)[0]
             h2, gate_pre, lin_pre, gated = mlp_up(x1, g_mlp[l], w_gate[l], w_lin[l])
             saved.append((x, h, q, k, v, o, x1, h2, gate_pre, lin_pre, gated))
             if l < layers - 1:
-                x = fwd_sum(dot(gated, w_out[l]), x1)
+                x = tp_sum('fwd', 1, [(gated, w_out[l])], x1)[0]
 
         grads = [None] * layers
         d_table = jnp.zeros_like(table)
+        waiting = None
         for l in reversed(range(layers)):
             x, h, q, k, v, o, x1, h2, gate_pre, lin_pre, gated = saved[l]
             d_gated = dot(dy, w_out[l], NT)
             gelu_val, gelu_pull = jax.vjp(lambda gate_in: jax.nn.gelu(gate_in, approximate=True), gate_pre)
             d_lin = (d_gated * gelu_val).astype(BF16)
             d_gate = gelu_pull(d_gated * lin_pre)[0].astype(BF16)
-            d_mid, d_gm = bwd_sum(dot(d_gate, w_gate[l], NT) + dot(d_lin, w_lin[l], NT), x1, g_mlp[l], dy)
-            d_wout = cp_sum(dot(gated, dy, TN))
-            d_wgate = cp_sum(dot(h2, d_gate, TN))
-            d_wlin = cp_sum(dot(h2, d_lin, TN))
+            work = [(gated, dy), (h2, d_gate)] if waiting is None else [(gated, dy)] + waiting
+            d_mid, d_gm, done = tp_sum('bwd', 2 + 2 * (layers - 1 - l), [(d_gate, w_gate[l]), (d_lin, w_lin[l])], dy, True, x1, g_mlp[l], work)
+            d_wout = done[0]
+            if waiting is None:
+                d_wgate = done[1]
+                work = [(h2, d_lin), (o, d_mid)]
+            else:
+                grads[l + 1] += tuple(done[1:])
+                work = [(h2, d_gate), (h2, d_lin)]
             dq, dk, dv, dt = attn_bwd(d_mid, w_o[l], q, k, v, o, table, key_add, seq)
             d_table = d_table + dt
-            part = dot(dq, w_q[l], NT) + dot(dk, w_k[l], NT) + dot(dv, w_v[l], NT)
-            d_x, d_ga = bwd_sum(part, x, g_attn[l], d_mid)
-            d_wo = cp_sum(dot(o, d_mid, TN))
-            d_wq = cp_sum(dot(h, dq, TN))
-            d_wk = cp_sum(dot(h, dk, TN))
-            d_wv = cp_sum(dot(h, dv, TN))
-            grads[l] = (d_ga, d_gm, d_wq, d_wk, d_wv, d_wo, d_wgate, d_wlin, d_wout)
+            d_x, d_ga, done = tp_sum('bwd', 3 + 2 * (layers - 1 - l), [(dq, w_q[l]), (dk, w_k[l]), (dv, w_v[l])], d_mid, True, x, g_attn[l], work)
+            if waiting is None:
+                d_wlin, d_wo = done
+                waiting = [(h, dq), (h, dk), (h, dv)]
+                grads[l] = (d_ga, d_gm, d_wo, d_wgate, d_wlin, d_wout)
+            else:
+                d_wgate, d_wlin = done
+                grads[l] = (d_ga, d_gm, cp_sum(dot(o, d_mid, TN)), d_wgate, d_wlin, d_wout)
+                grads[l] += tuple(cp_sum(dot(h, d, TN)) for d in (dq, dk, dv))
             dy = d_x
         stacked = [jnp.stack([g[i] for g in grads]) for i in range(9)]
         d_bias = jnp.sum(jnp.where(onehot[None], d_table[:, None, :], 0.0), axis=2)
         d_bias = lax.psum(d_bias, 'cp').T
         d_gains = lax.psum(jnp.stack(stacked[:2]), ('tp', 'cp'))
         d_x = lax.all_to_all(dy.reshape(own_batch, seq, width), 'cp', split_axis=1, concat_axis=0, tiled=True)
-        return (d_x, d_bias, d_gains[0], d_gains[1]) + tuple(stacked[2:])
+        return (d_x, d_bias, d_gains[0], d_gains[1]) + tuple(stacked[6:]) + tuple(stacked[2:6])
 
     return jax.shard_map(local_program, mesh=mesh, in_specs=(seq_spec, seq_spec, P(None, 'cp'), P(None, 'tp')) + weight_specs, out_specs=(seq_spec, P(None, 'tp')) + weight_specs, check_vma=False)

time: 1350 us -> 831 us (0.62)
  waiting for transfers between devices: 880 us -> 0.12 us
  Pallas kernels: 43.6 us -> 529 us
  blocking collectives: 176 us -> 110 us
  matrix products: 115 us -> 53.4 us
  local copies, waits for them, and re-layouts: 33.7 us -> 80.1 us
  other arithmetic: 66.9 us -> 24.9 us
    pallas_call x0 -> x7, Pallas kernels: none -> 485 us  [tp_sum(): pl.pallas_call(functools.partial(sum_kernel, kind, transposed, len(pairs)...]
    reduce_scatter x14 -> x4, waiting for transfers between devices: 328 us -> 0.05 us  [cp_sum(): lax.psum_scatter(part, 'cp', scatter_dimension=0, tiled=True).astype(BF16)]
    reduce_scatter x7 -> x0, waiting for transfers between devices: 328 us -> none  [scatter_sum(): return lax.psum_scatter(partial, 'tp', scatter_dimension=0, tiled=True)]
    all_gather x13 -> x0, waiting for transfers between devices: 223 us -> none  [the longest x7 149 us: gather_rows(): return lax.all_gather(own, 'tp', axis=0, tiled=True)]
    dot_general x33 -> x10, matrix products: 115 us -> 53.4 us  [dot(): return lax.dot_general(a, b, dims, preferred_element_type=F32)]
    all_gather x8 -> x4, blocking collectives: 81.3 us -> 29.9 us  [cp_sum(): return lax.all_gather(own, 'cp', axis=0, tiled=True)]
    all_to_all x1 -> x0, blocking collectives: 29 us -> none  [to_batch(): lax.all_to_all(arr, 'cp', split_axis=0, concat_axis=1, tiled=True)]
    convert_element_type x14 -> x4, other arithmetic: 19.8 us -> 3.97 us  [cp_sum(): lax.psum_scatter(part, 'cp', scatter_dimension=0, tiled=True).astype(BF16)]
  transfers between devices with their start and end apart: 36 -> 7, of which waited for: 31 -> 0; matrix products, arithmetic and copies ran while one was open for 8% -> 11% of each run, Pallas kernels for 1% -> 34%
where the time goes in v2:
time: 831 us; the launch traced here: 827 us
  Pallas kernels  529 us (64%)
  blocking collectives  110 us (13%)
  local copies, waits for them, and re-layouts  80.1 us (10%)
  matrix products  53.4 us (6%)
  other arithmetic  24.9 us (3%)
  between operations  14.8 us (2%)
  starting transfers between devices  14 us (2%)
    pallas_call x7, Pallas kernels, tp_sum(): pl.pallas_call(functools.partial(sum_kernel, kind, transposed, len(pairs)...  485 us
    dot_general x10, matrix products, dot(): return lax.dot_general(a, b, dims, preferred_element_type=F32)  53.4 us
    psum x1, blocking collectives, local_program(): d_gains = lax.psum(jnp.stack(stacked[:2]), ('tp', 'cp'))  32.1 us
    all_gather x4, blocking collectives, cp_sum(): return lax.all_gather(own, 'cp', axis=0, tiled=True)  29.9 us
    unnamed x140, local copies, waits for them, and re-layouts  29.5 us
    pallas_call x2, Pallas kernels, attn_bwd(): pl.pallas_call(functools.partial(attn_bwd_kernel, seq, batch, heads), out...  28.2 us
    all_gather x1, blocking collectives, local_program(): mask_all = lax.all_gather(key_mask, 'cp', axis=1, tiled=True)  27.3 us
    psum x1, blocking collectives, local_program(): d_bias = lax.psum(d_bias, 'cp').T  21 us
  transfers between devices with their start and end apart: 7, of which 0 were waited for; matrix products, arithmetic and copies ran while one was open for 11% of the time, Pallas kernels for 34%

profile of v2, /device:TPU:0, one launch (start us, length us, event | category | flops | bytes accessed | tf_op | source)
XLA Modules:
  0.0 826.8 jit_solution(7107899803454352276)
XLA Ops:
  7.2 4.5 all-to-all-start.1
  11.7 27.3 %all_gather.15 = s32[8,512]{1,0:T(8,128)S(1)} all-gather(s32[8,128]{1,0:T(8,128)S(1)} %copy-done.62), channel_id=1, replica_groups=mesh['tp'=4,'cp'=4] {'cp'}, dimensions={1}, use_global_device_ids=true | all-gather | bytes 20480 | tf_op jit(solution)/shard_map/all_gather | solution.py:361
  57.3 4.5 all-to-all-start
  65.2 7.8 attn_fwd.2
  77.6 61.7 %tp_sum_0.2.refs_2_.refs_5_ = bf16[4,2,128,1024]{3,2,1,0:T(8,128)(2,1)} custom-call(bf16[4,256,256]{2,1,0:T(8,128)(2,1)} %bitcast.138, bf16[256,1024]{1,0:T(8,128)(2,1)} %get-tuple-element.93.refs_1_.wo_ref, bf16[4,2,128,1024]{3,2,1,0:T(8,128)(2,1)} %bitcast.153), custom_call_target="tpu_custom_call" | custom-call | flops 536870912 | bytes 16777216 | tf_op jit(solution)/shard_map/tp_sum_0/pallas_call | solution.py:316
  142.4 4.2 fusion.45
  146.7 3.5 copy.125
  150.1 3.9 copy.122
  154.0 8.3 %multiply_convert_fusion.5 = (bf16[1024,704]{1,0:T(8,128)(2,1)}, f32[1024,704]{1,0:T(8,128)}) fusion(f32[1024,704]{1,0:T(8,128)} %copy.125, f32[1024,704]{1,0:T(8,128)} %copy.122, bf16[1024,1024]{1,0:T(8,128)(2,1)} %bitcast.162, bf16[2,1024,704]{1,2,0:T(8,128)(2,1)} %param.24), kind=kOutput, calls=%fused_computation.23 | convolution fusion | flops 1482883072 | bytes 14155776 | tf_op jit(solution)/shard_map/dot_general | solution.py:31
  162.3 57.8 %tp_sum_1.1.refs_2_.refs_7_ = bf16[4,2,128,1024]{3,2,1,0:T(8,128)(2,1)} custom-call(bf16[4,256,704]{2,1,0:T(8,128)(2,1)} %bitcast.167, bf16[704,1024]{1,0:T(8,128)(2,1)} %slice_bitcast_fusion.refs_1_, bf16[4,2,128,1024]{3,2,1,0:T(8,128)(2,1)} %tp_sum_0.2.refs_2_.refs_5_), custom_call_target="tpu_custom_call" | custom-call | flops 1476395008 | bytes 16777216 | tf_op jit(solution)/shard_map/tp_sum_1/pallas_call | solution.py:316
  220.2 7.8 attn_fwd.3
  232.6 55.6 %tp_sum_0.3.refs_5_ = bf16[4,2,128,1024]{3,2,1,0:T(8,128)(2,1)} custom-call(bf16[4,256,256]{2,1,0:T(8,128)(2,1)} %bitcast.139, bf16[256,1024]{1,0:T(8,128)(2,1)} %get-tuple-element.92.refs_1_.wo_ref, bf16[4,2,128,1024]{3,2,1,0:T(8,128)(2,1)} %tp_sum_1.1.refs_2_.refs_7_), custom_call_target="tpu_custom_call" | custom-call | flops 536870912 | bytes 16777216 | tf_op jit(solution)/shard_map/tp_sum_0/pallas_call | solution.py:316
  295.8 3.6 copy.139
  301.9 5.8 fusion.46
  311.1 3.5 copy.138
  317.3 9.9 %multiply_convert_fusion.3 = (bf16[1024,704]{1,0:T(8,128)(2,1)}, bf16[1024,704]{1,0:T(8,128)(2,1)}, bf16[1024,704]{1,0:T(8,128)(2,1)}) fusion(f32[1024,704]{1,0:T(8,128)S(1)} %copy-done.42, f32[1024,704]{1,0:T(8,128)} %copy.134, f32[1024,704]{1,0:T(8,128)} %copy.138, bf16[1024,1024]{1,0:T(8,128)(2,1)} %bitcast.159, bf16[2,1024,704]{1,2,0:T(8,128)(2,1)} %param.23), kind=kOutput, calls=%fused_computation.21 | convolution fusion | flops 1494417408 | bytes 17039360 | tf_op jit(solution)/shard_map/dot_general | solution.py:31
  327.2 74.5 %tp_sum_2.1 = (bf16[4,2,128,1024]{3,2,1,0:T(8,128)(2,1)}, f32[1,1024]{1,0:T(1,128)}, bf16[4,176,1024]{2,1,0:T(8,128)(2,1)}, bf16[4,256,704]{2,1,0:T(8,128)(2,1)}) custom-call(bf16[4,256,704]{2,1,0:T(8,128)(2,1)} %bitcast.195, bf16[4,256,704]{2,1,0:T(8,128)(2,1)} %bitcast.168, bf16[1024,704]{1,0:T(8,128)(2,1)} %bitcast.172, bf16[1024,704]{1,0:T(8,128)(2,1)} %bitcast.174, ...), custom_call_target="tpu_custom_call" | custom-call | flops 5905580032 | bytes 16777216 | tf_op jit(solution)/shard_map/tp_sum_2/pallas_call | solution.py:316
  403.8 14.1 %attn_bwd.2 = (bf16[1024,256]{1,0:T(8,128)(2,1)S(1)}, bf16[1024,256]{1,0:T(8,128)(2,1)S(1)}, bf16[1024,256]{1,0:T(8,128)(2,1)S(1)}, f32[4,1024]{1,0:T(4,128)S(1)}) custom-call(bf16[1024,1024]{1,0:T(8,128)(2,1)} %bitcast.150, bf16[256,1024]{1,0:T(8,128)(2,1)S(1)} %copy-done.6, bf16[1024,256]{1,0:T(8,128)(2,1)S(1)} %copy-done.31, ...), custom_call_target="tpu_custom_call" | custom-call | flops 1879048192 | bytes 8388608 | tf_op jit(solution)/shard_map/attn_bwd/pallas_call | solution.py:126
  420.4 66.3 %tp_sum_3.1 = (bf16[4,2,128,1024]{3,2,1,0:T(8,128)(2,1)}, f32[1,1024]{1,0:T(1,128)}, bf16[4,256,704]{2,1,0:T(8,128)(2,1)}, bf16[4,64,1024]{2,1,0:T(8,128)(2,1)}) custom-call(bf16[4,256,256]{2,1,0:T(8,128)(2,1)} %bitcast.140, bf16[4,256,256]{2,1,0:T(8,128)(2,1)} %bitcast.141, bf16[4,256,256]{2,1,0:T(8,128)(2,1)} %bitcast.142, bf16[1024,256]{1,0:T(8,128)(2,1)} %copy-done.5, ...), custom_call_target="tpu_custom_call" | custom-call | flops 3623878656 | bytes 16777216 | tf_op jit(solution)/shard_map/tp_sum_3/pallas_call | solution.py:316
  486.7 10.1 %multiply_convert_fusion.2 = (bf16[1024,704]{1,0:T(8,128)(2,1)}, bf16[1024,704]{1,0:T(8,128)(2,1)}) fusion(f32[1024,704]{1,0:T(8,128)} %copy.125, f32[1024,704]{1,0:T(8,128)} %copy.122, f32[1024,704]{1,0:T(8,128)} %get-tuple-element.109, bf16[1024,1024]{1,0:T(8,128)(2,1)} %bitcast.191, bf16[2,704,1024]{2,1,0:T(8,128)(2,1)} %param.25), kind=kOutput, calls=%fused_computation.19 | convolution fusion | flops 1492975616 | bytes 15859712 | tf_op jit(solution)/shard_map/dot_general | solution.py:31
  496.8 79.5 %tp_sum_4.1 = (bf16[4,2,128,1024]{3,2,1,0:T(8,128)(2,1)}, f32[1,1024]{1,0:T(1,128)}, bf16[4,176,1024]{2,1,0:T(8,128)(2,1)}, bf16[4,256,256]{2,1,0:T(8,128)(2,1)}...) custom-call(bf16[4,256,704]{2,1,0:T(8,128)(2,1)} %bitcast.194, bf16[4,256,704]{2,1,0:T(8,128)(2,1)} %bitcast.193, ...), custom_call_target="tpu_custom_call" | custom-call | flops 6039797760 | bytes 16777216 | tf_op jit(solution)/shard_map/tp_sum_4/pallas_call | solution.py:316
  578.4 14.0 %attn_bwd.3 = (bf16[1024,256]{1,0:T(8,128)(2,1)S(1)}, bf16[1024,256]{1,0:T(8,128)(2,1)S(1)}, bf16[1024,256]{1,0:T(8,128)(2,1)S(1)}, f32[4,1024]{1,0:T(4,128)S(1)}) custom-call(bf16[1024,1024]{1,0:T(8,128)(2,1)} %bitcast.155, bf16[256,1024]{1,0:T(8,128)(2,1)S(1)} %copy-done.4, bf16[1024,256]{1,0:T(8,128)(2,1)S(1)} %copy-done.25, ...), custom_call_target="tpu_custom_call" | custom-call | flops 1879048192 | bytes 8388608 | tf_op jit(solution)/shard_map/attn_bwd/pallas_call | solution.py:126
  605.3 89.9 %tp_sum_5.1 = (bf16[4,2,128,1024]{3,2,1,0:T(8,128)(2,1)}, f32[1,1024]{1,0:T(1,128)}, bf16[4,256,704]{2,1,0:T(8,128)(2,1)}, bf16[4,256,704]{2,1,0:T(8,128)(2,1)}) custom-call(bf16[4,256,256]{2,1,0:T(8,128)(2,1)} %bitcast.143, bf16[4,256,256]{2,1,0:T(8,128)(2,1)} %bitcast.144, bf16[4,256,256]{2,1,0:T(8,128)(2,1)} %bitcast.145, bf16[1024,256]{1,0:T(8,128)(2,1)} %copy-done.12, ...), custom_call_target="tpu_custom_call" | custom-call | flops 4563402752 | bytes 16777216 | tf_op jit(solution)/shard_map/tp_sum_5/pallas_call | solution.py:316
  695.2 5.1 copy.145
  700.3 4.5 all-to-all-start.2
  717.0 21.0 %psum.14 = f32[32,4]{0,1:T(4,128)} all-reduce(f32[32,4]{0,1:T(4,128)S(1)} %bitcast.189), channel_id=1, replica_groups=mesh['tp'=4,'cp'=4] {'cp'}, use_global_device_ids=true, to_apply=%region_4.5 | all-reduce | flops 128 | bytes 1024 | tf_op jit(solution)/shard_map/psum | solution.py:408
  738.0 32.1 %psum.15 = f32[2,2,1024]{2,1,0:T(2,128)S(1)} all-reduce(f32[2,2,1024]{2,1,0:T(2,128)S(1)} %pad_maximum_fusion.7), channel_id=1, replica_groups=mesh['tp'=4,'cp'=4] {'tp','cp'}, use_global_device_ids=true, to_apply=%region_5.6 | all-reduce | flops 4096 | bytes 32768 | tf_op jit(solution)/shard_map/psum | solution.py:409
  778.3 3.5 copy.146
  784.9 8.0 all_gather.16
  792.8 7.3 all_gather.17
  800.1 7.4 all_gather.18
  808.5 7.3 all_gather.19
  (205 shorter events, 97.7 us)
Async XLA Ops:
  7.2 4.6 copy-start.62
  7.2 50.1 %all-to-all-start.1 = ((bf16[8,128,1024]{2,1,0:T(8,128)(2,1)}), bf16[8,128,1024]{2,1,0:T(8,128)(2,1)}, u32[]{:S(2)}, u32[]{:S(2)}) async-start(bf16[8,128,1024]{2,1,0:T(8,128)(2,1)} %param.13), calls=%async_computation.1 | async-start | bytes 4194304 | tf_op jit(solution)/shard_map/all_to_all | solution.py:357
  51.9 89.7 %copy-start.57 = (f32[1,1024]{1,0:T(1,128)}, f32[1,1024]{1,0:T(1,128)S(1)}, u32[]{:S(2)}) copy-start(f32[1,1024]{1,0:T(1,128)S(1)} %get-tuple-element.105.refs_6_) | copy-start | bytes 12292
  51.9 262.7 %copy-start.59 = (f32[1,1024]{1,0:T(1,128)}, f32[1,1024]{1,0:T(1,128)S(1)}, u32[]{:S(2)}) copy-start(f32[1,1024]{1,0:T(1,128)S(1)} %get-tuple-element.104.refs_6_) | copy-start | bytes 12292
  51.9 13.3 %copy-start.16 = (f32[1,1024]{1,0:T(1,128)}, f32[1,1024]{1,0:T(1,128)S(1)}, u32[]{:S(2)}) copy-start(f32[1,1024]{1,0:T(1,128)S(1)} %get-tuple-element.103.g_ref.refs_8_) | copy-start | bytes 12292
  52.0 168.2 %copy-start.15 = (f32[1,1024]{1,0:T(1,128)}, f32[1,1024]{1,0:T(1,128)S(1)}, u32[]{:S(2)}) copy-start(f32[1,1024]{1,0:T(1,128)S(1)} %get-tuple-element.102.g_ref.refs_8_) | copy-start | bytes 12292
  53.4 11.8 %copy-start.12 = (bf16[1024,256]{1,0:T(8,128)(2,1)}, bf16[1024,256]{1,0:T(8,128)(2,1)S(1)}, u32[]{:S(2)}) copy-start(bf16[1024,256]{1,0:T(8,128)(2,1)S(1)} %get-tuple-element.99.wq_ref.refs_3_) | copy-start | bytes 1572868
  53.4 166.7 %copy-start.5 = (bf16[1024,256]{1,0:T(8,128)(2,1)}, bf16[1024,256]{1,0:T(8,128)(2,1)S(1)}, u32[]{:S(2)}) copy-start(bf16[1024,256]{1,0:T(8,128)(2,1)S(1)} %get-tuple-element.98.wq_ref.refs_3_) | copy-start | bytes 1572868
  57.3 7.9 copy-start.13
  57.3 162.8 %copy-start.7 = (bf16[1024,256]{1,0:T(8,128)(2,1)}, bf16[1024,256]{1,0:T(8,128)(2,1)S(1)}, u32[]{:S(2)}) copy-start(bf16[1024,256]{1,0:T(8,128)(2,1)S(1)} %get-tuple-element.94.wv_ref.refs_5_) | copy-start | bytes 1572868
  57.3 162.8 %copy-start.8 = (bf16[1024,256]{1,0:T(8,128)(2,1)}, bf16[1024,256]{1,0:T(8,128)(2,1)S(1)}, u32[]{:S(2)}) copy-start(bf16[1024,256]{1,0:T(8,128)(2,1)S(1)} %get-tuple-element.113.wk_ref.refs_4_) | copy-start | bytes 1572868
  57.3 242.1 %all-to-all-start = ((bf16[8,128,1024]{2,1,0:T(8,128)(2,1)}), bf16[8,128,1024]{2,1,0:T(8,128)(2,1)}, u32[]{:S(2)}, u32[]{:S(2)}) async-start(bf16[8,128,1024]{2,1,0:T(8,128)(2,1)} %param.14), calls=%async_computation | async-start | bytes 4194304 | tf_op jit(solution)/shard_map/all_to_all | solution.py:357
  61.8 720.0 %reduce-scatter.5.cloned.1.call-start = ((), (), s32[]{:S(2)}) async-start(), calls=%async_computation.7 | async-start | bytes 1310720 | tf_op jit(solution)/shard_map/reduce_scatter | solution.py:339
  301.3 6.3 copy-start.39
  327.2 74.6 %copy-start.3 = (bf16[1024,256]{1,0:T(8,128)(2,1)S(1)}, bf16[1024,256]{1,0:T(8,128)(2,1)}, u32[]{:S(2)}) copy-start(bf16[1024,256]{1,0:T(8,128)(2,1)} %copy-done.2) | copy-start | bytes 1572868
  327.2 74.6 %copy-start.6 = (bf16[256,1024]{1,0:T(8,128)(2,1)S(1)}, bf16[256,1024]{1,0:T(8,128)(2,1)}, u32[]{:S(2)}) copy-start(bf16[256,1024]{1,0:T(8,128)(2,1)} %get-tuple-element.92.refs_1_.wo_ref) | copy-start | bytes 1572868
  327.2 74.6 %copy-start.31 = (bf16[1024,256]{1,0:T(8,128)(2,1)S(1)}, bf16[1024,256]{1,0:T(8,128)(2,1)}, u32[]{:S(2)}) copy-start(bf16[1024,256]{1,0:T(8,128)(2,1)} %copy-done.30) | copy-start | bytes 1572868
  496.7 79.5 %copy-start.1 = (bf16[1024,256]{1,0:T(8,128)(2,1)S(1)}, bf16[1024,256]{1,0:T(8,128)(2,1)}, u32[]{:S(2)}) copy-start(bf16[1024,256]{1,0:T(8,128)(2,1)} %copy-done) | copy-start | bytes 1572868
  496.8 79.5 %copy-start.4 = (bf16[256,1024]{1,0:T(8,128)(2,1)S(1)}, bf16[256,1024]{1,0:T(8,128)(2,1)}, u32[]{:S(2)}) copy-start(bf16[256,1024]{1,0:T(8,128)(2,1)} %get-tuple-element.93.refs_1_.wo_ref) | copy-start | bytes 1572868
  496.8 79.5 %copy-start.25 = (bf16[1024,256]{1,0:T(8,128)(2,1)S(1)}, bf16[1024,256]{1,0:T(8,128)(2,1)}, u32[]{:S(2)}) copy-start(bf16[1024,256]{1,0:T(8,128)(2,1)} %copy-done.24) | copy-start | bytes 1572868
  578.4 14.9 %copy-start.23 = (bf16[1024,1024]{1,0:T(8,128)(2,1)S(1)}, bf16[1024,1024]{1,0:T(8,128)(2,1)}, u32[]{:S(2)}) copy-start(bf16[1024,1024]{1,0:T(8,128)(2,1)} %copy-done.22) | copy-start | bytes 6291460
  595.0 187.9 %reduce-scatter.7.cloned.1.call-start = ((), (), s32[]{:S(2)}) async-start(), calls=%async_computation.8 | async-start | bytes 1310720 | tf_op jit(solution)/shard_map/reduce_scatter | solution.py:339
  598.5 185.5 %reduce-scatter.9.cloned.1.call-start = ((), (), s32[]{:S(2)}) async-start(), calls=%async_computation.9 | async-start | bytes 1310720 | tf_op jit(solution)/shard_map/reduce_scatter | solution.py:339
  700.3 78.0 %all-to-all-start.2 = ((bf16[2,512,1024]{2,0,1:T(2,128)(2,1)}), bf16[2,512,1024]{2,0,1:T(2,128)(2,1)}, u32[]{:S(2)}, u32[]{:S(2)}) async-start(bf16[2,512,1024]{2,0,1:T(2,128)(2,1)} %copy.145), calls=%async_computation.2 | async-start | bytes 4194304 | tf_op jit(solution)/shard_map/all_to_all | solution.py:410
  704.8 102.7 %reduce-scatter.11.cloned.1.call-start = ((), (), s32[]{:S(2)}) async-start(), calls=%async_computation.10 | async-start | bytes 1310720 | tf_op jit(solution)/shard_map/reduce_scatter | solution.py:339
  711.7 26.2 %copy-start.63 = (f32[1,1024]{1,0:T(1,128)S(1)}, f32[1,1024]{1,0:T(1,128)}, u32[]{:S(2)}) copy-start(f32[1,1024]{1,0:T(1,128)} %get-tuple-element.71) | copy-start | bytes 12292
  711.7 26.2 %copy-start.65 = (f32[1,1024]{1,0:T(1,128)S(1)}, f32[1,1024]{1,0:T(1,128)}, u32[]{:S(2)}) copy-start(f32[1,1024]{1,0:T(1,128)} %get-tuple-element.70) | copy-start | bytes 12292
  711.7 26.2 %copy-start.64 = (f32[1,1024]{1,0:T(1,128)S(1)}, f32[1,1024]{1,0:T(1,128)}, u32[]{:S(2)}) copy-start(f32[1,1024]{1,0:T(1,128)} %get-tuple-element.69) | copy-start | bytes 12292
  711.8 26.2 %copy-start.66 = (f32[1,1024]{1,0:T(1,128)S(1)}, f32[1,1024]{1,0:T(1,128)}, u32[]{:S(2)}) copy-start(f32[1,1024]{1,0:T(1,128)} %get-tuple-element.68) | copy-start | bytes 12292
  781.8 34.0 %copy-start.56 = (bf16[4,256,256]{2,1,0:T(8,128)(2,1)S(1)}, bf16[4,256,256]{2,1,0:T(8,128)(2,1)}, u32[]{:S(2)}) copy-start(bf16[4,256,256]{2,1,0:T(8,128)(2,1)} %get-tuple-element.73) | copy-start | bytes 1572868
  782.8 34.0 %copy-start.55 = (bf16[4,256,256]{2,1,0:T(8,128)(2,1)S(1)}, bf16[4,256,256]{2,1,0:T(8,128)(2,1)}, u32[]{:S(2)}) copy-start(bf16[4,256,256]{2,1,0:T(8,128)(2,1)} %get-tuple-element.74) | copy-start | bytes 1572868
  800.1 17.8 %copy-start.54 = (bf16[4,256,256]{2,1,0:T(8,128)(2,1)S(1)}, bf16[4,256,256]{2,1,0:T(8,128)(2,1)}, u32[]{:S(2)}) copy-start(bf16[4,256,256]{2,1,0:T(8,128)(2,1)} %get-tuple-element.75) | copy-start | bytes 1572868
  (43 other events, 85.0 us)
Sparse Core Ops, SparseCore 0:
  595.1 20.3 reduce-scatter.4
  618.6 26.9 reduce-scatter.6
  648.6 26.9 reduce-scatter.8
  708.5 27.3 reduce-scatter.10

commit v3 on v1

v3 whole, which is shorter than its diff:
```python
import functools
import jax
import jax.numpy as jnp
import numpy as np
from jax import lax
from jax.experimental import pallas as pl
from jax.experimental.pallas import tpu as pltpu
from jax.sharding import PartitionSpec as P

NORM_EPS = 1e-6
MASK_NEG = -1e9
HEAD = 64
F32 = jnp.float32
BF16 = jnp.bfloat16
NT = (((1,), (1,)), ((), ()))
TN = (((0,), (0,)), ((), ()))


def rel_bucket(rel_pos):
    distance = jnp.minimum(jnp.abs(rel_pos), 128)
    distance_sq = distance * distance
    log_part = 8 + sum((distance_sq >= 64 * 2 ** power).astype(jnp.int32) for power in range(1, 8))
    return jnp.where(distance < 8, distance, log_part) + 16 * (rel_pos > 0).astype(jnp.int32)


def bucket_onehot(seq):
    rel = jnp.arange(2 * seq) - seq
    return (rel_bucket(rel)[None, :] == jnp.arange(32)[:, None]) & (jnp.arange(2 * seq) > 0)[None, :]


def dot(a, b, dims=(((1,), (0,)), ((), ()))):
    return lax.dot_general(a, b, dims, preferred_element_type=F32)


def toeplitz(row, seq):
    base = pltpu.roll(row, seq, 1)
    rows = jnp.concatenate([base if i == 0 else pltpu.roll(base, i, 1) for i in range(8)], axis=0)
    size = 8
    while size < seq:
        rows = jnp.concatenate([rows, pltpu.roll(rows, size, 1)], axis=0)
        size *= 2
    return rows[:, :seq]


def diag_sums(mat, seq):
    wide = jnp.concatenate([mat, jnp.zeros_like(mat)], axis=1)
    size = seq
    while size > 1:
        half = size // 2
        wide = wide[:half] + pltpu.roll(wide[half:size], 2 * seq - half, 1)
        size = half
    return pltpu.roll(wide, seq, 1)


def place():
    tp, cp = lax.axis_index('tp'), lax.axis_index('cp')
    z, y = tp // 2, tp % 2
    x, core = cp // 2, cp % 2
    peers = {'z': (1 - z, y, x, core), 'y': (z, 1 - y, x, core), 'x': (z, y, 1 - x, core), 'core': (z, y, x, 1 - core),
             'zy': (1 - z, 1 - y, x, core), 'xc': (z, y, 1 - x, 1 - core)}
    ids = {name: {'tp': p[0] * 2 + p[1], 'cp': p[2] * 2 + p[3]} for name, p in peers.items()}
    return tp, cp, z, y, x, core, ids


def meet(ids, names):
    barrier = pltpu.get_barrier_semaphore()
    for name in names:
        pl.semaphore_signal(barrier, inc=1, device_id=ids[name], device_id_type=pl.DeviceIdType.MESH)
    pl.semaphore_wait(barrier, len(names))


def remote(src, dst, send, recv, target):
    copy = pltpu.make_async_remote_copy(src_ref=src, dst_ref=dst, send_sem=send, recv_sem=recv,
                                        device_id=target, device_id_type=pl.DeviceIdType.MESH)
    copy.start()
    return copy


class Stream:
    def __init__(self, part, near, far, out, send, recv, first, second, a, b, index):
        self.part, self.near, self.far, self.out = part, near, far, out
        self.send, self.recv = send, recv
        self.first, self.second = first, second
        self.own, self.pass_on = index(a, b), index(a, 1 - b)
        self.away_far, self.away = index(1 - a, 1 - b), index(1 - a, b)
        self.copies = {}

    def start(self, slot, src, dst, target):
        self.copies[slot] = remote(src, dst, self.send.at[slot], self.recv.at[slot], target)

    def send_away(self, slot):
        quarter = self.away_far if slot == 0 else self.away
        self.start(slot, self.part(quarter), self.near.at[slot], self.first)

    def forward(self):
        self.copies[0].wait_recv()
        ref = self.part(self.pass_on)
        ref[...] += self.near[0]
        self.start(2, ref, self.far, self.second)

    def total(self):
        self.copies[1].wait_recv()
        self.copies[2].wait_recv()
        return self.part(self.own)[...] + self.near[1] + self.far[...]

    def publish(self):
        out = self.out(self.own)
        self.start(3, out, out, self.first)
        self.start(4, out, out, self.second)

    def finish(self):
        self.out(self.own)[...] = self.total().astype(BF16)
        self.publish()

    def gather(self):
        self.copies[4].wait_recv()
        out = self.out(self.pass_on)
        self.start(5, out, out, self.first)

    def close(self):
        self.copies[3].wait_recv()
        self.copies[5].wait_recv()
        for copy in self.copies.values():
            copy.wait_send()


def colours(part, near, far, out, send, recv, ids, z, y):
    def make(c, first, second, a, b, index):
        return Stream(lambda q: part.at[q[0], q[1], c], None if near is None else near.at[c], None if far is None else far.at[c],
                      lambda q: out(q, c), send.at[c], recv.at[c], ids[first], ids[second], a, b, index)
    return [make(0, 'z', 'y', z, y, lambda a, b: (a, b)), make(1, 'y', 'z', y, z, lambda a, b: (b, a))]


def grad_stream(part, near, far, out, send, recv, ids, x, core):
    return Stream(lambda q: part.at[q], near, far, lambda q: out.at[q], send, recv, ids['core'], ids['x'], core, x, lambda a, b: b * 2 + a)


def grad_into(part, a, b):
    quarter, width = part.shape[1], part.shape[2]
    for lo in range(0, width, 256):
        block = dot(a, b[:, lo:lo + 256], TN)
        for q in range(4):
            part[q, :, lo:lo + 256] = block[q * quarter:(q + 1) * quarter]


def norm_parts(rows):
    xf = rows.astype(F32)
    inv = lax.rsqrt(jnp.mean(xf * xf, axis=-1, keepdims=True) + NORM_EPS)
    return inv, xf * inv


def norm(rows, gain):
    return (norm_parts(rows)[1] * gain).astype(BF16)


def norm_back(d_norm, rows, gain):
    inv, normed = norm_parts(rows)
    d_normed = d_norm * gain
    return inv * (d_normed - normed * jnp.mean(d_normed * normed, axis=-1, keepdims=True)), d_norm * normed


def exchange_kernel(x_ref, mask_ref, wo_ref, xo_ref, mo_ref, wf_ref, send, recv):
    tp, cp, z, y, x, core, ids = place()
    names = ['x', 'core', 'xc', 'z', 'y', 'zy']
    meet(ids, names)
    copies, weights = [], []
    for i, name in enumerate(names[:3]):
        copies.append(remote(mask_ref.at[ids[name]['cp']], mo_ref.at[cp], send.at[i], recv.at[i], ids[name]))
        copies.append(remote(x_ref.at[ids[name]['cp']], xo_ref.at[:, cp], send.at[3 + i], recv.at[3 + i], ids[name]))
    for i, name in enumerate(names[3:]):
        weights.append(remote(wo_ref.at[core], wf_ref.at[core, tp], send.at[6 + i], recv.at[6 + i], ids[name]))
    mo_ref[cp] = mask_ref[cp]
    for b in range(2):
        xo_ref[b, cp] = x_ref[cp, b]
    for layer in range(2):
        wf_ref[layer, tp] = wo_ref[layer]
    for i, name in enumerate(names[3:]):
        weights[i].wait_recv()
        got = wf_ref.at[core, ids[name]['tp']]
        copies.append(remote(got, got, send.at[9 + i], recv.at[9 + i], ids['core']))
    for copy in copies:
        copy.wait_recv()
    for copy in copies + weights:
        copy.wait_send()


def exchange(x_in, key_mask, w_o):
    batch, blk, width = x_in.shape
    return pl.pallas_call(
        exchange_kernel,
        out_shape=[jax.ShapeDtypeStruct((2, 4, blk, width), BF16), jax.ShapeDtypeStruct((4, 2, blk), jnp.int32),
                   jax.ShapeDtypeStruct((2, 4) + w_o.shape[1:], BF16)],
        in_specs=vmem_specs(3), out_specs=vmem_specs(3),
        scratch_shapes=[pltpu.SemaphoreType.DMA((12,)), pltpu.SemaphoreType.DMA((12,))],
        compiler_params=pltpu.CompilerParams(collective_id=0, has_side_effects=True, vmem_limit_bytes=40 << 20),
        name="exchange",
    )(x_in.reshape(4, 2, blk, width), key_mask.reshape(4, 2, blk), w_o)


def key_add(mask_ref, b):
    row = jnp.concatenate([mask_ref[j, pl.ds(b, 1), :] for j in range(4)], axis=1)
    return jnp.where(row > 0, 0.0, MASK_NEG).astype(F32)


def exp_scores(q, k, bias, add):
    s = dot(q, k, NT) + bias + add
    e = jnp.exp(s - jnp.max(s, axis=-1, keepdims=True))
    return e, jnp.sum(e, axis=-1, keepdims=True)


def attn_kernel(layer, seq, with_dy, *refs):
    refs = list(refs)
    x_ref, g_ref, wq_all, wk_all, wv_all, t_ref, mask_ref, wf_all = [refs.pop(0) for _ in range(8)]
    if with_dy:
        dy_ref = refs.pop(0)
    x1_ref, q_ref, k_ref, v_ref, o_ref = [refs.pop(0) for _ in range(5)]
    if with_dy:
        dyo_ref = refs.pop(0)
    wq_ref, wk_ref, wv_ref, wf_ref, wsem, bias_ref, of_ref, send, recv, osend, orecv = [refs.pop(0) for _ in range(11)]
    loads = load_layer(layer, [wq_all, wk_all, wv_all, wf_all], [wq_ref, wk_ref, wv_ref, wf_ref], wsem)
    tp, cp, z, y, x, core, ids = place()
    heads = t_ref.shape[0]
    meet(ids, ['z', 'y', 'zy'] + (['x', 'core', 'xc'] if with_dy else []))
    dys = []
    if with_dy:
        for i, name in enumerate(['x', 'core', 'xc']):
            dys.append(remote(dy_ref.at[ids[name]['cp']], dyo_ref.at[:, cp], osend.at[3 + i], orecv.at[3 + i], ids[name]))
        for b in range(2):
            dyo_ref[b, cp] = dy_ref[cp, b]
    out = []
    for copy in loads[:3]:
        copy.wait()
    for step in range(2):
        b = 1 - z if step == 0 else z
        for half in range(2):
            rows = pl.ds(half * 256, 256)
            h = norm(x_ref[b, rows, :], g_ref[layer:layer + 1, :])
            q_ref[b, rows, :] = dot(h, wq_ref[...]).astype(BF16)
            k_ref[b, rows, :] = dot(h, wk_ref[...]).astype(BF16)
            v_ref[b, rows, :] = dot(h, wv_ref[...]).astype(BF16)
        add = key_add(mask_ref, b)
        for head in range(heads):
            if step == 0:
                bias_ref[head] = toeplitz(t_ref[head:head + 1, :], seq)
            cols = pl.ds(head * HEAD, HEAD)
            e, total = exp_scores(q_ref[b, :, cols], k_ref[b, :, cols], bias_ref[head], add)
            o = (dot(e.astype(BF16), v_ref[b, :, cols]) / total).astype(BF16)
            o_ref[b, 0, :, cols] = o[:seq // 2]
            o_ref[b, 1, :, cols] = o[seq // 2:]
        if step == 0:
            out.append(remote(o_ref.at[b, 1 - y], of_ref.at[tp], osend.at[0], orecv.at[0], ids['zy']))
            out.append(remote(o_ref.at[b, y], of_ref.at[tp], osend.at[1], orecv.at[1], ids['z']))
        else:
            out.append(remote(o_ref.at[b, 1 - y], of_ref.at[tp], osend.at[2], orecv.at[2], ids['y']))
    of_ref[tp] = o_ref[z, y]
    loads[3].wait()
    for copy in out:
        copy.wait_recv()
    streams = colours(None, None, None, lambda q, c: x1_ref.at[q[0], q[1], c], send, recv, ids, z, y)
    for c, s in enumerate(streams):
        rows = pl.ds(c * 128, 128)
        total = sum(dot(of_ref[j, rows, :], wf_ref[j]) for j in range(4))
        res = x_ref[z, pl.ds(pl.multiple_of(y * 256 + c * 128, 128), 128), :].astype(F32)
        x1_ref[z, y, c] = (res + total).astype(BF16)
        s.publish()
    for s in streams:
        s.gather()
    for s in streams:
        s.close()
    for copy in out:
        copy.wait_send()
    for copy in dys:
        copy.wait()


def load_layer(layer, stacks, refs, sems):
    copies = [pltpu.make_async_copy(w.at[layer], r, sems.at[i]) for i, (w, r) in enumerate(zip(stacks, refs))]
    for copy in copies:
        copy.start()
    return copies


def layer_scratch(*stacks):
    return [pltpu.VMEM(w.shape[1:], w.dtype) for w in stacks] + [pltpu.SemaphoreType.DMA((len(stacks),))]


def any_specs(n):
    return [pl.BlockSpec(memory_space=pl.ANY)] * n


def attn_layer(layer, collective_id, x, gains, w_q, w_k, w_v, table, mask, w_full, d_y=None):
    seq = 512
    width, cols = w_q.shape[1], w_q.shape[2]
    operands = [x.reshape(2, seq, width), gains, w_q, w_k, w_v, table, mask, w_full]
    in_specs = vmem_specs(2) + any_specs(3) + vmem_specs(2) + any_specs(1)
    head_shape = jax.ShapeDtypeStruct((2, seq, cols), BF16)
    out_shape = [jax.ShapeDtypeStruct((2, 2, 2, 128, width), BF16)] + [head_shape] * 3 + [jax.ShapeDtypeStruct((2, 2, seq // 2, cols), BF16)]
    if d_y is not None:
        operands.append(d_y.reshape(4, 2, 128, width))
        in_specs += vmem_specs(1)
        out_shape.append(jax.ShapeDtypeStruct((2, 4, 128, width), BF16))
    dma = pltpu.SemaphoreType.DMA
    return pl.pallas_call(
        functools.partial(attn_kernel, layer, seq, d_y is not None),
        out_shape=out_shape, in_specs=in_specs, out_specs=vmem_specs(len(out_shape)),
        scratch_shapes=layer_scratch(w_q, w_k, w_v, w_full) + [pltpu.VMEM((table.shape[0], seq, seq), F32), pltpu.VMEM((4, 256, cols), BF16), dma((2, 6)), dma((2, 6)), dma((6,)), dma((6,))],
        compiler_params=pltpu.CompilerParams(collective_id=collective_id, has_side_effects=True, vmem_limit_bytes=48 << 20),
        cost_estimate=pl.CostEstimate(flops=4 << 30, bytes_accessed=16 << 20, transcendentals=0),
        name=f"attn_fwd_{layer}",
    )(*operands)


def gelu_parts(g):
    inner = np.float32(np.sqrt(2 / np.pi)) * (g + 0.044715 * (g * g * g))
    t = jnp.tanh(inner)
    cdf = 0.5 * (1.0 + t)
    slope = cdf + 0.5 * g * (1.0 - t * t) * np.float32(np.sqrt(2 / np.pi)) * (1.0 + 3 * 0.044715 * (g * g))
    return g * cdf, slope


def order(z, y):
    return [(1 - z, 1 - y), (1 - z, y), (z, 1 - y), (z, y)]


def mlp_fwd_kernel(layer, x1_ref, g_ref, wg_all, wl_all, wo_all, out_ref, wg_ref, wl_ref, wo_ref, wsem, part, near, far, send, recv):
    loads = load_layer(layer, [wg_all, wl_all, wo_all], [wg_ref, wl_ref, wo_ref], wsem)
    tp, cp, z, y, x, core, ids = place()
    meet(ids, ['z', 'y'])
    for copy in loads:
        copy.wait()
    zy, yz = streams = colours(part, near, far, lambda q, c: out_ref.at[q[0], q[1], c], send, recv, ids, z, y)

    def compute(q):
        h2 = norm(x1_ref[q].reshape(256, -1), g_ref[layer:layer + 1, :])
        gated = (gelu_parts(dot(h2, wg_ref[...], NT))[0] * dot(h2, wl_ref[...], NT)).astype(BF16)
        part[q] = dot(gated, wo_ref[...]).reshape(part.shape[2:])

    quarters = order(z, y)
    compute(quarters[0])
    zy.send_away(0)
    yz.send_away(0)
    compute(quarters[1])
    zy.send_away(1)
    compute(quarters[2])
    yz.send_away(1)
    compute(quarters[3])
    for s in streams:
        s.forward()
    for c, s in enumerate(streams):
        out_ref[z, y, c] = (x1_ref[z, y, c].astype(F32) + s.total()).astype(BF16)
        s.publish()
    for s in streams:
        s.gather()
    for s in streams:
        s.close()


def sum_scratch(width, blocks=()):
    return [pltpu.VMEM((2, 2, 2) + blocks, F32), pltpu.VMEM((2, 2) + blocks, F32), pltpu.VMEM((2,) + blocks, F32)]


def mlp_fwd(layer, collective_id, x1, gains, wg_t, wl_t, w_out):
    dma = pltpu.SemaphoreType.DMA
    return pl.pallas_call(
        functools.partial(mlp_fwd_kernel, layer),
        out_shape=jax.ShapeDtypeStruct(x1.shape, BF16),
        in_specs=vmem_specs(2) + any_specs(3), out_specs=pl.BlockSpec(memory_space=pltpu.VMEM),
        scratch_shapes=layer_scratch(wg_t, wl_t, w_out) + sum_scratch(0, x1.shape[3:]) + [dma((2, 6)), dma((2, 6))],
        compiler_params=pltpu.CompilerParams(collective_id=collective_id, has_side_effects=True, vmem_limit_bytes=48 << 20),
        cost_estimate=pl.CostEstimate(flops=5 << 30, bytes_accessed=16 << 20, transcendentals=0),
        name=f"mlp_fwd_{layer}",
    )(x1, gains, wg_t, wl_t, w_out)


def mlp_bwd_kernel(layer, x1_ref, dy_ref, g_ref, wg_all, wl_all, wo_all, dm_ref, dg_ref, lin_part, gout_ref, ggate_ref,
                   wg_ref, wl_ref, wo_ref, wsem, part, near, far, h2_ref, gated_ref, dgate_ref, dlin_ref, p0, n0, f0, p1, n1, f1, send, recv):
    loads = load_layer(layer, [wg_all, wl_all, wo_all], [wg_ref, wl_ref, wo_ref], wsem)
    tp, cp, z, y, x, core, ids = place()
    meet(ids, ['z', 'y', 'x', 'core'])
    zy, yz = streams = colours(part, near, far, lambda q, c: dm_ref.at[q[0], q[1], c], send, recv, ids, z, y)
    g_out = grad_stream(p0, n0, f0, gout_ref, send.at[2], recv.at[2], ids, x, core)
    g_gate = grad_stream(p1, n1, f1, ggate_ref, send.at[3], recv.at[3], ids, x, core)
    gain = g_ref[layer:layer + 1, :]
    for copy in loads:
        copy.wait()

    def compute(q):
        h2 = norm(x1_ref[q].reshape(256, -1), gain)
        rows = pl.ds(pl.multiple_of((q[0] * 2 + q[1]) * 256, 256), 256)
        h2_ref[rows, :] = h2
        value, slope = gelu_parts(dot(h2, wg_ref[...], NT))
        lin = dot(h2, wl_ref[...], NT)
        gated_ref[rows, :] = (value * lin).astype(BF16)
        d_gated = dot(dy_ref[q].reshape(256, -1), wo_ref[...], NT)
        d_lin = (d_gated * value).astype(BF16)
        d_gate = (d_gated * lin * slope).astype(BF16)
        dlin_ref[rows, :] = d_lin
        dgate_ref[rows, :] = d_gate
        part[q] = (dot(d_gate, wg_ref[...]) + dot(d_lin, wl_ref[...])).reshape(part.shape[2:])

    quarters = order(z, y)
    compute(quarters[0])
    zy.send_away(0)
    yz.send_away(0)
    compute(quarters[1])
    zy.send_away(1)
    compute(quarters[2])
    yz.send_away(1)
    compute(quarters[3])
    grad_into(p0, gated_ref[...], dy_ref[...].reshape(h2_ref.shape))
    g_out.send_away(0)
    g_out.send_away(1)
    for s in streams:
        s.forward()
    grad_into(p1, dgate_ref[...], h2_ref)
    g_gate.send_away(0)
    g_gate.send_away(1)
    g_out.forward()
    grad_into(lin_part, dlin_ref[...], h2_ref)
    g_gate.forward()
    d_gain = 0.0
    for c, s in enumerate(streams):
        d_x, dg = norm_back(s.total(), x1_ref[z, y, c], gain)
        dm_ref[z, y, c] = (d_x + dy_ref[z, y, c].astype(F32)).astype(BF16)
        s.publish()
        d_gain = d_gain + jnp.sum(dg, axis=0, keepdims=True)
    dg_ref[...] = d_gain
    g_out.finish()
    for s in streams:
        s.gather()
    g_out.gather()
    g_gate.finish()
    g_gate.gather()
    for s in streams + [g_out, g_gate]:
        s.close()


def mlp_bwd(layer, collective_id, x1, dy, gains, wg_t, wl_t, w_out):
    dma = pltpu.SemaphoreType.DMA
    ff, width = wg_t.shape[1:]
    block = (ff // 4, width)
    rows = 1024
    grad_scratch = [pltpu.VMEM((4,) + block, F32), pltpu.VMEM((2,) + block, F32), pltpu.VMEM(block, F32)]
    out_shape = [jax.ShapeDtypeStruct(x1.shape, BF16), jax.ShapeDtypeStruct((1, width), F32), jax.ShapeDtypeStruct((4,) + block, F32)]
    out_shape += [jax.ShapeDtypeStruct((4,) + block, BF16)] * 2
    return pl.pallas_call(
        functools.partial(mlp_bwd_kernel, layer),
        out_shape=out_shape,
        in_specs=vmem_specs(3) + any_specs(3), out_specs=vmem_specs(5),
        scratch_shapes=layer_scratch(wg_t, wl_t, w_out) + sum_scratch(0, x1.shape[3:]) + [pltpu.VMEM((rows, width), BF16)] + [pltpu.VMEM((rows, ff), BF16)] * 3
        + grad_scratch * 2 + [dma((4, 6)), dma((4, 6))],
        compiler_params=pltpu.CompilerParams(collective_id=collective_id, has_side_effects=True, vmem_limit_bytes=60 << 20),
        cost_estimate=pl.CostEstimate(flops=12 << 30, bytes_accessed=32 << 20, transcendentals=0),
        name=f"mlp_bwd_{layer}",
    )(x1, dy, gains, wg_t, wl_t, w_out)


def attn_bwd_kernel(layer, seq, last, *refs):
    refs = list(refs)
    x_ref, dm_ref, lin_part, q_ref, k_ref, v_ref, o_ref, g_ref, wq_all, wk_all, wv_all, wo_all, t_ref, mask_ref = [refs.pop(0) for _ in range(14)]
    if last:
        small_ref = refs.pop(0)
    dx_ref = refs.pop(0)
    if last:
        small_out = refs.pop(0)
    else:
        dg_ref, dt_ref = refs.pop(0), refs.pop(0)
    grad_out = [refs.pop(0) for _ in range(5)]
    wq_ref, wk_ref, wv_ref, wo_ref, wsem = [refs.pop(0) for _ in range(5)]
    loads = load_layer(layer, [wq_all, wk_all, wv_all, wo_all], [wq_ref, wk_ref, wv_ref, wo_ref], wsem)
    part, near, far = [refs.pop(0) for _ in range(3)]
    bias_ref, acc_ref, do_ref, dq_ref, dk_ref, dv_ref, h_ref = [refs.pop(0) for _ in range(7)]
    lin_near, lin_far = refs.pop(0), refs.pop(0)
    grad_scratch = [[refs.pop(0) for _ in range(3)] for _ in range(4)]
    send, recv = refs.pop(0), refs.pop(0)
    if last:
        own_ref, acc_small, got_small, csend, crecv = [refs.pop(0) for _ in range(5)]
    tp, cp, z, y, x, core, ids = place()
    heads = t_ref.shape[0]
    across, deep = part.shape[3], part.shape[4]
    meet(ids, ['z', 'y', 'x', 'core'] + (['xc'] if last else []))
    if last:
        def region(q, c):
            return dx_ref.at[:, q[0], q[1], c]
    else:
        def region(q, c):
            return dx_ref.at[q[0], :, q[1], c]
    zy, yz = streams = colours(part, near, far, region, send, recv, ids, z, y)
    g_lin = grad_stream(lin_part, lin_near, lin_far, grad_out[0], send.at[2], recv.at[2], ids, x, core)
    g_o, g_q, g_k, g_v = [grad_stream(s[0], s[1], s[2], out, send.at[3 + i], recv.at[3 + i], ids, x, core)
                          for i, (s, out) in enumerate(zip(grad_scratch, grad_out[1:]))]
    gain = g_ref[layer:layer + 1, :]
    g_lin.send_away(0)
    g_lin.send_away(1)
    for copy in loads:
        copy.wait()

    def attend(b, step):
        add = key_add(mask_ref, b)
        d_mid = dm_ref[b].reshape(seq, -1)
        do_ref[...] = dot(d_mid, wo_ref[...], NT).astype(BF16)
        for head in range(heads):
            if step == 0:
                bias_ref[head] = toeplitz(t_ref[head:head + 1, :], seq)
            cols = pl.ds(head * HEAD, HEAD)
            q, k, v, do = q_ref[b, :, cols], k_ref[b, :, cols], v_ref[b, :, cols], do_ref[:, cols]
            e, total = exp_scores(q, k, bias_ref[head], add)
            p = e * (1.0 / total)
            row_dot = jnp.sum(do.astype(F32) * o_ref[b, :, cols].astype(F32), axis=-1, keepdims=True)
            ds = p * (dot(do, v, NT) - row_dot)
            if step == 0:
                acc_ref[head] = ds
            else:
                sums = diag_sums(acc_ref[head] + ds, seq)
                if last:
                    acc_small[0, 8 + head:9 + head, :] = small_ref[8 + head:9 + head, :] + sums
                else:
                    dt_ref[head:head + 1, :] = sums
            dsl = ds.astype(BF16)
            dq_ref[b, :, cols] = dot(dsl, k).astype(BF16)
            dk_ref[b, :, cols] = dot(dsl, q, TN).astype(BF16)
            dv_ref[b, :, cols] = dot(p.astype(BF16), do, TN).astype(BF16)
            if step == 0 and head == 0:
                g_lin.forward()
        for half in range(2):
            rows = pl.ds(half * 256, 256)
            h_ref[pl.ds(pl.multiple_of(b * seq + half * 256, 256), 256), :] = norm(x_ref[b, rows, :], gain)

    def compute(q):
        def rows(ref):
            whole = ref[q[0]].reshape(across, 2, 2 * deep, ref.shape[-1]) if across > 1 else None
            if across == 1:
                return ref[q[0], pl.ds(pl.multiple_of(q[1] * 2 * deep, 2 * deep), 2 * deep), :]
            pieces = [ref[q[0], pl.ds(pl.multiple_of(j * 4 * deep + q[1] * 2 * deep, 2 * deep), 2 * deep), :] for j in range(across)]
            return jnp.concatenate(pieces, axis=0)
        total = dot(rows(dq_ref), wq_ref[...], NT) + dot(rows(dk_ref), wk_ref[...], NT) + dot(rows(dv_ref), wv_ref[...], NT)
        total = total.reshape(across, 2, deep, total.shape[-1])
        for c in range(2):
            part[q[0], q[1], c] = total[:, c]

    quarters = order(z, y)
    attend(1 - z, 0)
    compute(quarters[0])
    zy.send_away(0)
    yz.send_away(0)
    compute(quarters[1])
    zy.send_away(1)
    grad_into(grad_scratch[0][0], o_ref[...].reshape(2 * seq, -1), dm_ref[...].reshape(2 * seq, -1))
    g_o.send_away(0)
    g_o.send_away(1)
    attend(z, 1)
    compute(quarters[2])
    yz.send_away(1)
    g_o.forward()
    compute(quarters[3])
    for s in streams:
        s.forward()
    for g, scratch, d_ref in zip([g_q, g_k, g_v], grad_scratch[1:], [dq_ref, dk_ref, dv_ref]):
        grad_into(scratch[0], h_ref[...], d_ref[...].reshape(2 * seq, -1))
        g.send_away(0)
        g.send_away(1)
    g_lin.finish()
    g_o.finish()
    for g in [g_q, g_k, g_v]:
        g.forward()

    d_gain = 0.0
    moves = []
    for c, s in enumerate(streams):
        def own(ref):
            pieces = [ref[z, pl.ds(pl.multiple_of(j * 4 * deep + y * 2 * deep + c * deep, deep), deep), :] for j in range(across)]
            return jnp.concatenate(pieces, axis=0)
        d_x, dg = norm_back(s.total().reshape(across * deep, -1), own(x_ref), gain)
        d_gain = d_gain + jnp.sum(dg, axis=0, keepdims=True)
        d_x = (d_x + own(dm_ref).astype(F32)).astype(BF16).reshape(across, deep, -1)
        if last:
            own_ref[c] = d_x
            dx_ref[cp, z, y, c] = own_ref[c, cp]
            moves.append([remote(own_ref.at[c, ids[name]['cp']], dx_ref.at[cp, z, y, c], csend.at[c, i], crecv.at[c, i], ids[name])
                          for i, name in enumerate(['x', 'xc', 'core'])])
        else:
            dx_ref[z, :, y, c] = d_x
            s.publish()
    if last:
        acc_small[0, 0:4, :] = jnp.concatenate([small_ref[0:3, :], d_gain], axis=0)
        acc_small[0, 4:8, :] = jnp.zeros((4, d_gain.shape[1]), F32)
        acc_small[0, 12:16, :] = jnp.zeros((4, d_gain.shape[1]), F32)
        for c, s in enumerate(streams):
            for copy in moves[c]:
                copy.wait_recv()
            s.publish()
        smalls = []
        for i, name in enumerate(['x', 'core', 'z', 'y']):
            rows = pl.ds(0, 16 if i < 2 else 8)
            smalls.append(remote(acc_small.at[i, rows], got_small.at[i, rows], csend.at[2, i], crecv.at[2, i], ids[name]))
            smalls[i].wait_recv()
            acc_small[i + 1, rows, :] = acc_small[i, rows, :] + got_small[i, rows, :]
        small_out[0:8, :] = acc_small[4, 0:8, :]
        small_out[8:16, :] = acc_small[2, 8:16, :]
        for copy in smalls + moves[0] + moves[1]:
            copy.wait_send()
    else:
        dg_ref[...] = d_gain
    for s in streams:
        s.gather()
    g_lin.gather()
    g_o.gather()
    for g in [g_q, g_k, g_v]:
        g.finish()
    for g in [g_q, g_k, g_v]:
        g.gather()
    for s in streams + [g_lin, g_o, g_q, g_k, g_v]:
        s.close()


def attn_bwd(layer, collective_id, x, d_mid, lin_part, q, k, v, o, gains, w_q, w_k, w_v, w_o, table, mask, small=None):
    seq, width = 512, w_q.shape[1]
    cols = w_q.shape[2]
    last = small is not None
    dma = pltpu.SemaphoreType.DMA
    operands = [x.reshape(2, seq, width), d_mid.reshape(2, seq, width), lin_part, q, k, v, o.reshape(2, seq, cols), gains, w_q, w_k, w_v, w_o, table, mask]
    in_specs = vmem_specs(8) + any_specs(4) + vmem_specs(2)
    blocks = (4, 32, width) if last else (1, 128, width)
    if last:
        operands.append(small)
        in_specs += vmem_specs(1)
        out_shape = [jax.ShapeDtypeStruct((4, 2, 2, 2, 32, width), BF16), jax.ShapeDtypeStruct((16, width), F32)]
    else:
        out_shape = [jax.ShapeDtypeStruct((2, 1, 2, 2, 128, width), BF16), jax.ShapeDtypeStruct((1, width), F32), jax.ShapeDtypeStruct(table.shape, F32)]
    shapes = [(cols // 4, width)] + [(width // 4, cols)] * 3
    lin_block = lin_part.shape[1:]
    out_shape += [jax.ShapeDtypeStruct((4,) + s, BF16) for s in [lin_block] + shapes]
    scratch = layer_scratch(w_q, w_k, w_v, w_o) + sum_scratch(0, blocks) + [pltpu.VMEM((table.shape[0], seq, seq), F32)] * 2 + [pltpu.VMEM((seq, cols), BF16)]
    scratch += [pltpu.VMEM((2, seq, cols), BF16)] * 3 + [pltpu.VMEM((2 * seq, width), BF16)]
    scratch += [pltpu.VMEM((2,) + lin_block, F32), pltpu.VMEM(lin_block, F32)]
    for s in shapes:
        scratch += [pltpu.VMEM((4,) + s, F32), pltpu.VMEM((2,) + s, F32), pltpu.VMEM(s, F32)]
    scratch += [dma((7, 6)), dma((7, 6))]
    if last:
        scratch += [pltpu.VMEM((2, 4, 32, width), BF16), pltpu.VMEM((5, 16, width), F32), pltpu.VMEM((4, 16, width), F32), dma((3, 4)), dma((3, 4))]
    return pl.pallas_call(
        functools.partial(attn_bwd_kernel, layer, seq, last),
        out_shape=out_shape, in_specs=in_specs, out_specs=vmem_specs(len(out_shape)),
        scratch_shapes=scratch,
        compiler_params=pltpu.CompilerParams(collective_id=collective_id, has_side_effects=True, vmem_limit_bytes=62 << 20),
        cost_estimate=pl.CostEstimate(flops=8 << 30, bytes_accessed=32 << 20, transcendentals=0),
        name=f"attn_bwd_{layer}",
    )(*operands)


def vmem_specs(n):
    return [pl.BlockSpec(memory_space=pltpu.VMEM)] * n


def solution(mesh):
    seq_spec = P(None, 'cp', None)
    col_spec = P(None, None, 'tp')
    row_spec = P(None, 'tp', None)
    weight_specs = (P(), P(), col_spec, col_spec, col_spec, row_spec, col_spec, col_spec, row_spec)

    def local_program(x_in, d_y, key_mask, rel_bias, g_attn, g_mlp, w_q, w_k, w_v, w_o, w_gate, w_lin, w_out):
        width = x_in.shape[2]
        quarters = (2, 2, 2, 128, width)
        onehot = bucket_onehot(512)
        table = jnp.sum(jnp.where(onehot[None], rel_bias.T[:, :, None], 0.0), axis=1)
        wg_t, wl_t = jnp.swapaxes(w_gate, 1, 2), jnp.swapaxes(w_lin, 1, 2)
        x0, mask, w_full = exchange(x_in, key_mask, w_o)

        a0, q0, k0, v0, o0, dy = attn_layer(0, 1, x0, g_attn, w_q, w_k, w_v, table, mask, w_full, d_y)
        x1 = mlp_fwd(0, 2, a0, g_mlp, wg_t, wl_t, w_out)
        a1, q1, k1, v1, o1 = attn_layer(1, 3, x1, g_attn, w_q, w_k, w_v, table, mask, w_full)

        dm, dgm1, lin, out1, gate1 = mlp_bwd(1, 4, a1, dy.reshape(quarters), g_mlp, wg_t, wl_t, w_out)
        dx, dga1, dt1, lin1, wo1, wq1, wk1, wv1 = attn_bwd(1, 5, x1, dm, lin, q1, k1, v1, o1, g_attn, w_q, w_k, w_v, w_o, table, mask)
        dm, dgm0, lin, out0, gate0 = mlp_bwd(0, 6, a0, dx.reshape(quarters), g_mlp, wg_t, wl_t, w_out)
        small = jnp.concatenate([dga1, dgm1, dgm0, jnp.zeros((5, width), F32), dt1, jnp.zeros((4, width), F32)], axis=0)
        d_x, small, lin0, wo0, wq0, wk0, wv0 = attn_bwd(0, 7, x0, dm, lin, q0, k0, v0, o0, g_attn, w_q, w_k, w_v, w_o, table, mask, small)

        def both(first, second, like, swap=False):
            shape = (like.shape[2], like.shape[1]) if swap else like.shape[1:]
            pair = jnp.stack([first.reshape(shape), second.reshape(shape)])
            return jnp.swapaxes(pair, 1, 2) if swap else pair

        d_bias = jnp.sum(jnp.where(onehot[None], small[8:12][:, None, :], 0.0), axis=2).T
        d_ga = jnp.stack([small[3], small[0]])
        d_gm = jnp.stack([small[2], small[1]])
        return (d_x.reshape(x_in.shape), d_bias, d_ga, d_gm, both(wq0, wq1, w_q), both(wk0, wk1, w_k), both(wv0, wv1, w_v),
                both(wo0, wo1, w_o), both(gate0, gate1, w_gate, True), both(lin0, lin1, w_lin, True), both(out0, out1, w_out))

    return jax.shard_map(local_program, mesh=mesh, in_specs=(seq_spec, seq_spec, P(None, 'cp'), P(None, 'tp')) + weight_specs, out_specs=(seq_spec, P(None, 'tp')) + weight_specs, check_vma=False)
```

time: 1350 us -> 526 us (0.39)
  waiting for transfers between devices: 880 us -> 0 us
  Pallas kernels: 43.6 us -> 483 us
  blocking collectives: 176 us -> 0 us
  matrix products: 115 us -> 0 us
  other arithmetic: 66.9 us -> 11.7 us
  between operations: 15.8 us -> 1.41 us
    reduce_scatter x21 -> x0, waiting for transfers between devices: 656 us -> none  [the longest x14 328 us: cp_sum(): lax.psum_scatter(part, 'cp', scatter_dimension=0, tiled=True).astype(BF16)]
    pallas_call x4 -> x8, Pallas kernels: 43.6 us -> 483 us  [the longest x2 171 us: attn_bwd(): pl.pallas_call(functools.partial(attn_bwd_kernel, layer, seq, last), out_...]
    all_gather x13 -> x0, waiting for transfers between devices: 223 us -> none  [the longest x7 149 us: gather_rows(): return lax.all_gather(own, 'tp', axis=0, tiled=True)]
    dot_general x33 -> x0, matrix products: 115 us -> none  [dot(): return lax.dot_general(a, b, dims, preferred_element_type=F32)]
    all_gather x9 -> x0, blocking collectives: 109 us -> none  [the longest x8 81.3 us: cp_sum(): return lax.all_gather(own, 'cp', axis=0, tiled=True)]
    psum x2 -> x0, blocking collectives: 38.4 us -> none  [the longest x1 32 us: local_program(): d_gains = lax.psum(jnp.stack(stacked[:2]), ('tp', 'cp'))]
    convert_element_type x18 -> x0, other arithmetic: 30.5 us -> none  [the longest x14 19.8 us: cp_sum(): lax.psum_scatter(part, 'cp', scatter_dimension=0, tiled=True).astype(BF16)]
    all_to_all x1 -> x0, blocking collectives: 29 us -> none  [to_batch(): lax.all_to_all(arr, 'cp', split_axis=0, concat_axis=1, tiled=True)]
  transfers between devices with their start and end apart: 36 -> 0, of which waited for: 31 -> 0; matrix products, arithmetic and copies ran while one was open for 8% -> 0% of each run, Pallas kernels for 1% -> 0%
where the time goes in v3:
time: 526 us; the launch traced here: 517 us
  Pallas kernels  483 us (92%)
  local copies, waits for them, and re-layouts  20.9 us (4%)
  other arithmetic  11.7 us (2%)
    pallas_call x2, Pallas kernels, attn_bwd(): pl.pallas_call(functools.partial(attn_bwd_kernel, layer, seq, last), out_...  171 us
    pallas_call x2, Pallas kernels, mlp_bwd(): pl.pallas_call(functools.partial(mlp_bwd_kernel, layer), out_shape=out_sh...  150 us
    pallas_call x2, Pallas kernels, attn_layer(): pl.pallas_call(functools.partial(attn_kernel, layer, seq, d_y is not None...  74.1 us
    pallas_call x1, Pallas kernels, mlp_fwd(): pl.pallas_call(functools.partial(mlp_fwd_kernel, layer), out_shape=jax.Sh...  56.1 us
    pallas_call x1, Pallas kernels, exchange(): pl.pallas_call(exchange_kernel, out_shape=[jax.ShapeDtypeStruct((2, 4, bl...  31.2 us
    unnamed x79, local copies, waits for them, and re-layouts  18.9 us

profile of v3, /device:TPU:0, one launch (start us, length us, event | category | flops | bytes accessed | tf_op | source)
XLA Modules:
  0.0 516.7 jit_solution(10223188808867617120)
XLA Ops:
  0.7 0.8 select_reduce_fusion.1.refs_5_.refs_12_
  1.6 1.6 copy-done
  3.2 1.2 copy-done.1
  4.4 0.7 copy-done.3
  5.1 31.2 %exchange.1 = (bf16[2,4,128,1024]{3,2,1,0:T(8,128)(2,1)S(1)}, s32[4,2,128]{2,1,0:T(2,128)S(1)}, bf16[2,4,256,1024]{3,2,1,0:T(8,128)(2,1)S(1)}) custom-call(bf16[4,2,128,1024]{3,2,1,0:T(8,128)(2,1)S(1)} %bitcast.34, s32[4,2,128]{2,1,0:T(2,128)S(1)} %bitcast.35, bf16[2,256,1024]{2,1,0:T(8,128)(2,1)S(1)} %copy-done.1), custom_call_target="tpu_custom_call" | custom-call | tf_op jit(solution)/shard_map/exchange/pallas_call | solution.py:189
  36.3 2.0 copy-done.4
  38.4 1.3 copy-done.5
  39.7 40.0 %attn_fwd_0.1 = (bf16[2,2,2,128,1024]{4,3,2,1,0:T(8,128)(2,1)}, bf16[2,512,256]{2,1,0:T(8,128)(2,1)S(1)}, bf16[2,512,256]{2,1,0:T(8,128)(2,1)S(1)}, bf16[2,512,2...) custom-call(bf16[2,512,1024]{2,1,0:T(8,128)(2,1)} %bitcast.36, ...), custom_call_target="tpu_custom_call" | custom-call | flops 4294967296 | bytes 16777216 | tf_op jit(solution)/shard_map/attn_fwd_0/pallas_call | solution.py:303
  79.7 0.8 copy-done.16
  80.5 0.8 copy-done.17
  81.3 0.8 copy-done.18
  82.1 1.8 copy-done.15
  83.9 56.1 %mlp_fwd_0.1 = bf16[2,2,2,128,1024]{4,3,2,1,0:T(8,128)(2,1)S(1)} custom-call(bf16[2,2,2,128,1024]{4,3,2,1,0:T(8,128)(2,1)S(1)} %copy-done.15, f32[2,1024]{1,0:T(2,128)S(1)} %copy-done.9, bf16[2,704,1024]{2,1,0:T(8,128)(2,1)} %bitcast.59, bf16[2,704,1024]{2,1,0:T(8,128)(2,1)} %bitcast.62, bf16[2,704,1024]{2,1,0:T(8,128)(2,1)} %wo_all.5), custom_call_target="tpu_custom_call" | custom-call | flops 5368709120 | bytes 16777216 | tf_op jit(solution)/shard_map/mlp_fwd_0/pallas_call | solution.py:364
  140.0 1.3 copy-done.12
  141.3 34.1 %attn_fwd_1.1 = (bf16[2,2,2,128,1024]{4,3,2,1,0:T(8,128)(2,1)}, bf16[2,512,256]{2,1,0:T(8,128)(2,1)S(1)}, bf16[2,512,256]{2,1,0:T(8,128)(2,1)S(1)}, bf16[2,512,2...) custom-call(bf16[2,512,1024]{2,1,0:T(8,128)(2,1)} %bitcast.38, f32[2,1024]{1,0:T(2,128)S(1)} %copy-done.10, ...), custom_call_target="tpu_custom_call" | custom-call | flops 4294967296 | bytes 16777216 | tf_op jit(solution)/shard_map/attn_fwd_1/pallas_call | solution.py:303
  175.4 0.8 copy-done.14
  176.2 0.8 copy-done.19
  177.0 0.8 copy-done.20
  177.8 0.8 copy-done.21
  178.6 73.9 %mlp_bwd_1.1 = (bf16[2,2,2,128,1024]{4,3,2,1,0:T(8,128)(2,1)}, f32[1,1024]{1,0:T(1,128)}, f32[4,176,1024]{2,1,0:T(8,128)}, bf16[4,176,1024]{2,1,0:T(8,128)(2,1)}, bf16[4,176,1024]{2,1,0:T(8,128)(2,1)}) custom-call(bf16[2,2,2,128,1024]{4,3,2,1,0:T(8,128)(2,1)} %get-tuple-element.54.x1_ref, bf16[2,2,2,128,1024]{4,3,2,1,0:T(8,128)(2,1)} %bitcast.68, ...), custom_call_target="tpu_custom_call" | custom-call | flops 12884901888 | bytes 33554432 | tf_op jit(solution)/shard_map/mlp_bwd_1/pallas_call | solution.py:446
  252.4 77.2 %attn_bwd_1.1 = (bf16[2,1,2,2,128,1024]{5,4,3,2,1,0:T(8,128)(2,1)}, f32[1,1024]{1,0:T(1,128)}, f32[4,1024]{1,0:T(4,128)}, bf16[4,176,1024]{2,1,0:T(8,128)(2,1)},...) custom-call(bf16[2,512,1024]{2,1,0:T(8,128)(2,1)} %bitcast.39, ...), custom_call_target="tpu_custom_call" | custom-call | flops 8589934592 | bytes 33554432 | tf_op jit(solution)/shard_map/attn_bwd_1/pallas_call | solution.py:641
  329.7 76.0 %mlp_bwd_0.1 = (bf16[2,2,2,128,1024]{4,3,2,1,0:T(8,128)(2,1)}, f32[1,1024]{1,0:T(1,128)}, f32[4,176,1024]{2,1,0:T(8,128)}, bf16[4,176,1024]{2,1,0:T(8,128)(2,1)}, bf16[4,176,1024]{2,1,0:T(8,128)(2,1)}) custom-call(bf16[2,2,2,128,1024]{4,3,2,1,0:T(8,128)(2,1)} %get-tuple-element.53.x1_ref, bf16[2,2,2,128,1024]{4,3,2,1,0:T(8,128)(2,1)} %bitcast.67, ...), custom_call_target="tpu_custom_call" | custom-call | flops 12884901888 | bytes 33554432 | tf_op jit(solution)/shard_map/mlp_bwd_0/pallas_call | solution.py:446
  405.8 1.9 concatenate.3.refs_14_
  407.7 94.2 %attn_bwd_0.1 = (bf16[4,2,2,2,32,1024]{5,4,3,2,1,0:T(8,128)(2,1)}, f32[16,1024]{1,0:T(8,128)}, bf16[4,176,1024]{2,1,0:T(8,128)(2,1)}, bf16[4,64,1024]{2,1,0:T(8,...) custom-call(bf16[2,512,1024]{2,1,0:T(8,128)(2,1)} %bitcast.37, ...), custom_call_target="tpu_custom_call" | custom-call | flops 8589934592 | bytes 33554432 | tf_op jit(solution)/shard_map/attn_bwd_0/pallas_call | solution.py:641
  502.0 2.8 pad_maximum_fusion.1
  504.8 0.7 select_reduce_fusion
  506.2 1.1 pad_maximum_fusion.3
  507.2 1.1 pad_maximum_fusion.4
  508.5 1.8 pad_maximum_fusion
  510.3 1.0 copy-done.25
  512.2 2.8 maximum_bitcast_fusion
  514.9 1.3 copy.25
  (71 shorter events, 1.9 us)
Async XLA Ops:
  0.6 39.0 %copy-start.10 = (f32[2,1024]{1,0:T(2,128)S(1)}, f32[2,1024]{1,0:T(2,128)}, u32[]{:S(2)}) copy-start(f32[2,1024]{1,0:T(2,128)} %refs_7_.3) | copy-start | bytes 24580
  1.6 1.6 copy-start
  3.2 1.2 copy-start.1
  5.1 136.2 %copy-start.2 = (f32[4,1024]{1,0:T(4,128)}, f32[4,1024]{1,0:T(4,128)S(1)}, u32[]{:S(2)}) copy-start(f32[4,1024]{1,0:T(4,128)S(1)} %select_reduce_fusion.1.refs_5_.refs_12_) | copy-start | bytes 49156
  5.1 34.6 %copy-start.6 = (bf16[2,1024,256]{2,1,0:T(8,128)(2,1)S(1)}, bf16[2,1024,256]{2,1,0:T(8,128)(2,1)}, u32[]{:S(2)}) copy-start(bf16[2,1024,256]{2,1,0:T(8,128)(2,1)} %refs_8_.3) | copy-start | bytes 3145732
  5.1 34.6 %copy-start.7 = (bf16[2,1024,256]{2,1,0:T(8,128)(2,1)S(1)}, bf16[2,1024,256]{2,1,0:T(8,128)(2,1)}, u32[]{:S(2)}) copy-start(bf16[2,1024,256]{2,1,0:T(8,128)(2,1)} %refs_9_.3) | copy-start | bytes 3145732
  5.1 34.6 %copy-start.8 = (bf16[2,1024,256]{2,1,0:T(8,128)(2,1)S(1)}, bf16[2,1024,256]{2,1,0:T(8,128)(2,1)}, u32[]{:S(2)}) copy-start(bf16[2,1024,256]{2,1,0:T(8,128)(2,1)} %refs_10_.3) | copy-start | bytes 3145732
  36.3 2.1 copy-start.4
  38.4 1.3 copy-start.5
  39.7 101.6 %copy-start.11 = (s32[4,2,128]{2,1,0:T(2,128)}, s32[4,2,128]{2,1,0:T(2,128)S(1)}, u32[]{:S(2)}) copy-start(s32[4,2,128]{2,1,0:T(2,128)S(1)} %get-tuple-element.51.refs_6_.refs_13_) | copy-start | bytes 12292
  39.7 42.4 %copy-start.9 = (f32[2,1024]{1,0:T(2,128)S(1)}, f32[2,1024]{1,0:T(2,128)}, u32[]{:S(2)}) copy-start(f32[2,1024]{1,0:T(2,128)} %g_ref.5) | copy-start | bytes 24580
  81.3 0.8 copy-start.18
  82.1 57.8 %copy-start.13 = (bf16[2,2,256,256]{3,2,1,0:T(8,128)(2,1)}, bf16[2,2,256,256]{3,2,1,0:T(8,128)(2,1)S(1)}, u32[]{:S(2)}) copy-start(bf16[2,2,256,256]{3,2,1,0:T(8,128)(2,1)S(1)} %get-tuple-element.68) | copy-start | bytes 1572868
  82.1 1.8 copy-start.15
  139.9 1.3 copy-start.12
  329.6 76.1 %copy-start.35 = (f32[4,1024]{1,0:T(4,128)S(1)}, f32[4,1024]{1,0:T(4,128)}, u32[]{:S(2)}) copy-start(f32[4,1024]{1,0:T(4,128)} %get-tuple-element.72) | copy-start | bytes 49156
  329.7 76.1 %copy-start.37 = (f32[1,1024]{1,0:T(1,128)S(1)}, f32[1,1024]{1,0:T(1,128)}, u32[]{:S(2)}) copy-start(f32[1,1024]{1,0:T(1,128)} %get-tuple-element.70) | copy-start | bytes 12292
  329.7 76.1 %copy-start.38 = (f32[1,1024]{1,0:T(1,128)S(1)}, f32[1,1024]{1,0:T(1,128)}, u32[]{:S(2)}) copy-start(f32[1,1024]{1,0:T(1,128)} %get-tuple-element.69) | copy-start | bytes 12292
  407.7 94.2 %copy-start.33 = (bf16[4,256,256]{2,1,0:T(8,128)(2,1)S(1)}, bf16[4,256,256]{2,1,0:T(8,128)(2,1)}, u32[]{:S(2)}) copy-start(bf16[4,256,256]{2,1,0:T(8,128)(2,1)} %get-tuple-element.76) | copy-start | bytes 1572868
  407.7 94.2 %copy-start.34 = (bf16[4,256,256]{2,1,0:T(8,128)(2,1)S(1)}, bf16[4,256,256]{2,1,0:T(8,128)(2,1)}, u32[]{:S(2)}) copy-start(bf16[4,256,256]{2,1,0:T(8,128)(2,1)} %get-tuple-element.78) | copy-start | bytes 1572868
  501.9 2.8 copy-start.36
  502.0 4.2 copy-start.30
  502.0 4.2 copy-start.32
  504.8 2.5 copy-start.29
  504.8 2.5 copy-start.31
  506.1 2.1 copy-start.24
  506.1 2.3 copy-start.27
  508.5 1.8 copy-start.23
  508.5 2.8 copy-start.25
  508.5 3.3 copy-start.26
  508.5 3.7 copy-start.28
  512.2 2.8 copy-start.22
  (7 other events, 5.4 us)

commit v4 on v3

--- a/solution.py
+++ b/solution.py
@@ -208,25 +208,12 @@
     return e, jnp.sum(e, axis=-1, keepdims=True)
 
 
-def attn_kernel(layer, seq, with_dy, *refs):
-    refs = list(refs)
-    x_ref, g_ref, wq_all, wk_all, wv_all, t_ref, mask_ref, wf_all = [refs.pop(0) for _ in range(8)]
-    if with_dy:
-        dy_ref = refs.pop(0)
-    x1_ref, q_ref, k_ref, v_ref, o_ref = [refs.pop(0) for _ in range(5)]
-    if with_dy:
-        dyo_ref = refs.pop(0)
-    wq_ref, wk_ref, wv_ref, wf_ref, wsem, bias_ref, of_ref, send, recv, osend, orecv = [refs.pop(0) for _ in range(11)]
+def attn_kernel(layer, seq, x_ref, g_ref, wq_all, wk_all, wv_all, t_ref, mask_ref, wf_all, x1_ref, q_out, k_out, v_out, o_out,
+                wq_ref, wk_ref, wv_ref, wf_ref, wsem, q_ref, k_ref, v_ref, o_ref, ssem, bias_ref, of_ref, send, recv, osend, orecv):
     loads = load_layer(layer, [wq_all, wk_all, wv_all, wf_all], [wq_ref, wk_ref, wv_ref, wf_ref], wsem)
     tp, cp, z, y, x, core, ids = place()
     heads = t_ref.shape[0]
-    meet(ids, ['z', 'y', 'zy'] + (['x', 'core', 'xc'] if with_dy else []))
-    dys = []
-    if with_dy:
-        for i, name in enumerate(['x', 'core', 'xc']):
-            dys.append(remote(dy_ref.at[ids[name]['cp']], dyo_ref.at[:, cp], osend.at[3 + i], orecv.at[3 + i], ids[name]))
-        for b in range(2):
-            dyo_ref[b, cp] = dy_ref[cp, b]
+    meet(ids, ['z', 'y', 'zy'])
     out = []
     for copy in loads[:3]:
         copy.wait()
@@ -253,6 +240,10 @@
         else:
             out.append(remote(o_ref.at[b, 1 - y], of_ref.at[tp], osend.at[2], orecv.at[2], ids['y']))
     of_ref[tp] = o_ref[z, y]
+    saves = [pltpu.make_async_copy(src, dst, ssem.at[i]) for i, (src, dst) in
+             enumerate([(q_ref, q_out), (k_ref, k_out), (v_ref, v_out), (o_ref, o_out)])]
+    for copy in saves:
+        copy.start()
     loads[3].wait()
     for copy in out:
         copy.wait_recv()
@@ -269,7 +260,7 @@
         s.close()
     for copy in out:
         copy.wait_send()
-    for copy in dys:
+    for copy in saves:
         copy.wait()
 
 
@@ -288,26 +279,22 @@
     return [pl.BlockSpec(memory_space=pl.ANY)] * n
 
 
-def attn_layer(layer, collective_id, x, gains, w_q, w_k, w_v, table, mask, w_full, d_y=None):
+def attn_layer(layer, collective_id, x, gains, w_q, w_k, w_v, table, mask, w_full):
     seq = 512
     width, cols = w_q.shape[1], w_q.shape[2]
-    operands = [x.reshape(2, seq, width), gains, w_q, w_k, w_v, table, mask, w_full]
-    in_specs = vmem_specs(2) + any_specs(3) + vmem_specs(2) + any_specs(1)
-    head_shape = jax.ShapeDtypeStruct((2, seq, cols), BF16)
-    out_shape = [jax.ShapeDtypeStruct((2, 2, 2, 128, width), BF16)] + [head_shape] * 3 + [jax.ShapeDtypeStruct((2, 2, seq // 2, cols), BF16)]
-    if d_y is not None:
-        operands.append(d_y.reshape(4, 2, 128, width))
-        in_specs += vmem_specs(1)
-        out_shape.append(jax.ShapeDtypeStruct((2, 4, 128, width), BF16))
+    head_shape = (2, seq, cols)
+    o_shape = (2, 2, seq // 2, cols)
+    out_shape = [jax.ShapeDtypeStruct((2, 2, 2, 128, width), BF16)] + [jax.ShapeDtypeStruct(h, BF16) for h in [head_shape] * 3 + [o_shape]]
     dma = pltpu.SemaphoreType.DMA
     return pl.pallas_call(
-        functools.partial(attn_kernel, layer, seq, d_y is not None),
-        out_shape=out_shape, in_specs=in_specs, out_specs=vmem_specs(len(out_shape)),
-        scratch_shapes=layer_scratch(w_q, w_k, w_v, w_full) + [pltpu.VMEM((table.shape[0], seq, seq), F32), pltpu.VMEM((4, 256, cols), BF16), dma((2, 6)), dma((2, 6)), dma((6,)), dma((6,))],
-        compiler_params=pltpu.CompilerParams(collective_id=collective_id, has_side_effects=True, vmem_limit_bytes=48 << 20),
+        functools.partial(attn_kernel, layer, seq),
+        out_shape=out_shape, in_specs=vmem_specs(2) + any_specs(3) + vmem_specs(2) + any_specs(1), out_specs=vmem_specs(1) + any_specs(4),
+        scratch_shapes=layer_scratch(w_q, w_k, w_v, w_full) + [pltpu.VMEM(head_shape, BF16)] * 3 + [pltpu.VMEM(o_shape, BF16), dma((4,))]
+        + [pltpu.VMEM((table.shape[0], seq, seq), F32), pltpu.VMEM((4, 256, cols), BF16), dma((2, 6)), dma((2, 6)), dma((3,)), dma((3,))],
+        compiler_params=pltpu.CompilerParams(collective_id=collective_id, has_side_effects=True, vmem_limit_bytes=40 << 20),
         cost_estimate=pl.CostEstimate(flops=4 << 30, bytes_accessed=16 << 20, transcendentals=0),
         name=f"attn_fwd_{layer}",
-    )(*operands)
+    )(x.reshape(2, seq, width), gains, w_q, w_k, w_v, table, mask, w_full)
 
 
 def gelu_parts(g):
@@ -322,10 +309,15 @@
     return [(1 - z, 1 - y), (1 - z, y), (z, 1 - y), (z, y)]
 
 
-def mlp_fwd_kernel(layer, x1_ref, g_ref, wg_all, wl_all, wo_all, out_ref, wg_ref, wl_ref, wo_ref, wsem, part, near, far, send, recv):
+def mlp_fwd_kernel(layer, x1_ref, dy_ref, g_ref, wg_all, wl_all, wo_all, out_ref, dyo_ref, wg_ref, wl_ref, wo_ref, wsem,
+                   part, near, far, send, recv, dsend, drecv, own_sem):
     loads = load_layer(layer, [wg_all, wl_all, wo_all], [wg_ref, wl_ref, wo_ref], wsem)
     tp, cp, z, y, x, core, ids = place()
-    meet(ids, ['z', 'y'])
+    meet(ids, ['z', 'y', 'x', 'core', 'xc'])
+    moves = [remote(dy_ref.at[ids[name]['cp']], dyo_ref.at[:, cp], dsend.at[i], drecv.at[i], ids[name])
+             for i, name in enumerate(['x', 'xc', 'core'])]
+    own = pltpu.make_async_copy(dy_ref.at[cp], dyo_ref.at[:, cp], own_sem)
+    own.start()
     for copy in loads:
         copy.wait()
     zy, yz = streams = colours(part, near, far, lambda q, c: out_ref.at[q[0], q[1], c], send, recv, ids, z, y)
@@ -353,34 +345,50 @@
         s.gather()
     for s in streams:
         s.close()
+    for copy in moves + [own]:
+        copy.wait()
 
 
 def sum_scratch(width, blocks=()):
     return [pltpu.VMEM((2, 2, 2) + blocks, F32), pltpu.VMEM((2, 2) + blocks, F32), pltpu.VMEM((2,) + blocks, F32)]
 
 
-def mlp_fwd(layer, collective_id, x1, gains, wg_t, wl_t, w_out):
+def mlp_fwd(layer, collective_id, x1, d_y, gains, wg_t, wl_t, w_out):
     dma = pltpu.SemaphoreType.DMA
+    width = x1.shape[-1]
     return pl.pallas_call(
         functools.partial(mlp_fwd_kernel, layer),
-        out_shape=jax.ShapeDtypeStruct(x1.shape, BF16),
-        in_specs=vmem_specs(2) + any_specs(3), out_specs=pl.BlockSpec(memory_space=pltpu.VMEM),
-        scratch_shapes=layer_scratch(wg_t, wl_t, w_out) + sum_scratch(0, x1.shape[3:]) + [dma((2, 6)), dma((2, 6))],
-        compiler_params=pltpu.CompilerParams(collective_id=collective_id, has_side_effects=True, vmem_limit_bytes=48 << 20),
+        out_shape=[jax.ShapeDtypeStruct(x1.shape, BF16), jax.ShapeDtypeStruct((2, 4, 128, width), BF16)],
+        in_specs=vmem_specs(3) + any_specs(3), out_specs=vmem_specs(1) + any_specs(1),
+        scratch_shapes=layer_scratch(wg_t, wl_t, w_out) + sum_scratch(0, x1.shape[3:]) + [dma((2, 6)), dma((2, 6)), dma((3,)), dma((3,)), dma],
+        compiler_params=pltpu.CompilerParams(collective_id=collective_id, has_side_effects=True, vmem_limit_bytes=40 << 20),
         cost_estimate=pl.CostEstimate(flops=5 << 30, bytes_accessed=16 << 20, transcendentals=0),
         name=f"mlp_fwd_{layer}",
-    )(x1, gains, wg_t, wl_t, w_out)
-
-
-def mlp_bwd_kernel(layer, x1_ref, dy_ref, g_ref, wg_all, wl_all, wo_all, dm_ref, dg_ref, lin_part, gout_ref, ggate_ref,
-                   wg_ref, wl_ref, wo_ref, wsem, part, near, far, h2_ref, gated_ref, dgate_ref, dlin_ref, p0, n0, f0, p1, n1, f1, send, recv):
+    )(x1, d_y.reshape(4, 2, 128, width), gains, wg_t, wl_t, w_out)
+
+
+def mlp_bwd_kernel(layer, n_carry, *refs):
+    refs = list(refs)
+    x1_ref, dy_ref, g_ref, wg_all, wl_all, wo_all = [refs.pop(0) for _ in range(6)]
+    carried = [refs.pop(0) for _ in range(n_carry)]
+    dm_ref, dg_ref, lin_out, gout_ref, ggate_ref = [refs.pop(0) for _ in range(5)]
+    carried_out = [refs.pop(0) for _ in range(n_carry)]
+    wg_ref, wl_ref, wo_ref, wsem, part, near, far, h2_ref, gated_ref, dgate_ref, dlin_ref = [refs.pop(0) for _ in range(11)]
+    lin_part, lin_sem, p0, n0, f0, p1, n1, f1 = [refs.pop(0) for _ in range(8)]
+    carry_scratch = [[refs.pop(0) for _ in range(2)] for _ in range(n_carry)]
+    send, recv = refs
     loads = load_layer(layer, [wg_all, wl_all, wo_all], [wg_ref, wl_ref, wo_ref], wsem)
     tp, cp, z, y, x, core, ids = place()
     meet(ids, ['z', 'y', 'x', 'core'])
     zy, yz = streams = colours(part, near, far, lambda q, c: dm_ref.at[q[0], q[1], c], send, recv, ids, z, y)
     g_out = grad_stream(p0, n0, f0, gout_ref, send.at[2], recv.at[2], ids, x, core)
     g_gate = grad_stream(p1, n1, f1, ggate_ref, send.at[3], recv.at[3], ids, x, core)
+    g_carry = [grad_stream(p, s[0], s[1], out, send.at[4 + i], recv.at[4 + i], ids, x, core)
+               for i, (p, s, out) in enumerate(zip(carried, carry_scratch, carried_out))]
     gain = g_ref[layer:layer + 1, :]
+    for g in g_carry:
+        g.send_away(0)
+        g.send_away(1)
     for copy in loads:
         copy.wait()
 
@@ -402,6 +410,8 @@
     compute(quarters[0])
     zy.send_away(0)
     yz.send_away(0)
+    for g in g_carry:
+        g.forward()
     compute(quarters[1])
     zy.send_away(1)
     compute(quarters[2])
@@ -410,14 +420,19 @@
     grad_into(p0, gated_ref[...], dy_ref[...].reshape(h2_ref.shape))
     g_out.send_away(0)
     g_out.send_away(1)
-    for s in streams:
-        s.forward()
     grad_into(p1, dgate_ref[...], h2_ref)
+    g_out.forward()
     g_gate.send_away(0)
     g_gate.send_away(1)
-    g_out.forward()
+    for s in streams:
+        s.forward()
+    g_gate.forward()
     grad_into(lin_part, dlin_ref[...], h2_ref)
-    g_gate.forward()
+    save = pltpu.make_async_copy(lin_part, lin_out, lin_sem)
+    save.start()
+    for g in g_carry:
+        g.finish()
+    g_out.finish()
     d_gain = 0.0
     for c, s in enumerate(streams):
         d_x, dg = norm_back(s.total(), x1_ref[z, y, c], gain)
@@ -425,34 +440,43 @@
         s.publish()
         d_gain = d_gain + jnp.sum(dg, axis=0, keepdims=True)
     dg_ref[...] = d_gain
-    g_out.finish()
+    for g in g_carry:
+        g.gather()
+    g_gate.finish()
     for s in streams:
         s.gather()
     g_out.gather()
-    g_gate.finish()
     g_gate.gather()
-    for s in streams + [g_out, g_gate]:
+    for s in g_carry + streams + [g_out, g_gate]:
         s.close()
-
-
-def mlp_bwd(layer, collective_id, x1, dy, gains, wg_t, wl_t, w_out):
+    save.wait()
+
+
+def grad_scratch_of(block):
+    return [pltpu.VMEM((4,) + block, F32), pltpu.VMEM((2,) + block, F32), pltpu.VMEM(block, F32)]
+
+
+def mlp_bwd(layer, collective_id, x1, dy, gains, wg_t, wl_t, w_out, carried=()):
     dma = pltpu.SemaphoreType.DMA
     ff, width = wg_t.shape[1:]
     block = (ff // 4, width)
     rows = 1024
-    grad_scratch = [pltpu.VMEM((4,) + block, F32), pltpu.VMEM((2,) + block, F32), pltpu.VMEM(block, F32)]
     out_shape = [jax.ShapeDtypeStruct(x1.shape, BF16), jax.ShapeDtypeStruct((1, width), F32), jax.ShapeDtypeStruct((4,) + block, F32)]
-    out_shape += [jax.ShapeDtypeStruct((4,) + block, BF16)] * 2
+    out_shape += [jax.ShapeDtypeStruct((4,) + block, BF16)] * 2 + [jax.ShapeDtypeStruct(c.shape, BF16) for c in carried]
+    scratch = layer_scratch(wg_t, wl_t, w_out) + sum_scratch(0, x1.shape[3:]) + [pltpu.VMEM((rows, width), BF16)] + [pltpu.VMEM((rows, ff), BF16)] * 3
+    scratch += [pltpu.VMEM((4,) + block, F32), dma] + grad_scratch_of(block) * 2
+    for c in carried:
+        scratch += grad_scratch_of(c.shape[1:])[1:]
+    n = 4 + len(carried)
     return pl.pallas_call(
-        functools.partial(mlp_bwd_kernel, layer),
+        functools.partial(mlp_bwd_kernel, layer, len(carried)),
         out_shape=out_shape,
-        in_specs=vmem_specs(3) + any_specs(3), out_specs=vmem_specs(5),
-        scratch_shapes=layer_scratch(wg_t, wl_t, w_out) + sum_scratch(0, x1.shape[3:]) + [pltpu.VMEM((rows, width), BF16)] + [pltpu.VMEM((rows, ff), BF16)] * 3
-        + grad_scratch * 2 + [dma((4, 6)), dma((4, 6))],
-        compiler_params=pltpu.CompilerParams(collective_id=collective_id, has_side_effects=True, vmem_limit_bytes=60 << 20),
+        in_specs=vmem_specs(3) + any_specs(3) + vmem_specs(len(carried)), out_specs=vmem_specs(2) + any_specs(1) + vmem_specs(2 + len(carried)),
+        scratch_shapes=scratch + [dma((n, 6)), dma((n, 6))],
+        compiler_params=pltpu.CompilerParams(collective_id=collective_id, has_side_effects=True, vmem_limit_bytes=58 << 20),
         cost_estimate=pl.CostEstimate(flops=12 << 30, bytes_accessed=32 << 20, transcendentals=0),
         name=f"mlp_bwd_{layer}",
-    )(x1, dy, gains, wg_t, wl_t, w_out)
+    )(x1, dy, gains, wg_t, wl_t, w_out, *carried)
 
 
 def attn_bwd_kernel(layer, seq, last, *refs):
@@ -464,14 +488,15 @@
     if last:
         small_out = refs.pop(0)
     else:
-        dg_ref, dt_ref = refs.pop(0), refs.pop(0)
-    grad_out = [refs.pop(0) for _ in range(5)]
+        dg_ref, dt_ref, q_part, k_part = [refs.pop(0) for _ in range(4)]
+    n_grads = 4 if last else 2
+    grad_out = [refs.pop(0) for _ in range(1 + n_grads)]
     wq_ref, wk_ref, wv_ref, wo_ref, wsem = [refs.pop(0) for _ in range(5)]
     loads = load_layer(layer, [wq_all, wk_all, wv_all, wo_all], [wq_ref, wk_ref, wv_ref, wo_ref], wsem)
     part, near, far = [refs.pop(0) for _ in range(3)]
     bias_ref, acc_ref, do_ref, dq_ref, dk_ref, dv_ref, h_ref = [refs.pop(0) for _ in range(7)]
     lin_near, lin_far = refs.pop(0), refs.pop(0)
-    grad_scratch = [[refs.pop(0) for _ in range(3)] for _ in range(4)]
+    grad_scratch = [[refs.pop(0) for _ in range(3)] for _ in range(n_grads)]
     send, recv = refs.pop(0), refs.pop(0)
     if last:
         own_ref, acc_small, got_small, csend, crecv = [refs.pop(0) for _ in range(5)]
@@ -487,7 +512,7 @@
             return dx_ref.at[q[0], :, q[1], c]
     zy, yz = streams = colours(part, near, far, region, send, recv, ids, z, y)
     g_lin = grad_stream(lin_part, lin_near, lin_far, grad_out[0], send.at[2], recv.at[2], ids, x, core)
-    g_o, g_q, g_k, g_v = [grad_stream(s[0], s[1], s[2], out, send.at[3 + i], recv.at[3 + i], ids, x, core)
+    g_o, *g_qkv = [grad_stream(s[0], s[1], s[2], out, send.at[3 + i], recv.at[3 + i], ids, x, core)
                           for i, (s, out) in enumerate(zip(grad_scratch, grad_out[1:]))]
     gain = g_ref[layer:layer + 1, :]
     g_lin.send_away(0)
@@ -553,16 +578,19 @@
     yz.send_away(1)
     g_o.forward()
     compute(quarters[3])
-    for s in streams:
-        s.forward()
-    for g, scratch, d_ref in zip([g_q, g_k, g_v], grad_scratch[1:], [dq_ref, dk_ref, dv_ref]):
+    for g, scratch, d_ref in zip(g_qkv, grad_scratch[1:], [dv_ref, dk_ref, dq_ref]):
         grad_into(scratch[0], h_ref[...], d_ref[...].reshape(2 * seq, -1))
         g.send_away(0)
         g.send_away(1)
+    for s in streams:
+        s.forward()
+    for g in g_qkv:
+        g.forward()
+    if not last:
+        for p, d_ref in zip([q_part, k_part], [dq_ref, dk_ref]):
+            grad_into(p, h_ref[...], d_ref[...].reshape(2 * seq, -1))
     g_lin.finish()
     g_o.finish()
-    for g in [g_q, g_k, g_v]:
-        g.forward()
 
     d_gain = 0.0
     moves = []
@@ -581,6 +609,8 @@
         else:
             dx_ref[z, :, y, c] = d_x
             s.publish()
+    for g in g_qkv:
+        g.finish()
     if last:
         acc_small[0, 0:4, :] = jnp.concatenate([small_ref[0:3, :], d_gain], axis=0)
         acc_small[0, 4:8, :] = jnp.zeros((4, d_gain.shape[1]), F32)
@@ -605,11 +635,9 @@
         s.gather()
     g_lin.gather()
     g_o.gather()
-    for g in [g_q, g_k, g_v]:
-        g.finish()
-    for g in [g_q, g_k, g_v]:
+    for g in g_qkv:
         g.gather()
-    for s in streams + [g_lin, g_o, g_q, g_k, g_v]:
+    for s in streams + [g_lin, g_o] + g_qkv:
         s.close()
 
 
@@ -627,14 +655,15 @@
         out_shape = [jax.ShapeDtypeStruct((4, 2, 2, 2, 32, width), BF16), jax.ShapeDtypeStruct((16, width), F32)]
     else:
         out_shape = [jax.ShapeDtypeStruct((2, 1, 2, 2, 128, width), BF16), jax.ShapeDtypeStruct((1, width), F32), jax.ShapeDtypeStruct(table.shape, F32)]
-    shapes = [(cols // 4, width)] + [(width // 4, cols)] * 3
+        out_shape += [jax.ShapeDtypeStruct((4, width // 4, cols), F32)] * 2
+    shapes = [(cols // 4, width)] + [(width // 4, cols)] * (3 if last else 1)
     lin_block = lin_part.shape[1:]
     out_shape += [jax.ShapeDtypeStruct((4,) + s, BF16) for s in [lin_block] + shapes]
     scratch = layer_scratch(w_q, w_k, w_v, w_o) + sum_scratch(0, blocks) + [pltpu.VMEM((table.shape[0], seq, seq), F32)] * 2 + [pltpu.VMEM((seq, cols), BF16)]
     scratch += [pltpu.VMEM((2, seq, cols), BF16)] * 3 + [pltpu.VMEM((2 * seq, width), BF16)]
     scratch += [pltpu.VMEM((2,) + lin_block, F32), pltpu.VMEM(lin_block, F32)]
     for s in shapes:
-        scratch += [pltpu.VMEM((4,) + s, F32), pltpu.VMEM((2,) + s, F32), pltpu.VMEM(s, F32)]
+        scratch += grad_scratch_of(s)
     scratch += [dma((7, 6)), dma((7, 6))]
     if last:
         scratch += [pltpu.VMEM((2, 4, 32, width), BF16), pltpu.VMEM((5, 16, width), F32), pltpu.VMEM((4, 16, width), F32), dma((3, 4)), dma((3, 4))]
@@ -666,15 +695,15 @@
         wg_t, wl_t = jnp.swapaxes(w_gate, 1, 2), jnp.swapaxes(w_lin, 1, 2)
         x0, mask, w_full = exchange(x_in, key_mask, w_o)
 
-        a0, q0, k0, v0, o0, dy = attn_layer(0, 1, x0, g_attn, w_q, w_k, w_v, table, mask, w_full, d_y)
-        x1 = mlp_fwd(0, 2, a0, g_mlp, wg_t, wl_t, w_out)
+        a0, q0, k0, v0, o0 = attn_layer(0, 1, x0, g_attn, w_q, w_k, w_v, table, mask, w_full)
+        x1, dy = mlp_fwd(0, 2, a0, d_y, g_mlp, wg_t, wl_t, w_out)
         a1, q1, k1, v1, o1 = attn_layer(1, 3, x1, g_attn, w_q, w_k, w_v, table, mask, w_full)
 
         dm, dgm1, lin, out1, gate1 = mlp_bwd(1, 4, a1, dy.reshape(quarters), g_mlp, wg_t, wl_t, w_out)
-        dx, dga1, dt1, lin1, wo1, wq1, wk1, wv1 = attn_bwd(1, 5, x1, dm, lin, q1, k1, v1, o1, g_attn, w_q, w_k, w_v, w_o, table, mask)
-        dm, dgm0, lin, out0, gate0 = mlp_bwd(0, 6, a0, dx.reshape(quarters), g_mlp, wg_t, wl_t, w_out)
+        dx, dga1, dt1, q_part, k_part, lin1, wo1, wv1 = attn_bwd(1, 5, x1, dm, lin, q1, k1, v1, o1, g_attn, w_q, w_k, w_v, w_o, table, mask)
+        dm, dgm0, lin, out0, gate0, wq1, wk1 = mlp_bwd(0, 6, a0, dx.reshape(quarters), g_mlp, wg_t, wl_t, w_out, (q_part, k_part))
         small = jnp.concatenate([dga1, dgm1, dgm0, jnp.zeros((5, width), F32), dt1, jnp.zeros((4, width), F32)], axis=0)
-        d_x, small, lin0, wo0, wq0, wk0, wv0 = attn_bwd(0, 7, x0, dm, lin, q0, k0, v0, o0, g_attn, w_q, w_k, w_v, w_o, table, mask, small)
+        d_x, small, lin0, wo0, wv0, wk0, wq0 = attn_bwd(0, 7, x0, dm, lin, q0, k0, v0, o0, g_attn, w_q, w_k, w_v, w_o, table, mask, small)
 
         def both(first, second, like, swap=False):
             shape = (like.shape[2], like.shape[1]) if swap else like.shape[1:]

time: 526 us -> 517 us (0.983)
  Pallas kernels: 483 us -> 474 us
    pallas_call x2, Pallas kernels: 171 us -> 163 us  [attn_bwd(): pl.pallas_call(functools.partial(attn_bwd_kernel, layer, seq, last), out_...]
    unnamed x79 -> x89, local copies, waits for them, and re-layouts: 18.9 us -> 19.9 us
where the time goes in v4:
time: 517 us; the launch traced here: 510 us
  Pallas kernels  474 us (92%)
  local copies, waits for them, and re-layouts  21.2 us (4%)
  other arithmetic  12.8 us (2%)
    pallas_call x2, Pallas kernels, attn_bwd(): pl.pallas_call(functools.partial(attn_bwd_kernel, layer, seq, last), out_...  163 us
    pallas_call x2, Pallas kernels, mlp_bwd(): pl.pallas_call(functools.partial(mlp_bwd_kernel, layer, len(carried)), ou...  153 us
    pallas_call x2, Pallas kernels, attn_layer(): pl.pallas_call(functools.partial(attn_kernel, layer, seq), out_shape=out_...  69.4 us
    pallas_call x1, Pallas kernels, mlp_fwd(): pl.pallas_call(functools.partial(mlp_fwd_kernel, layer), out_shape=[jax.S...  57.8 us
    pallas_call x1, Pallas kernels, exchange(): pl.pallas_call(exchange_kernel, out_shape=[jax.ShapeDtypeStruct((2, 4, bl...  31.2 us
    unnamed x89, local copies, waits for them, and re-layouts  19.9 us

profile of v4, /device:TPU:0, one launch (start us, length us, event | category | flops | bytes accessed | tf_op | source)
XLA Modules:
  0.0 509.5 jit_solution(1671380502588794571)
XLA Ops:
  0.7 1.6 copy-done
  2.3 1.2 copy-done.1
  3.5 0.7 copy-done.3
  4.2 31.2 %exchange.1 = (bf16[2,4,128,1024]{3,2,1,0:T(8,128)(2,1)S(1)}, s32[4,2,128]{2,1,0:T(2,128)S(1)}, bf16[2,4,256,1024]{3,2,1,0:T(8,128)(2,1)S(1)}) custom-call(bf16[4,2,128,1024]{3,2,1,0:T(8,128)(2,1)S(1)} %bitcast.34, s32[4,2,128]{2,1,0:T(2,128)S(1)} %bitcast.35, bf16[2,256,1024]{2,1,0:T(8,128)(2,1)S(1)} %copy-done.1), custom_call_target="tpu_custom_call" | custom-call | tf_op jit(solution)/shard_map/exchange/pallas_call | solution.py:189
  35.7 35.8 %attn_fwd_0.1 = (bf16[2,2,2,128,1024]{4,3,2,1,0:T(8,128)(2,1)S(1)}, bf16[2,512,256]{2,1,0:T(8,128)(2,1)S(1)}, bf16[2,512,256]{2,1,0:T(8,128)(2,1)S(1)}, bf16[2,5...) custom-call(bf16[2,512,1024]{2,1,0:T(8,128)(2,1)S(1)} %bitcast.43, f32[2,1024]{1,0:T(2,128)S(1)} %copy-done.13, ...), custom_call_target="tpu_custom_call" | custom-call | flops 4294967296 | bytes 16777216 | tf_op jit(solution)/shard_map/attn_fwd_0/pallas_call | solution.py:289
  71.6 0.8 copy-done.21
  72.4 0.8 copy-done.22
  73.2 0.8 copy-done.23
  74.0 2.8 copy-done.5
  76.8 1.6 copy-done.6
  78.3 57.8 %mlp_fwd_0.1 = (bf16[2,2,2,128,1024]{4,3,2,1,0:T(8,128)(2,1)S(1)}, bf16[2,4,128,1024]{3,2,1,0:T(8,128)(2,1)S(1)}) custom-call(bf16[2,2,2,128,1024]{4,3,2,1,0:T(8,128)(2,1)S(1)} %get-tuple-element.56.x1_ref.refs_0_, bf16[4,2,128,1024]{3,2,1,0:T(8,128)(2,1)S(1)} %bitcast.42, f32[2,1024]{1,0:T(2,128)S(1)} %copy-done.12, bf16[2,704,1024]{2,1,0:T(8,128)(2,1)S(1)} %bitcast.38, ...), custom_call_target="tpu_custom_call" | custom-call | flops 5368709120 | bytes 16777216 | tf_op jit(solution)/shard_map/mlp_fwd_0/pallas_call | solution.py:359
  136.2 1.3 copy-done.16
  137.5 2.0 copy-done.11
  139.5 33.6 %attn_fwd_1.1 = (bf16[2,2,2,128,1024]{4,3,2,1,0:T(8,128)(2,1)S(1)}, bf16[2,512,256]{2,1,0:T(8,128)(2,1)S(1)}, bf16[2,512,256]{2,1,0:T(8,128)(2,1)S(1)}, bf16[2,5...) custom-call(bf16[2,512,1024]{2,1,0:T(8,128)(2,1)S(1)} %bitcast.45, f32[2,1024]{1,0:T(2,128)S(1)} %copy-done.13, ...), custom_call_target="tpu_custom_call" | custom-call | flops 4294967296 | bytes 16777216 | tf_op jit(solution)/shard_map/attn_fwd_1/pallas_call | solution.py:289
  173.1 0.8 copy-done.18
  173.9 1.3 copy-done.20
  175.2 0.8 copy-done.24
  176.0 0.8 copy-done.25
  176.8 0.8 copy-done.26
  177.6 73.3 %mlp_bwd_1.1 = (bf16[2,2,2,128,1024]{4,3,2,1,0:T(8,128)(2,1)}, f32[1,1024]{1,0:T(1,128)}, f32[4,176,1024]{2,1,0:T(8,128)}, bf16[4,176,1024]{2,1,0:T(8,128)(2,1)}, bf16[4,176,1024]{2,1,0:T(8,128)(2,1)}) custom-call(bf16[2,2,2,128,1024]{4,3,2,1,0:T(8,128)(2,1)} %copy-done.20, bf16[2,2,2,128,1024]{4,3,2,1,0:T(8,128)(2,1)} %bitcast.47, f32[2,1024]{1,0:T(2,128)} %refs_2_.3, ...), custom_call_target="tpu_custom_call" | custom-call | flops 12884901888 | bytes 33554432 | tf_op jit(solution)/shard_map/mlp_bwd_1/pallas_call | solution.py:471
  250.8 72.4 %attn_bwd_1.1 = (bf16[2,1,2,2,128,1024]{5,4,3,2,1,0:T(8,128)(2,1)}, f32[1,1024]{1,0:T(1,128)}, f32[4,1024]{1,0:T(4,128)}, f32[4,256,256]{2,1,0:T(8,128)}, f32[4,...) custom-call(bf16[2,512,1024]{2,1,0:T(8,128)(2,1)} %bitcast.46, ...), custom_call_target="tpu_custom_call" | custom-call | flops 8589934592 | bytes 33554432 | tf_op jit(solution)/shard_map/attn_bwd_1/pallas_call | solution.py:670
  323.3 79.6 %mlp_bwd_0.1 = (bf16[2,2,2,128,1024]{4,3,2,1,0:T(8,128)(2,1)}, f32[1,1024]{1,0:T(1,128)}, f32[4,176,1024]{2,1,0:T(8,128)}, bf16[4,176,1024]{2,1,0:T(8,128)(2,1)}...) custom-call(bf16[2,2,2,128,1024]{4,3,2,1,0:T(8,128)(2,1)} %copy-done.19, ...), custom_call_target="tpu_custom_call" | custom-call | flops 12884901888 | bytes 33554432 | tf_op jit(solution)/shard_map/mlp_bwd_0/pallas_call | solution.py:471
  403.0 3.2 pad_maximum_fusion
  406.2 1.3 concatenate.3.refs_14_
  407.5 90.5 %attn_bwd_0.1 = (bf16[4,2,2,2,32,1024]{5,4,3,2,1,0:T(8,128)(2,1)}, f32[16,1024]{1,0:T(8,128)}, bf16[4,176,1024]{2,1,0:T(8,128)(2,1)}, bf16[4,64,1024]{2,1,0:T(8,...) custom-call(bf16[2,512,1024]{2,1,0:T(8,128)(2,1)} %bitcast.44, ...), custom_call_target="tpu_custom_call" | custom-call | flops 8589934592 | bytes 33554432 | tf_op jit(solution)/shard_map/attn_bwd_0/pallas_call | solution.py:670
  498.0 4.4 maximum_bitcast_fusion
  502.5 1.1 pad_maximum_fusion.4
  504.0 1.1 pad_maximum_fusion.3
  505.1 1.5 pad_maximum_fusion.1
  506.6 0.6 pad_maximum_fusion.5
  507.3 0.7 select_reduce_fusion
  508.0 1.3 copy.25
  (81 shorter events, 0.8 us)
Async XLA Ops:
  0.6 34.9 %copy-start.43 = (f32[32,4]{0,1:T(4,128)S(1)}, f32[32,4]{0,1:T(4,128)}, u32[]{:S(2)}) copy-start(f32[32,4]{0,1:T(4,128)} %param.16) | copy-start | bytes 1540
  0.7 1.6 copy-start
  4.2 31.5 %copy-start.8 = (bf16[2,1024,256]{2,1,0:T(8,128)(2,1)S(1)}, bf16[2,1024,256]{2,1,0:T(8,128)(2,1)}, u32[]{:S(2)}) copy-start(bf16[2,1024,256]{2,1,0:T(8,128)(2,1)} %refs_8_.3) | copy-start | bytes 3145732
  4.2 31.5 %copy-start.9 = (bf16[2,1024,256]{2,1,0:T(8,128)(2,1)S(1)}, bf16[2,1024,256]{2,1,0:T(8,128)(2,1)}, u32[]{:S(2)}) copy-start(bf16[2,1024,256]{2,1,0:T(8,128)(2,1)} %refs_9_.3) | copy-start | bytes 3145732
  4.2 31.5 %copy-start.10 = (bf16[2,1024,256]{2,1,0:T(8,128)(2,1)S(1)}, bf16[2,1024,256]{2,1,0:T(8,128)(2,1)}, u32[]{:S(2)}) copy-start(bf16[2,1024,256]{2,1,0:T(8,128)(2,1)} %refs_10_.3) | copy-start | bytes 3145732
  4.2 31.5 %copy-start.13 = (f32[2,1024]{1,0:T(2,128)S(1)}, f32[2,1024]{1,0:T(2,128)}, u32[]{:S(2)}) copy-start(f32[2,1024]{1,0:T(2,128)} %refs_7_.3) | copy-start | bytes 24580
  35.4 36.1 %copy-start.7 = (bf16[2,4,128,1024]{3,2,1,0:T(8,128)(2,1)}, bf16[2,4,128,1024]{3,2,1,0:T(8,128)(2,1)S(1)}, u32[]{:S(2)}) copy-start(bf16[2,4,128,1024]{3,2,1,0:T(8,128)(2,1)S(1)} %get-tuple-element.53) | copy-start | bytes 6291460
  35.4 102.1 %copy-start.14 = (s32[4,2,128]{2,1,0:T(2,128)}, s32[4,2,128]{2,1,0:T(2,128)S(1)}, u32[]{:S(2)}) copy-start(s32[4,2,128]{2,1,0:T(2,128)S(1)} %get-tuple-element.54.mask_ref.refs_13_) | copy-start | bytes 12292
  35.7 101.8 %copy-start.2 = (f32[4,1024]{1,0:T(4,128)}, f32[4,1024]{1,0:T(4,128)S(1)}, u32[]{:S(2)}) copy-start(f32[4,1024]{1,0:T(4,128)S(1)} %select_reduce_fusion.1.t_ref.refs_12_) | copy-start | bytes 49156
  35.7 38.3 %copy-start.4 = (bf16[2,1024,704]{1,2,0:T(8,128)(2,1)S(1)}, bf16[2,1024,704]{1,2,0:T(8,128)(2,1)}, u32[]{:S(2)}) copy-start(bf16[2,1024,704]{1,2,0:T(8,128)(2,1)} %param.23) | copy-start | bytes 8650756
  35.7 38.3 %copy-start.12 = (f32[2,1024]{1,0:T(2,128)S(1)}, f32[2,1024]{1,0:T(2,128)}, u32[]{:S(2)}) copy-start(f32[2,1024]{1,0:T(2,128)} %refs_2_.3) | copy-start | bytes 24580
  74.0 62.2 %copy-start.17 = (bf16[2,2,256,256]{3,2,1,0:T(8,128)(2,1)}, bf16[2,2,256,256]{3,2,1,0:T(8,128)(2,1)S(1)}, u32[]{:S(2)}) copy-start(bf16[2,2,256,256]{3,2,1,0:T(8,128)(2,1)S(1)} %get-tuple-element.74) | copy-start | bytes 1572868
  74.0 62.2 %copy-start.19 = (bf16[2,2,2,128,1024]{4,3,2,1,0:T(8,128)(2,1)}, bf16[2,2,2,128,1024]{4,3,2,1,0:T(8,128)(2,1)S(1)}, u32[]{:S(2)}) copy-start(bf16[2,2,2,128,1024]{4,3,2,1,0:T(8,128)(2,1)S(1)} %get-tuple-element.56.x1_ref.refs_0_) | copy-start | bytes 6291460
  74.0 2.8 copy-start.5
  76.8 1.6 copy-start.6
  137.5 35.6 %copy-start.15 = (bf16[2,2,2,128,1024]{4,3,2,1,0:T(8,128)(2,1)}, bf16[2,2,2,128,1024]{4,3,2,1,0:T(8,128)(2,1)S(1)}, u32[]{:S(2)}) copy-start(bf16[2,2,2,128,1024]{4,3,2,1,0:T(8,128)(2,1)S(1)} %get-tuple-element.57) | copy-start | bytes 6291460
  137.5 2.0 copy-start.11
  323.3 79.7 %copy-start.29 = (bf16[4,176,1024]{2,1,0:T(8,128)(2,1)S(1)}, bf16[4,176,1024]{2,1,0:T(8,128)(2,1)}, u32[]{:S(2)}) copy-start(bf16[4,176,1024]{2,1,0:T(8,128)(2,1)} %get-tuple-element.94) | copy-start | bytes 4325380
  402.9 3.3 copy-start.38
  402.9 3.2 copy-start.40
  402.9 3.2 copy-start.41
  403.0 3.2 copy-start.42
  407.5 90.5 %copy-start.28 = (bf16[4,176,1024]{2,1,0:T(8,128)(2,1)S(1)}, bf16[4,176,1024]{2,1,0:T(8,128)(2,1)}, u32[]{:S(2)}) copy-start(bf16[4,176,1024]{2,1,0:T(8,128)(2,1)} %get-tuple-element.90) | copy-start | bytes 4325380
  498.0 4.4 copy-start.31
  498.0 4.4 copy-start.33
  502.5 1.6 copy-start.32
  502.5 2.6 copy-start.34
  502.5 2.6 copy-start.35
  502.5 2.6 copy-start.36
  502.5 2.6 copy-start.37
  505.1 1.5 copy-start.39
  505.1 2.9 copy-start.27
  (12 other events, 11.3 us)

commit v5 on v4

--- a/solution.py
+++ b/solution.py
@@ -131,8 +131,27 @@
     return [make(0, 'z', 'y', z, y, lambda a, b: (a, b)), make(1, 'y', 'z', y, z, lambda a, b: (b, a))]
 
 
-def grad_stream(part, near, far, out, send, recv, ids, x, core):
-    return Stream(lambda q: part.at[q], near, far, lambda q: out.at[q], send, recv, ids['core'], ids['x'], core, x, lambda a, b: b * 2 + a)
+class GradStream(Stream):
+    def __init__(self, part, near, far, own_ref, out, send, recv, local, ids, x, core):
+        super().__init__(lambda q: part.at[q], near, far, lambda q: out.at[q], send, recv,
+                         ids['core'], ids['x'], core, x, lambda a, b: b * 2 + a)
+        self.own_ref, self.local = own_ref, local
+
+    def send_both(self):
+        self.send_away(0)
+        self.send_away(1)
+
+    def finish(self):
+        self.own_ref[...] = self.total().astype(BF16)
+        out = self.out(self.own)
+        self.start(4, self.own_ref, out, self.second)
+        self.start(3, self.own_ref, out, self.first)
+        self.kept = pltpu.make_async_copy(self.own_ref, out, self.local)
+        self.kept.start()
+
+    def close(self):
+        super().close()
+        self.kept.wait()
 
 
 def grad_into(part, a, b):
@@ -367,39 +386,54 @@
     )(x1, d_y.reshape(4, 2, 128, width), gains, wg_t, wl_t, w_out)
 
 
-def mlp_bwd_kernel(layer, n_carry, *refs):
+def layer_bwd_kernel(layer, seq, last, *refs):
     refs = list(refs)
-    x1_ref, dy_ref, g_ref, wg_all, wl_all, wo_all = [refs.pop(0) for _ in range(6)]
-    carried = [refs.pop(0) for _ in range(n_carry)]
-    dm_ref, dg_ref, lin_out, gout_ref, ggate_ref = [refs.pop(0) for _ in range(5)]
-    carried_out = [refs.pop(0) for _ in range(n_carry)]
-    wg_ref, wl_ref, wo_ref, wsem, part, near, far, h2_ref, gated_ref, dgate_ref, dlin_ref = [refs.pop(0) for _ in range(11)]
-    lin_part, lin_sem, p0, n0, f0, p1, n1, f1 = [refs.pop(0) for _ in range(8)]
-    carry_scratch = [[refs.pop(0) for _ in range(2)] for _ in range(n_carry)]
-    send, recv = refs
-    loads = load_layer(layer, [wg_all, wl_all, wo_all], [wg_ref, wl_ref, wo_ref], wsem)
+    take = lambda n: [refs.pop(0) for _ in range(n)]
+    stacks = take(7)
+    arrays = take(7)
+    ga_ref, gm_ref, t_ref, mask_ref = take(4)
+    if last:
+        small_ref, = take(1)
+    dx_ref, small_out = take(2)
+    grad_out = take(7)
+    weights, holds = take(7), take(7)
+    wsem, hsem = take(2)
+    wg_ref, wl_ref, wd_ref, wq_ref, wk_ref, wv_ref, wo_ref = weights
+    x1_ref, dy_ref, x_ref, q_ref, k_ref, v_ref, o_ref = holds
+    part, near, far, dm_ref, h_ref, gated_ref, dgate_ref, dlin_ref = take(8)
+    bias_ref, do_ref, dq_ref, dk_ref, dv_ref, dt_ref = take(6)
+    grad_scratch = [take(4) for _ in range(7)]
+    send, recv, local = take(3)
+    if last:
+        own_ref, acc_small, got_small, csend, crecv = take(5)
     tp, cp, z, y, x, core, ids = place()
-    meet(ids, ['z', 'y', 'x', 'core'])
-    zy, yz = streams = colours(part, near, far, lambda q, c: dm_ref.at[q[0], q[1], c], send, recv, ids, z, y)
-    g_out = grad_stream(p0, n0, f0, gout_ref, send.at[2], recv.at[2], ids, x, core)
-    g_gate = grad_stream(p1, n1, f1, ggate_ref, send.at[3], recv.at[3], ids, x, core)
-    g_carry = [grad_stream(p, s[0], s[1], out, send.at[4 + i], recv.at[4 + i], ids, x, core)
-               for i, (p, s, out) in enumerate(zip(carried, carry_scratch, carried_out))]
-    gain = g_ref[layer:layer + 1, :]
-    for g in g_carry:
-        g.send_away(0)
-        g.send_away(1)
-    for copy in loads:
+    w_loads = [pltpu.make_async_copy(w.at[layer], r, wsem.at[i]) for i, (w, r) in enumerate(zip(stacks, weights))]
+    a_loads = [pltpu.make_async_copy(w, r, hsem.at[i]) for i, (w, r) in enumerate(zip(arrays, holds))]
+    first_loads = [a_loads[0], w_loads[0], w_loads[1], a_loads[1], w_loads[2]]
+    later_loads = a_loads[2:] + w_loads[3:]
+    for copy in first_loads + later_loads:
+        copy.start()
+    meet(ids, ['z', 'y', 'x', 'core'] + (['xc'] if last else []))
+    heads = t_ref.shape[0]
+    width = x_ref.shape[-1]
+    deep = 32 if last else 128
+    across = 128 // deep
+    g_out, g_gate, g_lin, g_o, g_q, g_k, g_v = grads = [
+        GradStream(*grad_scratch[i], grad_out[i], send.at[4 + i], recv.at[4 + i], local.at[i], ids, x, core) for i in range(7)]
+    p_out, p_gate, p_lin, p_o, p_q, p_k, p_v = [g[0] for g in grad_scratch]
+    zy, yz = mlp_sum = colours(part, near, far, lambda q, c: dm_ref.at[q[0], q[1], c], send.at[0:2], recv.at[0:2], ids, z, y)
+    for copy in first_loads:
         copy.wait()
-
-    def compute(q):
+    gain = gm_ref[layer:layer + 1, :]
+
+    def mlp_quarter(q):
         h2 = norm(x1_ref[q].reshape(256, -1), gain)
         rows = pl.ds(pl.multiple_of((q[0] * 2 + q[1]) * 256, 256), 256)
-        h2_ref[rows, :] = h2
+        h_ref[rows, :] = h2
         value, slope = gelu_parts(dot(h2, wg_ref[...], NT))
         lin = dot(h2, wl_ref[...], NT)
         gated_ref[rows, :] = (value * lin).astype(BF16)
-        d_gated = dot(dy_ref[q].reshape(256, -1), wo_ref[...], NT)
+        d_gated = dot(dy_ref[q].reshape(256, -1), wd_ref[...], NT)
         d_lin = (d_gated * value).astype(BF16)
         d_gate = (d_gated * lin * slope).astype(BF16)
         dlin_ref[rows, :] = d_lin
@@ -407,273 +441,209 @@
         part[q] = (dot(d_gate, wg_ref[...]) + dot(d_lin, wl_ref[...])).reshape(part.shape[2:])
 
     quarters = order(z, y)
-    compute(quarters[0])
+    mlp_quarter(quarters[0])
     zy.send_away(0)
     yz.send_away(0)
-    for g in g_carry:
-        g.forward()
-    compute(quarters[1])
+    mlp_quarter(quarters[1])
     zy.send_away(1)
-    compute(quarters[2])
+    mlp_quarter(quarters[2])
     yz.send_away(1)
-    compute(quarters[3])
-    grad_into(p0, gated_ref[...], dy_ref[...].reshape(h2_ref.shape))
-    g_out.send_away(0)
-    g_out.send_away(1)
-    grad_into(p1, dgate_ref[...], h2_ref)
+    mlp_quarter(quarters[3])
+    grad_into(p_out, gated_ref[...], dy_ref[...].reshape(h_ref.shape))
+    g_out.send_both()
+    grad_into(p_gate, dgate_ref[...], h_ref)
+    g_gate.send_both()
     g_out.forward()
-    g_gate.send_away(0)
-    g_gate.send_away(1)
-    for s in streams:
+    for s in mlp_sum:
         s.forward()
+    grad_into(p_lin, dlin_ref[...], h_ref)
+    g_lin.send_both()
     g_gate.forward()
-    grad_into(lin_part, dlin_ref[...], h2_ref)
-    save = pltpu.make_async_copy(lin_part, lin_out, lin_sem)
-    save.start()
-    for g in g_carry:
-        g.finish()
+    for copy in later_loads:
+        copy.wait()
+    gain_a = ga_ref[layer:layer + 1, :]
+    for b in range(2):
+        h_ref[b * seq:(b + 1) * seq, :] = norm(x_ref[b], gain_a)
+    g_lin.forward()
     g_out.finish()
-    d_gain = 0.0
-    for c, s in enumerate(streams):
+    dg_m = 0.0
+    for c, s in enumerate(mlp_sum):
         d_x, dg = norm_back(s.total(), x1_ref[z, y, c], gain)
         dm_ref[z, y, c] = (d_x + dy_ref[z, y, c].astype(F32)).astype(BF16)
         s.publish()
-        d_gain = d_gain + jnp.sum(dg, axis=0, keepdims=True)
-    dg_ref[...] = d_gain
-    for g in g_carry:
-        g.gather()
+        dg_m = dg_m + jnp.sum(dg, axis=0, keepdims=True)
     g_gate.finish()
-    for s in streams:
+    for s in mlp_sum:
         s.gather()
     g_out.gather()
-    g_gate.gather()
-    for s in g_carry + streams + [g_out, g_gate]:
+    for s in mlp_sum:
         s.close()
-    save.wait()
-
-
-def grad_scratch_of(block):
-    return [pltpu.VMEM((4,) + block, F32), pltpu.VMEM((2,) + block, F32), pltpu.VMEM(block, F32)]
-
-
-def mlp_bwd(layer, collective_id, x1, dy, gains, wg_t, wl_t, w_out, carried=()):
-    dma = pltpu.SemaphoreType.DMA
-    ff, width = wg_t.shape[1:]
-    block = (ff // 4, width)
-    rows = 1024
-    out_shape = [jax.ShapeDtypeStruct(x1.shape, BF16), jax.ShapeDtypeStruct((1, width), F32), jax.ShapeDtypeStruct((4,) + block, F32)]
-    out_shape += [jax.ShapeDtypeStruct((4,) + block, BF16)] * 2 + [jax.ShapeDtypeStruct(c.shape, BF16) for c in carried]
-    scratch = layer_scratch(wg_t, wl_t, w_out) + sum_scratch(0, x1.shape[3:]) + [pltpu.VMEM((rows, width), BF16)] + [pltpu.VMEM((rows, ff), BF16)] * 3
-    scratch += [pltpu.VMEM((4,) + block, F32), dma] + grad_scratch_of(block) * 2
-    for c in carried:
-        scratch += grad_scratch_of(c.shape[1:])[1:]
-    n = 4 + len(carried)
-    return pl.pallas_call(
-        functools.partial(mlp_bwd_kernel, layer, len(carried)),
-        out_shape=out_shape,
-        in_specs=vmem_specs(3) + any_specs(3) + vmem_specs(len(carried)), out_specs=vmem_specs(2) + any_specs(1) + vmem_specs(2 + len(carried)),
-        scratch_shapes=scratch + [dma((n, 6)), dma((n, 6))],
-        compiler_params=pltpu.CompilerParams(collective_id=collective_id, has_side_effects=True, vmem_limit_bytes=58 << 20),
-        cost_estimate=pl.CostEstimate(flops=12 << 30, bytes_accessed=32 << 20, transcendentals=0),
-        name=f"mlp_bwd_{layer}",
-    )(x1, dy, gains, wg_t, wl_t, w_out, *carried)
-
-
-def attn_bwd_kernel(layer, seq, last, *refs):
-    refs = list(refs)
-    x_ref, dm_ref, lin_part, q_ref, k_ref, v_ref, o_ref, g_ref, wq_all, wk_all, wv_all, wo_all, t_ref, mask_ref = [refs.pop(0) for _ in range(14)]
-    if last:
-        small_ref = refs.pop(0)
-    dx_ref = refs.pop(0)
-    if last:
-        small_out = refs.pop(0)
-    else:
-        dg_ref, dt_ref, q_part, k_part = [refs.pop(0) for _ in range(4)]
-    n_grads = 4 if last else 2
-    grad_out = [refs.pop(0) for _ in range(1 + n_grads)]
-    wq_ref, wk_ref, wv_ref, wo_ref, wsem = [refs.pop(0) for _ in range(5)]
-    loads = load_layer(layer, [wq_all, wk_all, wv_all, wo_all], [wq_ref, wk_ref, wv_ref, wo_ref], wsem)
-    part, near, far = [refs.pop(0) for _ in range(3)]
-    bias_ref, acc_ref, do_ref, dq_ref, dk_ref, dv_ref, h_ref = [refs.pop(0) for _ in range(7)]
-    lin_near, lin_far = refs.pop(0), refs.pop(0)
-    grad_scratch = [[refs.pop(0) for _ in range(3)] for _ in range(n_grads)]
-    send, recv = refs.pop(0), refs.pop(0)
-    if last:
-        own_ref, acc_small, got_small, csend, crecv = [refs.pop(0) for _ in range(5)]
-    tp, cp, z, y, x, core, ids = place()
-    heads = t_ref.shape[0]
-    across, deep = part.shape[3], part.shape[4]
-    meet(ids, ['z', 'y', 'x', 'core'] + (['xc'] if last else []))
+
     if last:
         def region(q, c):
             return dx_ref.at[:, q[0], q[1], c]
     else:
         def region(q, c):
-            return dx_ref.at[q[0], :, q[1], c]
-    zy, yz = streams = colours(part, near, far, region, send, recv, ids, z, y)
-    g_lin = grad_stream(lin_part, lin_near, lin_far, grad_out[0], send.at[2], recv.at[2], ids, x, core)
-    g_o, *g_qkv = [grad_stream(s[0], s[1], s[2], out, send.at[3 + i], recv.at[3 + i], ids, x, core)
-                          for i, (s, out) in enumerate(zip(grad_scratch, grad_out[1:]))]
-    gain = g_ref[layer:layer + 1, :]
-    g_lin.send_away(0)
-    g_lin.send_away(1)
-    for copy in loads:
-        copy.wait()
+            return dx_ref.at[q[0], q[1], c]
+    zy, yz = attn_sum = colours(part, near, far, region, send.at[2:4], recv.at[2:4], ids, z, y)
 
     def attend(b, step):
         add = key_add(mask_ref, b)
-        d_mid = dm_ref[b].reshape(seq, -1)
-        do_ref[...] = dot(d_mid, wo_ref[...], NT).astype(BF16)
+        do_ref[...] = dot(dm_ref[b].reshape(seq, width), wo_ref[...], NT).astype(BF16)
         for head in range(heads):
-            if step == 0:
-                bias_ref[head] = toeplitz(t_ref[head:head + 1, :], seq)
+            bias_ref[...] = toeplitz(t_ref[head:head + 1, :], seq)
             cols = pl.ds(head * HEAD, HEAD)
             q, k, v, do = q_ref[b, :, cols], k_ref[b, :, cols], v_ref[b, :, cols], do_ref[:, cols]
-            e, total = exp_scores(q, k, bias_ref[head], add)
+            e, total = exp_scores(q, k, bias_ref[...], add)
             p = e * (1.0 / total)
             row_dot = jnp.sum(do.astype(F32) * o_ref[b, :, cols].astype(F32), axis=-1, keepdims=True)
             ds = p * (dot(do, v, NT) - row_dot)
-            if step == 0:
-                acc_ref[head] = ds
-            else:
-                sums = diag_sums(acc_ref[head] + ds, seq)
-                if last:
-                    acc_small[0, 8 + head:9 + head, :] = small_ref[8 + head:9 + head, :] + sums
-                else:
-                    dt_ref[head:head + 1, :] = sums
+            sums = diag_sums(ds, seq)
+            dt_ref[head:head + 1, :] = sums if step == 0 else dt_ref[head:head + 1, :] + sums
             dsl = ds.astype(BF16)
             dq_ref[b, :, cols] = dot(dsl, k).astype(BF16)
             dk_ref[b, :, cols] = dot(dsl, q, TN).astype(BF16)
             dv_ref[b, :, cols] = dot(p.astype(BF16), do, TN).astype(BF16)
-            if step == 0 and head == 0:
-                g_lin.forward()
-        for half in range(2):
-            rows = pl.ds(half * 256, 256)
-            h_ref[pl.ds(pl.multiple_of(b * seq + half * 256, 256), 256), :] = norm(x_ref[b, rows, :], gain)
-
-    def compute(q):
-        def rows(ref):
-            whole = ref[q[0]].reshape(across, 2, 2 * deep, ref.shape[-1]) if across > 1 else None
-            if across == 1:
-                return ref[q[0], pl.ds(pl.multiple_of(q[1] * 2 * deep, 2 * deep), 2 * deep), :]
-            pieces = [ref[q[0], pl.ds(pl.multiple_of(j * 4 * deep + q[1] * 2 * deep, 2 * deep), 2 * deep), :] for j in range(across)]
-            return jnp.concatenate(pieces, axis=0)
-        total = dot(rows(dq_ref), wq_ref[...], NT) + dot(rows(dk_ref), wk_ref[...], NT) + dot(rows(dv_ref), wv_ref[...], NT)
-        total = total.reshape(across, 2, deep, total.shape[-1])
+            if step == 1 and head == 0:
+                g_o.forward()
+
+    def pick(ref, q, offset, size):
+        pieces = [ref[q[0], pl.ds(pl.multiple_of(j * 4 * deep + q[1] * 2 * deep + offset, deep), size), :] for j in range(across)]
+        return pieces[0] if across == 1 else jnp.concatenate(pieces, axis=0)
+
+    def attn_quarter(q):
+        total = sum(dot(pick(d, q, 0, 2 * deep), w[...], NT) for d, w in [(dq_ref, wq_ref), (dk_ref, wk_ref), (dv_ref, wv_ref)])
+        total = total.reshape(across, 2, deep, width)
         for c in range(2):
-            part[q[0], q[1], c] = total[:, c]
-
-    quarters = order(z, y)
+            part[q[0], q[1], c] = total[:, c].reshape(across * deep, width)
+
     attend(1 - z, 0)
-    compute(quarters[0])
+    attn_quarter(quarters[0])
     zy.send_away(0)
     yz.send_away(0)
-    compute(quarters[1])
+    attn_quarter(quarters[1])
     zy.send_away(1)
-    grad_into(grad_scratch[0][0], o_ref[...].reshape(2 * seq, -1), dm_ref[...].reshape(2 * seq, -1))
-    g_o.send_away(0)
-    g_o.send_away(1)
+    grad_into(p_o, o_ref[...].reshape(2 * seq, -1), dm_ref[...].reshape(2 * seq, width))
+    g_o.send_both()
+    g_lin.finish()
     attend(z, 1)
-    compute(quarters[2])
+    attn_quarter(quarters[2])
     yz.send_away(1)
-    g_o.forward()
-    compute(quarters[3])
-    for g, scratch, d_ref in zip(g_qkv, grad_scratch[1:], [dv_ref, dk_ref, dq_ref]):
-        grad_into(scratch[0], h_ref[...], d_ref[...].reshape(2 * seq, -1))
-        g.send_away(0)
-        g.send_away(1)
-    for s in streams:
+    attn_quarter(quarters[3])
+    for g, p, d in [(g_q, p_q, dq_ref), (g_k, p_k, dk_ref), (g_v, p_v, dv_ref)]:
+        grad_into(p, h_ref[...], d[...].reshape(2 * seq, -1))
+        g.send_both()
+    for s in attn_sum:
         s.forward()
-    for g in g_qkv:
+    for g in [g_q, g_k, g_v]:
         g.forward()
-    if not last:
-        for p, d_ref in zip([q_part, k_part], [dq_ref, dk_ref]):
-            grad_into(p, h_ref[...], d_ref[...].reshape(2 * seq, -1))
-    g_lin.finish()
+    g_gate.gather()
+    g_lin.gather()
     g_o.finish()
-
-    d_gain = 0.0
+    dg_a = 0.0
     moves = []
-    for c, s in enumerate(streams):
-        def own(ref):
-            pieces = [ref[z, pl.ds(pl.multiple_of(j * 4 * deep + y * 2 * deep + c * deep, deep), deep), :] for j in range(across)]
-            return jnp.concatenate(pieces, axis=0)
-        d_x, dg = norm_back(s.total().reshape(across * deep, -1), own(x_ref), gain)
-        d_gain = d_gain + jnp.sum(dg, axis=0, keepdims=True)
-        d_x = (d_x + own(dm_ref).astype(F32)).astype(BF16).reshape(across, deep, -1)
+    dm_flat = dm_ref
+    for c, s in enumerate(attn_sum):
+        d_x, dg = norm_back(s.total(), pick(x_ref, (z, y), c * deep, deep), gain_a)
+        dg_a = dg_a + jnp.sum(dg, axis=0, keepdims=True)
         if last:
-            own_ref[c] = d_x
+            res = jnp.concatenate([dm_ref[z, j // 2, j % 2, pl.ds(pl.multiple_of(y * 2 * deep + c * deep, deep), deep), :] for j in range(4)], axis=0)
+        else:
+            res = dm_ref[z, y, c]
+        d_x = (d_x + res.astype(F32)).astype(BF16)
+        if last:
+            own_ref[c] = d_x.reshape(across, deep, width)
             dx_ref[cp, z, y, c] = own_ref[c, cp]
             moves.append([remote(own_ref.at[c, ids[name]['cp']], dx_ref.at[cp, z, y, c], csend.at[c, i], crecv.at[c, i], ids[name])
                           for i, name in enumerate(['x', 'xc', 'core'])])
         else:
-            dx_ref[z, :, y, c] = d_x
+            dx_ref[z, y, c] = d_x
             s.publish()
-    for g in g_qkv:
-        g.finish()
-    if last:
-        acc_small[0, 0:4, :] = jnp.concatenate([small_ref[0:3, :], d_gain], axis=0)
-        acc_small[0, 4:8, :] = jnp.zeros((4, d_gain.shape[1]), F32)
-        acc_small[0, 12:16, :] = jnp.zeros((4, d_gain.shape[1]), F32)
-        for c, s in enumerate(streams):
+    if not last:
+        small_out[0:1, :] = dg_a
+        small_out[1:2, :] = dg_m
+        small_out[2:4, :] = jnp.zeros((2, width), F32)
+        small_out[4:8, :] = dt_ref[0:4, :]
+        for g in [g_q, g_k, g_v]:
+            g.finish()
+        for s in attn_sum:
+            s.gather()
+    else:
+        acc_small[0, 0:2, :] = small_ref[0:2, :]
+        acc_small[0, 2:3, :] = dg_a
+        acc_small[0, 3:4, :] = dg_m
+        acc_small[0, 4:8, :] = jnp.zeros((4, width), F32)
+        acc_small[0, 8:12, :] = small_ref[4:8, :] + dt_ref[0:4, :]
+        acc_small[0, 12:16, :] = jnp.zeros((4, width), F32)
+        smalls = []
+
+        def small_start(i):
+            rows = pl.ds(0, 16 if i < 2 else 8)
+            smalls.append(remote(acc_small.at[i, rows], got_small.at[i, rows], csend.at[2, i], crecv.at[2, i], ids[['z', 'y', 'core', 'x'][3 - i]]))
+
+        def small_end(i):
+            rows = pl.ds(0, 16 if i < 2 else 8)
+            smalls[i].wait_recv()
+            acc_small[i + 1, rows, :] = acc_small[i, rows, :] + got_small[i, rows, :]
+
+        small_start(0)
+        for c, s in enumerate(attn_sum):
             for copy in moves[c]:
                 copy.wait_recv()
             s.publish()
-        smalls = []
-        for i, name in enumerate(['x', 'core', 'z', 'y']):
-            rows = pl.ds(0, 16 if i < 2 else 8)
-            smalls.append(remote(acc_small.at[i, rows], got_small.at[i, rows], csend.at[2, i], crecv.at[2, i], ids[name]))
-            smalls[i].wait_recv()
-            acc_small[i + 1, rows, :] = acc_small[i, rows, :] + got_small[i, rows, :]
+        g_q.finish()
+        small_end(0)
+        small_start(1)
+        g_k.finish()
+        small_end(1)
+        small_start(2)
+        g_v.finish()
+        for s in attn_sum:
+            s.gather()
+        small_end(2)
+        small_start(3)
+    g_o.gather()
+    for g in [g_q, g_k, g_v]:
+        g.gather()
+    if last:
+        small_end(3)
         small_out[0:8, :] = acc_small[4, 0:8, :]
         small_out[8:16, :] = acc_small[2, 8:16, :]
         for copy in smalls + moves[0] + moves[1]:
             copy.wait_send()
-    else:
-        dg_ref[...] = d_gain
-    for s in streams:
-        s.gather()
-    g_lin.gather()
-    g_o.gather()
-    for g in g_qkv:
-        g.gather()
-    for s in streams + [g_lin, g_o] + g_qkv:
+    for s in attn_sum + grads:
         s.close()
 
 
-def attn_bwd(layer, collective_id, x, d_mid, lin_part, q, k, v, o, gains, w_q, w_k, w_v, w_o, table, mask, small=None):
-    seq, width = 512, w_q.shape[1]
-    cols = w_q.shape[2]
+def layer_bwd(layer, collective_id, x1, dy, x, q, k, v, o, gains_a, gains_m, wg_t, wl_t, w_out, w_q, w_k, w_v, w_o, table, mask, small=None):
+    seq, width, cols = 512, w_q.shape[1], w_q.shape[2]
+    ff = w_out.shape[1]
+    rows = 2 * seq
     last = small is not None
     dma = pltpu.SemaphoreType.DMA
-    operands = [x.reshape(2, seq, width), d_mid.reshape(2, seq, width), lin_part, q, k, v, o.reshape(2, seq, cols), gains, w_q, w_k, w_v, w_o, table, mask]
-    in_specs = vmem_specs(8) + any_specs(4) + vmem_specs(2)
-    blocks = (4, 32, width) if last else (1, 128, width)
-    if last:
-        operands.append(small)
-        in_specs += vmem_specs(1)
-        out_shape = [jax.ShapeDtypeStruct((4, 2, 2, 2, 32, width), BF16), jax.ShapeDtypeStruct((16, width), F32)]
-    else:
-        out_shape = [jax.ShapeDtypeStruct((2, 1, 2, 2, 128, width), BF16), jax.ShapeDtypeStruct((1, width), F32), jax.ShapeDtypeStruct(table.shape, F32)]
-        out_shape += [jax.ShapeDtypeStruct((4, width // 4, cols), F32)] * 2
-    shapes = [(cols // 4, width)] + [(width // 4, cols)] * (3 if last else 1)
-    lin_block = lin_part.shape[1:]
-    out_shape += [jax.ShapeDtypeStruct((4,) + s, BF16) for s in [lin_block] + shapes]
-    scratch = layer_scratch(w_q, w_k, w_v, w_o) + sum_scratch(0, blocks) + [pltpu.VMEM((table.shape[0], seq, seq), F32)] * 2 + [pltpu.VMEM((seq, cols), BF16)]
-    scratch += [pltpu.VMEM((2, seq, cols), BF16)] * 3 + [pltpu.VMEM((2 * seq, width), BF16)]
-    scratch += [pltpu.VMEM((2,) + lin_block, F32), pltpu.VMEM(lin_block, F32)]
-    for s in shapes:
-        scratch += grad_scratch_of(s)
-    scratch += [dma((7, 6)), dma((7, 6))]
+    blocks = (2, 2, 2, 128, width)
+    stacks = [wg_t, wl_t, w_out, w_q, w_k, w_v, w_o]
+    arrays = [x1.reshape(blocks), dy.reshape(blocks), x.reshape(2, seq, width), q, k, v, o.reshape(2, seq, cols)]
+    operands = stacks + arrays + [gains_a, gains_m, table, mask] + ([small] if last else [])
+    in_specs = any_specs(14) + vmem_specs(5 if last else 4)
+    out_shape = [jax.ShapeDtypeStruct((4, 2, 2, 2, 32, width) if last else blocks, BF16), jax.ShapeDtypeStruct((16 if last else 8, width), F32)]
+    grads = [(ff // 4, width)] * 3 + [(cols // 4, width)] + [(width // 4, cols)] * 3
+    out_shape += [jax.ShapeDtypeStruct((4,) + g, BF16) for g in grads]
+    scratch = [pltpu.VMEM(w.shape[1:], BF16) for w in stacks] + [pltpu.VMEM(a.shape, BF16) for a in arrays] + [dma((7,)), dma((7,))]
+    scratch += sum_scratch(0, blocks[3:]) + [pltpu.VMEM(blocks, BF16), pltpu.VMEM((rows, width), BF16)] + [pltpu.VMEM((rows, ff), BF16)] * 3
+    scratch += [pltpu.VMEM((seq, seq), F32), pltpu.VMEM((seq, cols), BF16)] + [pltpu.VMEM((2, seq, cols), BF16)] * 3 + [pltpu.VMEM((8, 2 * seq), F32)]
+    for g in grads:
+        scratch += [pltpu.VMEM((4,) + g, F32), pltpu.VMEM((2,) + g, F32), pltpu.VMEM(g, F32), pltpu.VMEM(g, BF16)]
+    scratch += [dma((11, 6)), dma((11, 6)), dma((7,))]
     if last:
         scratch += [pltpu.VMEM((2, 4, 32, width), BF16), pltpu.VMEM((5, 16, width), F32), pltpu.VMEM((4, 16, width), F32), dma((3, 4)), dma((3, 4))]
     return pl.pallas_call(
-        functools.partial(attn_bwd_kernel, layer, seq, last),
-        out_shape=out_shape, in_specs=in_specs, out_specs=vmem_specs(len(out_shape)),
+        functools.partial(layer_bwd_kernel, layer, seq, last),
+        out_shape=out_shape, in_specs=in_specs, out_specs=vmem_specs(2) + any_specs(7),
         scratch_shapes=scratch,
-        compiler_params=pltpu.CompilerParams(collective_id=collective_id, has_side_effects=True, vmem_limit_bytes=62 << 20),
-        cost_estimate=pl.CostEstimate(flops=8 << 30, bytes_accessed=32 << 20, transcendentals=0),
-        name=f"attn_bwd_{layer}",
+        compiler_params=pltpu.CompilerParams(collective_id=collective_id, has_side_effects=True, vmem_limit_bytes=67043328),
+        cost_estimate=pl.CostEstimate(flops=20 << 30, bytes_accessed=48 << 20, transcendentals=0),
+        name=f"layer_bwd_{layer}",
     )(*operands)
 
 
@@ -699,11 +669,9 @@
         x1, dy = mlp_fwd(0, 2, a0, d_y, g_mlp, wg_t, wl_t, w_out)
         a1, q1, k1, v1, o1 = attn_layer(1, 3, x1, g_attn, w_q, w_k, w_v, table, mask, w_full)
 
-        dm, dgm1, lin, out1, gate1 = mlp_bwd(1, 4, a1, dy.reshape(quarters), g_mlp, wg_t, wl_t, w_out)
-        dx, dga1, dt1, q_part, k_part, lin1, wo1, wv1 = attn_bwd(1, 5, x1, dm, lin, q1, k1, v1, o1, g_attn, w_q, w_k, w_v, w_o, table, mask)
-        dm, dgm0, lin, out0, gate0, wq1, wk1 = mlp_bwd(0, 6, a0, dx.reshape(quarters), g_mlp, wg_t, wl_t, w_out, (q_part, k_part))
-        small = jnp.concatenate([dga1, dgm1, dgm0, jnp.zeros((5, width), F32), dt1, jnp.zeros((4, width), F32)], axis=0)
-        d_x, small, lin0, wo0, wv0, wk0, wq0 = attn_bwd(0, 7, x0, dm, lin, q0, k0, v0, o0, g_attn, w_q, w_k, w_v, w_o, table, mask, small)
+        rest = (g_attn, g_mlp, wg_t, wl_t, w_out, w_q, w_k, w_v, w_o, table, mask)
+        dx, small, out1, gate1, lin1, wo1, wq1, wk1, wv1 = layer_bwd(1, 4, a1, dy, x1, q1, k1, v1, o1, *rest)
+        d_x, small, out0, gate0, lin0, wo0, wq0, wk0, wv0 = layer_bwd(0, 5, a0, dx, x0, q0, k0, v0, o0, *rest, small)
 
         def both(first, second, like, swap=False):
             shape = (like.shape[2], like.shape[1]) if swap else like.shape[1:]
@@ -711,8 +679,8 @@
             return jnp.swapaxes(pair, 1, 2) if swap else pair
 
         d_bias = jnp.sum(jnp.where(onehot[None], small[8:12][:, None, :], 0.0), axis=2).T
-        d_ga = jnp.stack([small[3], small[0]])
-        d_gm = jnp.stack([small[2], small[1]])
+        d_ga = jnp.stack([small[2], small[0]])
+        d_gm = jnp.stack([small[3], small[1]])
         return (d_x.reshape(x_in.shape), d_bias, d_ga, d_gm, both(wq0, wq1, w_q), both(wk0, wk1, w_k), both(wv0, wv1, w_v),
                 both(wo0, wo1, w_o), both(gate0, gate1, w_gate, True), both(lin0, lin1, w_lin, True), both(out0, out1, w_out))
 

time: 517 us -> 487 us (0.942)
  Pallas kernels: 474 us -> 448 us
    pallas_call x4 -> x2, Pallas kernels: 316 us -> 289 us  [layer_bwd(): pl.pallas_call(functools.partial(layer_bwd_kernel, layer, seq, last), out...]
    unnamed x89 -> x87, local copies, waits for them, and re-layouts: 19.9 us -> 18.3 us
where the time goes in v5:
time: 487 us; the launch traced here: 479 us
  Pallas kernels  448 us (92%)
  local copies, waits for them, and re-layouts  18.3 us (4%)
  other arithmetic  12 us (2%)
    pallas_call x2, Pallas kernels, layer_bwd(): pl.pallas_call(functools.partial(layer_bwd_kernel, layer, seq, last), out...  289 us
    pallas_call x2, Pallas kernels, attn_layer(): pl.pallas_call(functools.partial(attn_kernel, layer, seq), out_shape=out_...  69.4 us
    pallas_call x1, Pallas kernels, mlp_fwd(): pl.pallas_call(functools.partial(mlp_fwd_kernel, layer), out_shape=[jax.S...  57.8 us
    pallas_call x1, Pallas kernels, exchange(): pl.pallas_call(exchange_kernel, out_shape=[jax.ShapeDtypeStruct((2, 4, bl...  31.2 us
    unnamed x87, local copies, waits for them, and re-layouts  18.3 us

profile of v5, /device:TPU:0, one launch (start us, length us, event | category | flops | bytes accessed | tf_op | source)
XLA Modules:
  0.0 479.3 jit_solution(2337539682812992011)
XLA Ops:
  0.7 0.6 copy-done.40
  1.3 0.8 select_reduce_fusion.1.t_ref.refs_16_
  2.2 1.6 copy-done
  3.8 1.2 copy-done.1
  5.0 0.7 copy-done.3
  5.7 31.2 %exchange.1 = (bf16[2,4,128,1024]{3,2,1,0:T(8,128)(2,1)S(1)}, s32[4,2,128]{2,1,0:T(2,128)S(1)}, bf16[2,4,256,1024]{3,2,1,0:T(8,128)(2,1)S(1)}) custom-call(bf16[4,2,128,1024]{3,2,1,0:T(8,128)(2,1)S(1)} %bitcast.31, s32[4,2,128]{2,1,0:T(2,128)S(1)} %bitcast.32, bf16[2,256,1024]{2,1,0:T(8,128)(2,1)S(1)} %copy-done.1), custom_call_target="tpu_custom_call" | custom-call | tf_op jit(solution)/shard_map/exchange/pallas_call | solution.py:208
  37.0 35.8 %attn_fwd_0.1 = (bf16[2,2,2,128,1024]{4,3,2,1,0:T(8,128)(2,1)S(1)}, bf16[2,512,256]{2,1,0:T(8,128)(2,1)S(1)}, bf16[2,512,256]{2,1,0:T(8,128)(2,1)S(1)}, bf16[2,5...) custom-call(bf16[2,512,1024]{2,1,0:T(8,128)(2,1)S(1)} %bitcast.40, f32[2,1024]{1,0:T(2,128)S(1)} %copy-done.14, ...), custom_call_target="tpu_custom_call" | custom-call | flops 4294967296 | bytes 16777216 | tf_op jit(solution)/shard_map/attn_fwd_0/pallas_call | solution.py:308
  72.8 0.8 copy-done.23
  73.6 0.8 copy-done.24
  74.5 0.8 copy-done.25
  75.3 2.5 copy-done.6
  77.8 57.8 %mlp_fwd_0.1 = (bf16[2,2,2,128,1024]{4,3,2,1,0:T(8,128)(2,1)S(1)}, bf16[2,4,128,1024]{3,2,1,0:T(8,128)(2,1)S(1)}) custom-call(bf16[2,2,2,128,1024]{4,3,2,1,0:T(8,128)(2,1)S(1)} %get-tuple-element.47.x1_ref.refs_7_, bf16[4,2,128,1024]{3,2,1,0:T(8,128)(2,1)S(1)} %bitcast.39, f32[2,1024]{1,0:T(2,128)S(1)} %copy-done.15, bf16[2,704,1024]{2,1,0:T(8,128)(2,1)S(1)} %bitcast.35, ...), custom_call_target="tpu_custom_call" | custom-call | flops 5368709120 | bytes 16777216 | tf_op jit(solution)/shard_map/mlp_fwd_0/pallas_call | solution.py:378
  135.6 1.3 copy-done.18
  137.0 33.6 %attn_fwd_1.1 = (bf16[2,2,2,128,1024]{4,3,2,1,0:T(8,128)(2,1)S(1)}, bf16[2,512,256]{2,1,0:T(8,128)(2,1)S(1)}, bf16[2,512,256]{2,1,0:T(8,128)(2,1)S(1)}, bf16[2,5...) custom-call(bf16[2,512,1024]{2,1,0:T(8,128)(2,1)S(1)} %bitcast.42, f32[2,1024]{1,0:T(2,128)S(1)} %copy-done.14, ...), custom_call_target="tpu_custom_call" | custom-call | flops 4294967296 | bytes 16777216 | tf_op jit(solution)/shard_map/attn_fwd_1/pallas_call | solution.py:308
  170.6 0.8 copy-done.20
  171.4 1.3 copy-done.22
  172.7 0.8 copy-done.26
  173.5 0.8 copy-done.27
  174.3 0.8 copy-done.28
  175.1 142.6 %layer_bwd_1.1 = (bf16[2,2,2,128,1024]{4,3,2,1,0:T(8,128)(2,1)}, f32[8,1024]{1,0:T(8,128)}, bf16[4,176,1024]{2,1,0:T(8,128)(2,1)}, bf16[4,176,1024]{2,1,0:T(8,12...) custom-call(bf16[2,704,1024]{2,1,0:T(8,128)(2,1)} %bitcast.33, ...), custom_call_target="tpu_custom_call" | custom-call | flops 21474836480 | bytes 50331648 | tf_op jit(solution)/shard_map/layer_bwd_1/pallas_call | solution.py:640
  317.7 146.8 %layer_bwd_0.1 = (bf16[4,2,2,2,32,1024]{5,4,3,2,1,0:T(8,128)(2,1)}, f32[16,1024]{1,0:T(8,128)}, bf16[4,176,1024]{2,1,0:T(8,128)(2,1)}, bf16[4,176,1024]{2,1,0:T(...) custom-call(bf16[2,704,1024]{2,1,0:T(8,128)(2,1)} %bitcast.34, ...), custom_call_target="tpu_custom_call" | custom-call | flops 21474836480 | bytes 50331648 | tf_op jit(solution)/shard_map/layer_bwd_0/pallas_call | solution.py:640
  464.5 3.1 pad_maximum_fusion.1
  467.7 0.7 select_reduce_fusion
  468.4 0.6 pad_maximum_fusion.5
  469.0 1.1 pad_maximum_fusion.3
  470.1 1.1 pad_maximum_fusion.4
  471.3 1.8 pad_maximum_fusion
  473.1 1.0 copy-done.31
  474.1 0.4 copy-done.33
  474.6 0.4 copy-done.34
  475.0 2.8 maximum_bitcast_fusion
  477.8 1.3 copy.25
  (74 shorter events, 0.4 us)
Async XLA Ops:
  0.6 36.3 %copy-start.14 = (f32[2,1024]{1,0:T(2,128)S(1)}, f32[2,1024]{1,0:T(2,128)}, u32[]{:S(2)}) copy-start(f32[2,1024]{1,0:T(2,128)} %refs_14_.3) | copy-start | bytes 24580
  2.2 1.6 copy-start
  5.7 131.3 %copy-start.2 = (f32[4,1024]{1,0:T(4,128)}, f32[4,1024]{1,0:T(4,128)S(1)}, u32[]{:S(2)}) copy-start(f32[4,1024]{1,0:T(4,128)S(1)} %select_reduce_fusion.1.t_ref.refs_16_) | copy-start | bytes 49156
  5.7 31.3 %copy-start.8 = (bf16[2,1024,256]{2,1,0:T(8,128)(2,1)S(1)}, bf16[2,1024,256]{2,1,0:T(8,128)(2,1)}, u32[]{:S(2)}) copy-start(bf16[2,1024,256]{2,1,0:T(8,128)(2,1)} %refs_3_.3) | copy-start | bytes 3145732
  5.7 31.3 %copy-start.10 = (bf16[2,1024,256]{2,1,0:T(8,128)(2,1)S(1)}, bf16[2,1024,256]{2,1,0:T(8,128)(2,1)}, u32[]{:S(2)}) copy-start(bf16[2,1024,256]{2,1,0:T(8,128)(2,1)} %refs_4_.3) | copy-start | bytes 3145732
  5.7 31.3 %copy-start.12 = (bf16[2,1024,256]{2,1,0:T(8,128)(2,1)S(1)}, bf16[2,1024,256]{2,1,0:T(8,128)(2,1)}, u32[]{:S(2)}) copy-start(bf16[2,1024,256]{2,1,0:T(8,128)(2,1)} %refs_5_.3) | copy-start | bytes 3145732
  36.9 35.9 %copy-start.7 = (bf16[2,4,128,1024]{3,2,1,0:T(8,128)(2,1)}, bf16[2,4,128,1024]{3,2,1,0:T(8,128)(2,1)S(1)}, u32[]{:S(2)}) copy-start(bf16[2,4,128,1024]{3,2,1,0:T(8,128)(2,1)S(1)} %get-tuple-element.44) | copy-start | bytes 6291460
  36.9 100.0 %copy-start.16 = (s32[4,2,128]{2,1,0:T(2,128)}, s32[4,2,128]{2,1,0:T(2,128)S(1)}, u32[]{:S(2)}) copy-start(s32[4,2,128]{2,1,0:T(2,128)S(1)} %get-tuple-element.45.mask_ref.refs_17_) | copy-start | bytes 12292
  37.0 38.3 %copy-start.4 = (bf16[2,1024,704]{1,2,0:T(8,128)(2,1)S(1)}, bf16[2,1024,704]{1,2,0:T(8,128)(2,1)}, u32[]{:S(2)}) copy-start(bf16[2,1024,704]{1,2,0:T(8,128)(2,1)} %param.23) | copy-start | bytes 8650756
  37.0 38.3 %copy-start.5 = (bf16[2,1024,704]{1,2,0:T(8,128)(2,1)S(1)}, bf16[2,1024,704]{1,2,0:T(8,128)(2,1)}, u32[]{:S(2)}) copy-start(bf16[2,1024,704]{1,2,0:T(8,128)(2,1)} %param.24) | copy-start | bytes 8650756
  37.0 38.3 %copy-start.15 = (f32[2,1024]{1,0:T(2,128)S(1)}, f32[2,1024]{1,0:T(2,128)}, u32[]{:S(2)}) copy-start(f32[2,1024]{1,0:T(2,128)} %refs_15_.3) | copy-start | bytes 24580
  75.2 60.4 %copy-start.19 = (bf16[2,2,256,256]{3,2,1,0:T(8,128)(2,1)}, bf16[2,2,256,256]{3,2,1,0:T(8,128)(2,1)S(1)}, u32[]{:S(2)}) copy-start(bf16[2,2,256,256]{3,2,1,0:T(8,128)(2,1)S(1)} %get-tuple-element.59) | copy-start | bytes 1572868
  75.2 60.4 %copy-start.21 = (bf16[2,2,2,128,1024]{4,3,2,1,0:T(8,128)(2,1)}, bf16[2,2,2,128,1024]{4,3,2,1,0:T(8,128)(2,1)S(1)}, u32[]{:S(2)}) copy-start(bf16[2,2,2,128,1024]{4,3,2,1,0:T(8,128)(2,1)S(1)} %get-tuple-element.47.x1_ref.refs_7_) | copy-start | bytes 6291460
  75.3 2.5 copy-start.6
  77.8 59.2 %copy-start.9 = (bf16[2,1024,256]{2,1,0:T(8,128)(2,1)S(1)}, bf16[2,1024,256]{2,1,0:T(8,128)(2,1)}, u32[]{:S(2)}) copy-start(bf16[2,1024,256]{2,1,0:T(8,128)(2,1)} %refs_3_.3) | copy-start | bytes 3145732
  77.8 59.2 %copy-start.11 = (bf16[2,1024,256]{2,1,0:T(8,128)(2,1)S(1)}, bf16[2,1024,256]{2,1,0:T(8,128)(2,1)}, u32[]{:S(2)}) copy-start(bf16[2,1024,256]{2,1,0:T(8,128)(2,1)} %refs_4_.3) | copy-start | bytes 3145732
  77.8 59.2 %copy-start.13 = (bf16[2,1024,256]{2,1,0:T(8,128)(2,1)S(1)}, bf16[2,1024,256]{2,1,0:T(8,128)(2,1)}, u32[]{:S(2)}) copy-start(bf16[2,1024,256]{2,1,0:T(8,128)(2,1)} %refs_5_.3) | copy-start | bytes 3145732
  135.6 1.3 copy-start.18
  136.9 33.6 %copy-start.17 = (bf16[2,2,2,128,1024]{4,3,2,1,0:T(8,128)(2,1)}, bf16[2,2,2,128,1024]{4,3,2,1,0:T(8,128)(2,1)S(1)}, u32[]{:S(2)}) copy-start(bf16[2,2,2,128,1024]{4,3,2,1,0:T(8,128)(2,1)S(1)} %get-tuple-element.48) | copy-start | bytes 6291460
  464.4 3.2 copy-start.42
  464.5 3.2 copy-start.41
  464.5 4.5 copy-start.37
  464.5 4.5 copy-start.39
  467.6 2.5 copy-start.36
  467.6 2.5 copy-start.38
  469.0 2.1 copy-start.32
  469.0 2.3 copy-start.35
  471.3 1.8 copy-start.30
  471.3 2.8 copy-start.31
  471.3 3.3 copy-start.33
  471.3 3.7 copy-start.34
  475.0 2.8 copy-start.29
  (11 other events, 9.4 us)

commit v6 on v5

--- a/solution.py
+++ b/solution.py
@@ -178,44 +178,6 @@
     return inv * (d_normed - normed * jnp.mean(d_normed * normed, axis=-1, keepdims=True)), d_norm * normed
 
 
-def exchange_kernel(x_ref, mask_ref, wo_ref, xo_ref, mo_ref, wf_ref, send, recv):
-    tp, cp, z, y, x, core, ids = place()
-    names = ['x', 'core', 'xc', 'z', 'y', 'zy']
-    meet(ids, names)
-    copies, weights = [], []
-    for i, name in enumerate(names[:3]):
-        copies.append(remote(mask_ref.at[ids[name]['cp']], mo_ref.at[cp], send.at[i], recv.at[i], ids[name]))
-        copies.append(remote(x_ref.at[ids[name]['cp']], xo_ref.at[:, cp], send.at[3 + i], recv.at[3 + i], ids[name]))
-    for i, name in enumerate(names[3:]):
-        weights.append(remote(wo_ref.at[core], wf_ref.at[core, tp], send.at[6 + i], recv.at[6 + i], ids[name]))
-    mo_ref[cp] = mask_ref[cp]
-    for b in range(2):
-        xo_ref[b, cp] = x_ref[cp, b]
-    for layer in range(2):
-        wf_ref[layer, tp] = wo_ref[layer]
-    for i, name in enumerate(names[3:]):
-        weights[i].wait_recv()
-        got = wf_ref.at[core, ids[name]['tp']]
-        copies.append(remote(got, got, send.at[9 + i], recv.at[9 + i], ids['core']))
-    for copy in copies:
-        copy.wait_recv()
-    for copy in copies + weights:
-        copy.wait_send()
-
-
-def exchange(x_in, key_mask, w_o):
-    batch, blk, width = x_in.shape
-    return pl.pallas_call(
-        exchange_kernel,
-        out_shape=[jax.ShapeDtypeStruct((2, 4, blk, width), BF16), jax.ShapeDtypeStruct((4, 2, blk), jnp.int32),
-                   jax.ShapeDtypeStruct((2, 4) + w_o.shape[1:], BF16)],
-        in_specs=vmem_specs(3), out_specs=vmem_specs(3),
-        scratch_shapes=[pltpu.SemaphoreType.DMA((12,)), pltpu.SemaphoreType.DMA((12,))],
-        compiler_params=pltpu.CompilerParams(collective_id=0, has_side_effects=True, vmem_limit_bytes=40 << 20),
-        name="exchange",
-    )(x_in.reshape(4, 2, blk, width), key_mask.reshape(4, 2, blk), w_o)
-
-
 def key_add(mask_ref, b):
     row = jnp.concatenate([mask_ref[j, pl.ds(b, 1), :] for j in range(4)], axis=1)
     return jnp.where(row > 0, 0.0, MASK_NEG).astype(F32)
@@ -227,93 +189,8 @@
     return e, jnp.sum(e, axis=-1, keepdims=True)
 
 
-def attn_kernel(layer, seq, x_ref, g_ref, wq_all, wk_all, wv_all, t_ref, mask_ref, wf_all, x1_ref, q_out, k_out, v_out, o_out,
-                wq_ref, wk_ref, wv_ref, wf_ref, wsem, q_ref, k_ref, v_ref, o_ref, ssem, bias_ref, of_ref, send, recv, osend, orecv):
-    loads = load_layer(layer, [wq_all, wk_all, wv_all, wf_all], [wq_ref, wk_ref, wv_ref, wf_ref], wsem)
-    tp, cp, z, y, x, core, ids = place()
-    heads = t_ref.shape[0]
-    meet(ids, ['z', 'y', 'zy'])
-    out = []
-    for copy in loads[:3]:
-        copy.wait()
-    for step in range(2):
-        b = 1 - z if step == 0 else z
-        for half in range(2):
-            rows = pl.ds(half * 256, 256)
-            h = norm(x_ref[b, rows, :], g_ref[layer:layer + 1, :])
-            q_ref[b, rows, :] = dot(h, wq_ref[...]).astype(BF16)
-            k_ref[b, rows, :] = dot(h, wk_ref[...]).astype(BF16)
-            v_ref[b, rows, :] = dot(h, wv_ref[...]).astype(BF16)
-        add = key_add(mask_ref, b)
-        for head in range(heads):
-            if step == 0:
-                bias_ref[head] = toeplitz(t_ref[head:head + 1, :], seq)
-            cols = pl.ds(head * HEAD, HEAD)
-            e, total = exp_scores(q_ref[b, :, cols], k_ref[b, :, cols], bias_ref[head], add)
-            o = (dot(e.astype(BF16), v_ref[b, :, cols]) / total).astype(BF16)
-            o_ref[b, 0, :, cols] = o[:seq // 2]
-            o_ref[b, 1, :, cols] = o[seq // 2:]
-        if step == 0:
-            out.append(remote(o_ref.at[b, 1 - y], of_ref.at[tp], osend.at[0], orecv.at[0], ids['zy']))
-            out.append(remote(o_ref.at[b, y], of_ref.at[tp], osend.at[1], orecv.at[1], ids['z']))
-        else:
-            out.append(remote(o_ref.at[b, 1 - y], of_ref.at[tp], osend.at[2], orecv.at[2], ids['y']))
-    of_ref[tp] = o_ref[z, y]
-    saves = [pltpu.make_async_copy(src, dst, ssem.at[i]) for i, (src, dst) in
-             enumerate([(q_ref, q_out), (k_ref, k_out), (v_ref, v_out), (o_ref, o_out)])]
-    for copy in saves:
-        copy.start()
-    loads[3].wait()
-    for copy in out:
-        copy.wait_recv()
-    streams = colours(None, None, None, lambda q, c: x1_ref.at[q[0], q[1], c], send, recv, ids, z, y)
-    for c, s in enumerate(streams):
-        rows = pl.ds(c * 128, 128)
-        total = sum(dot(of_ref[j, rows, :], wf_ref[j]) for j in range(4))
-        res = x_ref[z, pl.ds(pl.multiple_of(y * 256 + c * 128, 128), 128), :].astype(F32)
-        x1_ref[z, y, c] = (res + total).astype(BF16)
-        s.publish()
-    for s in streams:
-        s.gather()
-    for s in streams:
-        s.close()
-    for copy in out:
-        copy.wait_send()
-    for copy in saves:
-        copy.wait()
-
-
-def load_layer(layer, stacks, refs, sems):
-    copies = [pltpu.make_async_copy(w.at[layer], r, sems.at[i]) for i, (w, r) in enumerate(zip(stacks, refs))]
-    for copy in copies:
-        copy.start()
-    return copies
-
-
-def layer_scratch(*stacks):
-    return [pltpu.VMEM(w.shape[1:], w.dtype) for w in stacks] + [pltpu.SemaphoreType.DMA((len(stacks),))]
-
-
 def any_specs(n):
     return [pl.BlockSpec(memory_space=pl.ANY)] * n
-
-
-def attn_layer(layer, collective_id, x, gains, w_q, w_k, w_v, table, mask, w_full):
-    seq = 512
-    width, cols = w_q.shape[1], w_q.shape[2]
-    head_shape = (2, seq, cols)
-    o_shape = (2, 2, seq // 2, cols)
-    out_shape = [jax.ShapeDtypeStruct((2, 2, 2, 128, width), BF16)] + [jax.ShapeDtypeStruct(h, BF16) for h in [head_shape] * 3 + [o_shape]]
-    dma = pltpu.SemaphoreType.DMA
-    return pl.pallas_call(
-        functools.partial(attn_kernel, layer, seq),
-        out_shape=out_shape, in_specs=vmem_specs(2) + any_specs(3) + vmem_specs(2) + any_specs(1), out_specs=vmem_specs(1) + any_specs(4),
-        scratch_shapes=layer_scratch(w_q, w_k, w_v, w_full) + [pltpu.VMEM(head_shape, BF16)] * 3 + [pltpu.VMEM(o_shape, BF16), dma((4,))]
-        + [pltpu.VMEM((table.shape[0], seq, seq), F32), pltpu.VMEM((4, 256, cols), BF16), dma((2, 6)), dma((2, 6)), dma((3,)), dma((3,))],
-        compiler_params=pltpu.CompilerParams(collective_id=collective_id, has_side_effects=True, vmem_limit_bytes=40 << 20),
-        cost_estimate=pl.CostEstimate(flops=4 << 30, bytes_accessed=16 << 20, transcendentals=0),
-        name=f"attn_fwd_{layer}",
-    )(x.reshape(2, seq, width), gains, w_q, w_k, w_v, table, mask, w_full)
 
 
 def gelu_parts(g):
@@ -328,62 +205,182 @@
     return [(1 - z, 1 - y), (1 - z, y), (z, 1 - y), (z, y)]
 
 
-def mlp_fwd_kernel(layer, x1_ref, dy_ref, g_ref, wg_all, wl_all, wo_all, out_ref, dyo_ref, wg_ref, wl_ref, wo_ref, wsem,
-                   part, near, far, send, recv, dsend, drecv, own_sem):
-    loads = load_layer(layer, [wg_all, wl_all, wo_all], [wg_ref, wl_ref, wo_ref], wsem)
+def sum_scratch(width, blocks=()):
+    return [pltpu.VMEM((2, 2, 2) + blocks, F32), pltpu.VMEM((2, 2) + blocks, F32), pltpu.VMEM((2,) + blocks, F32)]
+
+
+def forward_kernel(seq, *refs):
+    refs = list(refs)
+    take = lambda n: [refs.pop(0) for _ in range(n)]
+    x_in, d_y, wo_in, wq_in, wk_in, wv_in, wg_in, wl_in, wd_in, mask_in, ga_ref, gm_ref, t_ref = take(13)
+    x0_out, a0_out, x1_out, a1_out, dy_out, q_out, k_out, v_out, o_out, mask_ref = take(10)
+    x0_ref, a0_ref, x1_ref, a1_ref, dyo_ref, q_ref, k_ref, v_ref, o_ref = take(9)
+    wq_ref, wk_ref, wv_ref, wg_ref, wl_ref, wd_ref, wf_ref = take(7)
+    bias_ref, of_ref, part, near, far = take(5)
+    xsend, xrecv, osend, orecv, send, recv, lsem, ssem = refs
     tp, cp, z, y, x, core, ids = place()
-    meet(ids, ['z', 'y', 'x', 'core', 'xc'])
-    moves = [remote(dy_ref.at[ids[name]['cp']], dyo_ref.at[:, cp], dsend.at[i], drecv.at[i], ids[name])
-             for i, name in enumerate(['x', 'xc', 'core'])]
-    own = pltpu.make_async_copy(dy_ref.at[cp], dyo_ref.at[:, cp], own_sem)
-    own.start()
-    for copy in loads:
+    near_by, far_by = ['core', 'x', 'xc'], ['z', 'y', 'zy']
+
+    def local(src, dst, sem):
+        copy = pltpu.make_async_copy(src, dst, sem)
+        copy.start()
+        return copy
+
+    own_x = local(x_in.at[cp], x0_ref.at[:, cp], lsem.at[0])
+    qkv_loads = [local(w, r, lsem.at[1 + i]) for i, (w, r) in enumerate([(wq_in, wq_ref), (wk_in, wk_ref), (wv_in, wv_ref)])]
+    own_w = [local(wo_in.at[layer], wf_ref.at[layer, tp], lsem.at[4 + layer]) for layer in range(2)]
+    mlp_loads = [local(w.at[0], r, lsem.at[6 + i]) for i, (w, r) in enumerate([(wg_in, wg_ref), (wl_in, wl_ref), (wd_in, wd_ref)])]
+    own_dy = local(d_y.at[cp], dyo_ref, lsem.at[9])
+    meet(ids, near_by + far_by)
+    masks, xs = [], []
+    for i, name in enumerate(near_by):
+        masks.append(remote(mask_in.at[ids[name]['cp']], mask_ref.at[cp], xsend.at[i], xrecv.at[i], ids[name]))
+        xs.append(remote(x_in.at[ids[name]['cp']], x0_ref.at[:, cp], xsend.at[3 + i], xrecv.at[3 + i], ids[name]))
+    weights = [remote(wo_in.at[core], wf_ref.at[core, tp], xsend.at[6 + i], xrecv.at[6 + i], ids[name]) for i, name in enumerate(far_by)]
+    mask_ref[cp] = mask_in[cp]
+    for head in range(t_ref.shape[0]):
+        bias_ref[head] = toeplitz(t_ref[head:head + 1, :], seq)
+
+    def project(layer, rows):
+        h = norm(rows, ga_ref[layer:layer + 1, :])
+        return [dot(h, w[layer]).astype(BF16) for w in (wq_ref, wk_ref, wv_ref)]
+
+    def attention(layer, b):
+        add = key_add(mask_ref, b)
+        for head in range(t_ref.shape[0]):
+            cols = pl.ds(head * HEAD, HEAD)
+            e, total = exp_scores(q_ref[layer, b, :, cols], k_ref[layer, b, :, cols], bias_ref[head], add)
+            o = (dot(e.astype(BF16), v_ref[layer, b, :, cols]) / total).astype(BF16)
+            o_ref[layer, b, 0, :, cols] = o[:seq // 2]
+            o_ref[layer, b, 1, :, cols] = o[seq // 2:]
+
+    def ship(layer, name, b, half):
+        i = layer * 3 + far_by.index(name)
+        return remote(o_ref.at[layer, b, half], of_ref.at[layer, tp], osend.at[i], orecv.at[i], ids[name])
+
+    def project_out(layer, sent, residual, out_ref):
+        of_ref[layer, tp] = o_ref[layer, z, y]
+        for copy in sent:
+            copy.wait_recv()
+        streams = colours(None, None, None, lambda q, c: out_ref.at[q[0], q[1], c], send.at[4 * layer:4 * layer + 2], recv.at[4 * layer:4 * layer + 2], ids, z, y)
+        for c, s in enumerate(streams):
+            rows = pl.ds(c * 128, 128)
+            total = sum(dot(of_ref[layer, j, rows, :], wf_ref[layer, j]) for j in range(4))
+            out_ref[z, y, c] = (residual(c).astype(F32) + total).astype(BF16)
+            s.publish()
+        for s in streams:
+            s.gather()
+        for s in streams:
+            s.close()
+
+    for copy in qkv_loads:
         copy.wait()
-    zy, yz = streams = colours(part, near, far, lambda q, c: out_ref.at[q[0], q[1], c], send, recv, ids, z, y)
-
-    def compute(q):
-        h2 = norm(x1_ref[q].reshape(256, -1), g_ref[layer:layer + 1, :])
+    for i, name in enumerate(['own'] + near_by):
+        if i == 0:
+            own_x.wait()
+            blk = cp
+        else:
+            xs[i - 1].wait_recv()
+            blk = ids[name]['cp']
+        for d_ref, value in zip((q_ref, k_ref, v_ref), project(0, x0_ref[:, blk].reshape(2 * 128, -1))):
+            for b in range(2):
+                d_ref[0, b, pl.ds(pl.multiple_of(blk * 128, 128), 128), :] = value[b * 128:(b + 1) * 128]
+    own_dy.wait()
+    saves = [local(x0_ref, x0_out, ssem.at[0]), local(dyo_ref, dy_out.at[:, cp], ssem.at[1])]
+    moves = [remote(d_y.at[ids[name]['cp']], dy_out.at[:, cp], xsend.at[12 + i], xrecv.at[12 + i], ids[name]) for i, name in enumerate(near_by)]
+    for copy in masks:
+        copy.wait_recv()
+    attention(0, 1 - z)
+    sent = [ship(0, 'zy', 1 - z, 1 - y), ship(0, 'z', 1 - z, y)]
+    passed = []
+    for i, name in enumerate(far_by):
+        weights[i].wait_recv()
+        got = wf_ref.at[core, ids[name]['tp']]
+        passed.append(remote(got, got, xsend.at[9 + i], xrecv.at[9 + i], ids['core']))
+    attention(0, z)
+    sent.append(ship(0, 'y', z, 1 - y))
+    for copy in own_w:
+        copy.wait()
+    for copy in passed:
+        copy.wait_recv()
+    project_out(0, sent, lambda c: x0_ref[z, y * 2 + c], a0_ref)
+    saves.append(local(a0_ref, a0_out, ssem.at[2]))
+
+    for copy in mlp_loads:
+        copy.wait()
+    zy, yz = streams = colours(part, near, far, lambda q, c: x1_ref.at[q[0], q[1], c], send.at[2:4], recv.at[2:4], ids, z, y)
+
+    def mlp_quarter(q):
+        h2 = norm(a0_ref[q].reshape(256, -1), gm_ref[0:1, :])
         gated = (gelu_parts(dot(h2, wg_ref[...], NT))[0] * dot(h2, wl_ref[...], NT)).astype(BF16)
-        part[q] = dot(gated, wo_ref[...]).reshape(part.shape[2:])
+        part[q] = dot(gated, wd_ref[...]).reshape(part.shape[2:])
 
     quarters = order(z, y)
-    compute(quarters[0])
+    mlp_quarter(quarters[0])
     zy.send_away(0)
     yz.send_away(0)
-    compute(quarters[1])
+    mlp_quarter(quarters[1])
     zy.send_away(1)
-    compute(quarters[2])
+    mlp_quarter(quarters[2])
     yz.send_away(1)
-    compute(quarters[3])
+    mlp_quarter(quarters[3])
     for s in streams:
         s.forward()
     for c, s in enumerate(streams):
-        out_ref[z, y, c] = (x1_ref[z, y, c].astype(F32) + s.total()).astype(BF16)
+        x1_ref[z, y, c] = (a0_ref[z, y, c].astype(F32) + s.total()).astype(BF16)
         s.publish()
     for s in streams:
         s.gather()
     for s in streams:
         s.close()
-    for copy in moves + [own]:
+    saves.append(local(x1_ref, x1_out, ssem.at[3]))
+
+    late = []
+    for step in range(2):
+        b = 1 - z if step == 0 else z
+        for half in range(2):
+            rows = pl.ds(half * 256, 256)
+            for d_ref, value in zip((q_ref, k_ref, v_ref), project(1, x1_ref[b, half].reshape(256, -1))):
+                d_ref[1, b, rows, :] = value
+        attention(1, b)
+        if step == 0:
+            late += [ship(1, 'zy', b, 1 - y), ship(1, 'z', b, y)]
+        else:
+            late.append(ship(1, 'y', b, 1 - y))
+    saves += [local(src, dst, ssem.at[4 + i]) for i, (src, dst) in enumerate([(q_ref, q_out), (k_ref, k_out), (v_ref, v_out), (o_ref, o_out)])]
+    project_out(1, late, lambda c: x1_ref[z, y, c], a1_ref)
+    saves.append(local(a1_ref, a1_out, ssem.at[8]))
+    for copy in masks + xs + weights + passed + sent + late:
+        copy.wait_send()
+    for copy in moves + saves:
         copy.wait()
 
 
-def sum_scratch(width, blocks=()):
-    return [pltpu.VMEM((2, 2, 2) + blocks, F32), pltpu.VMEM((2, 2) + blocks, F32), pltpu.VMEM((2,) + blocks, F32)]
-
-
-def mlp_fwd(layer, collective_id, x1, d_y, gains, wg_t, wl_t, w_out):
+def forward(x_in, d_y, key_mask, gains_a, gains_m, w_q, w_k, w_v, w_o, wg_t, wl_t, w_out, table):
+    batch, blk, width = x_in.shape
+    seq, cols = 4 * blk, w_q.shape[2]
     dma = pltpu.SemaphoreType.DMA
-    width = x1.shape[-1]
+    blocks = (2, 2, 2, blk, width)
+    arrived = (2, 4, blk, width)
+    heads = (2, 2, seq, cols)
+    halves = (2, 2, 2, seq // 2, cols)
+    hbm = [arrived, blocks, blocks, blocks, arrived, heads, heads, heads, halves]
+    operands = [x_in.reshape(4, 2, blk, width), d_y.reshape(4, 2, blk, width), w_o, w_q, w_k, w_v, wg_t, wl_t, w_out,
+                key_mask.reshape(4, 2, blk), gains_a, gains_m, table]
+    scratch = [pltpu.VMEM(h, BF16) for h in hbm[:4] + [(2, blk, width)] + hbm[5:]]
+    scratch += [pltpu.VMEM(w.shape, BF16) for w in (w_q, w_k, w_v)] + [pltpu.VMEM(w.shape[1:], BF16) for w in (wg_t, wl_t, w_out)]
+    scratch += [pltpu.VMEM((2, 4) + w_o.shape[1:], BF16), pltpu.VMEM((table.shape[0], seq, seq), F32), pltpu.VMEM((2, 4, 2 * blk, cols), BF16)]
+    scratch += sum_scratch(0, blocks[3:])
+    scratch += [dma((15,)), dma((15,)), dma((6,)), dma((6,)), dma((6, 6)), dma((6, 6)), dma((10,)), dma((9,))]
     return pl.pallas_call(
-        functools.partial(mlp_fwd_kernel, layer),
-        out_shape=[jax.ShapeDtypeStruct(x1.shape, BF16), jax.ShapeDtypeStruct((2, 4, 128, width), BF16)],
-        in_specs=vmem_specs(3) + any_specs(3), out_specs=vmem_specs(1) + any_specs(1),
-        scratch_shapes=layer_scratch(wg_t, wl_t, w_out) + sum_scratch(0, x1.shape[3:]) + [dma((2, 6)), dma((2, 6)), dma((3,)), dma((3,)), dma],
-        compiler_params=pltpu.CompilerParams(collective_id=collective_id, has_side_effects=True, vmem_limit_bytes=40 << 20),
-        cost_estimate=pl.CostEstimate(flops=5 << 30, bytes_accessed=16 << 20, transcendentals=0),
-        name=f"mlp_fwd_{layer}",
-    )(x1, d_y.reshape(4, 2, 128, width), gains, wg_t, wl_t, w_out)
+        functools.partial(forward_kernel, seq),
+        out_shape=[jax.ShapeDtypeStruct(h, BF16) for h in hbm] + [jax.ShapeDtypeStruct((4, 2, blk), jnp.int32)],
+        in_specs=any_specs(9) + vmem_specs(4), out_specs=any_specs(9) + vmem_specs(1),
+        scratch_shapes=scratch,
+        compiler_params=pltpu.CompilerParams(collective_id=0, has_side_effects=True, vmem_limit_bytes=62 << 20),
+        cost_estimate=pl.CostEstimate(flops=15 << 30, bytes_accessed=48 << 20, transcendentals=0),
+        name="forward",
+    )(*operands)
 
 
 def layer_bwd_kernel(layer, seq, last, *refs):
@@ -408,7 +405,7 @@
         own_ref, acc_small, got_small, csend, crecv = take(5)
     tp, cp, z, y, x, core, ids = place()
     w_loads = [pltpu.make_async_copy(w.at[layer], r, wsem.at[i]) for i, (w, r) in enumerate(zip(stacks, weights))]
-    a_loads = [pltpu.make_async_copy(w, r, hsem.at[i]) for i, (w, r) in enumerate(zip(arrays, holds))]
+    a_loads = [pltpu.make_async_copy(w if i < 3 else w.at[layer], r, hsem.at[i]) for i, (w, r) in enumerate(zip(arrays, holds))]
     first_loads = [a_loads[0], w_loads[0], w_loads[1], a_loads[1], w_loads[2]]
     later_loads = a_loads[2:] + w_loads[3:]
     for copy in first_loads + later_loads:
@@ -475,7 +472,6 @@
     g_gate.finish()
     for s in mlp_sum:
         s.gather()
-    g_out.gather()
     for s in mlp_sum:
         s.close()
 
@@ -526,6 +522,7 @@
     grad_into(p_o, o_ref[...].reshape(2 * seq, -1), dm_ref[...].reshape(2 * seq, width))
     g_o.send_both()
     g_lin.finish()
+    g_out.gather()
     attend(z, 1)
     attn_quarter(quarters[2])
     yz.send_away(1)
@@ -623,13 +620,13 @@
     dma = pltpu.SemaphoreType.DMA
     blocks = (2, 2, 2, 128, width)
     stacks = [wg_t, wl_t, w_out, w_q, w_k, w_v, w_o]
-    arrays = [x1.reshape(blocks), dy.reshape(blocks), x.reshape(2, seq, width), q, k, v, o.reshape(2, seq, cols)]
+    arrays = [x1.reshape(blocks), dy.reshape(blocks), x.reshape(2, seq, width), q, k, v, o.reshape(2, 2, seq, cols)]
     operands = stacks + arrays + [gains_a, gains_m, table, mask] + ([small] if last else [])
     in_specs = any_specs(14) + vmem_specs(5 if last else 4)
     out_shape = [jax.ShapeDtypeStruct((4, 2, 2, 2, 32, width) if last else blocks, BF16), jax.ShapeDtypeStruct((16 if last else 8, width), F32)]
     grads = [(ff // 4, width)] * 3 + [(cols // 4, width)] + [(width // 4, cols)] * 3
     out_shape += [jax.ShapeDtypeStruct((4,) + g, BF16) for g in grads]
-    scratch = [pltpu.VMEM(w.shape[1:], BF16) for w in stacks] + [pltpu.VMEM(a.shape, BF16) for a in arrays] + [dma((7,)), dma((7,))]
+    scratch = [pltpu.VMEM(w.shape[1:], BF16) for w in stacks] + [pltpu.VMEM(a.shape if i < 3 else a.shape[1:], BF16) for i, a in enumerate(arrays)] + [dma((7,)), dma((7,))]
     scratch += sum_scratch(0, blocks[3:]) + [pltpu.VMEM(blocks, BF16), pltpu.VMEM((rows, width), BF16)] + [pltpu.VMEM((rows, ff), BF16)] * 3
     scratch += [pltpu.VMEM((seq, seq), F32), pltpu.VMEM((seq, cols), BF16)] + [pltpu.VMEM((2, seq, cols), BF16)] * 3 + [pltpu.VMEM((8, 2 * seq), F32)]
     for g in grads:
@@ -659,19 +656,14 @@
 
     def local_program(x_in, d_y, key_mask, rel_bias, g_attn, g_mlp, w_q, w_k, w_v, w_o, w_gate, w_lin, w_out):
         width = x_in.shape[2]
-        quarters = (2, 2, 2, 128, width)
         onehot = bucket_onehot(512)
         table = jnp.sum(jnp.where(onehot[None], rel_bias.T[:, :, None], 0.0), axis=1)
         wg_t, wl_t = jnp.swapaxes(w_gate, 1, 2), jnp.swapaxes(w_lin, 1, 2)
-        x0, mask, w_full = exchange(x_in, key_mask, w_o)
-
-        a0, q0, k0, v0, o0 = attn_layer(0, 1, x0, g_attn, w_q, w_k, w_v, table, mask, w_full)
-        x1, dy = mlp_fwd(0, 2, a0, d_y, g_mlp, wg_t, wl_t, w_out)
-        a1, q1, k1, v1, o1 = attn_layer(1, 3, x1, g_attn, w_q, w_k, w_v, table, mask, w_full)
+        x0, a0, x1, a1, dy, q, k, v, o, mask = forward(x_in, d_y, key_mask, g_attn, g_mlp, w_q, w_k, w_v, w_o, wg_t, wl_t, w_out, table)
 
         rest = (g_attn, g_mlp, wg_t, wl_t, w_out, w_q, w_k, w_v, w_o, table, mask)
-        dx, small, out1, gate1, lin1, wo1, wq1, wk1, wv1 = layer_bwd(1, 4, a1, dy, x1, q1, k1, v1, o1, *rest)
-        d_x, small, out0, gate0, lin0, wo0, wq0, wk0, wv0 = layer_bwd(0, 5, a0, dx, x0, q0, k0, v0, o0, *rest, small)
+        dx, small, out1, gate1, lin1, wo1, wq1, wk1, wv1 = layer_bwd(1, 4, a1, dy, x1, q, k, v, o, *rest)
+        d_x, small, out0, gate0, lin0, wo0, wq0, wk0, wv0 = layer_bwd(0, 5, a0, dx, x0, q, k, v, o, *rest, small)
 
         def both(first, second, like, swap=False):
             shape = (like.shape[2], like.shape[1]) if swap else like.shape[1:]

time: 487 us -> 451 us (0.926)
  Pallas kernels: 448 us -> 424 us
  local copies, waits for them, and re-layouts: 18.3 us -> 4.03 us
    pallas_call x2, Pallas kernels: 289 us -> 274 us  [layer_bwd(): pl.pallas_call(functools.partial(layer_bwd_kernel, layer, seq, last), out...]
    unnamed x87 -> x29, local copies, waits for them, and re-layouts: 18.3 us -> 4.01 us
    pallas_call x4 -> x1, Pallas kernels: 158 us -> 150 us  [forward(): pl.pallas_call(functools.partial(forward_kernel, seq), out_shape=[jax.Sha...]
where the time goes in v6:
time: 451 us; the launch traced here: 442 us
  Pallas kernels  424 us (94%)
  other arithmetic  12.7 us (3%)
    pallas_call x2, Pallas kernels, layer_bwd(): pl.pallas_call(functools.partial(layer_bwd_kernel, layer, seq, last), out...  274 us
    pallas_call x1, Pallas kernels, forward(): pl.pallas_call(functools.partial(forward_kernel, seq), out_shape=[jax.Sha...  150 us

profile of v6, /device:TPU:0, one launch (start us, length us, event | category | flops | bytes accessed | tf_op | source)
XLA Modules:
  0.0 441.8 jit_solution(14191477256182782857)
XLA Ops:
  0.7 0.0 copy-start.11
  0.7 0.6 copy-done.11
  1.3 1.4 select_reduce_fusion.1.refs_12_.refs_16_
  2.8 149.8 %forward.1 = (bf16[2,4,128,1024]{3,2,1,0:T(8,128)(2,1)}, bf16[2,2,2,128,1024]{4,3,2,1,0:T(8,128)(2,1)}, bf16[2,2,2,128,1024]{4,3,2,1,0:T(8,128)(2,1)}, bf16[2,2,...) custom-call(bf16[4,2,128,1024]{3,2,1,0:T(8,128)(2,1)} %bitcast.53, ...), custom_call_target="tpu_custom_call" | custom-call | flops 16106127360 | bytes 50331648 | tf_op jit(solution)/shard_map/forward/pallas_call | solution.py:375
  152.6 129.9 %layer_bwd_1.1 = (bf16[2,2,2,128,1024]{4,3,2,1,0:T(8,128)(2,1)}, f32[8,1024]{1,0:T(8,128)}, bf16[4,176,1024]{2,1,0:T(8,128)(2,1)}, bf16[4,176,1024]{2,1,0:T(8,12...) custom-call(bf16[2,704,1024]{2,1,0:T(8,128)(2,1)} %bitcast.48, ...), custom_call_target="tpu_custom_call" | custom-call | flops 21474836480 | bytes 50331648 | tf_op jit(solution)/shard_map/layer_bwd_1/pallas_call | solution.py:637
  282.5 144.2 %layer_bwd_0.1 = (bf16[4,2,2,2,32,1024]{5,4,3,2,1,0:T(8,128)(2,1)}, f32[16,1024]{1,0:T(8,128)}, bf16[4,176,1024]{2,1,0:T(8,128)(2,1)}, bf16[4,176,1024]{2,1,0:T(...) custom-call(bf16[2,704,1024]{2,1,0:T(8,128)(2,1)} %bitcast.49, ...), custom_call_target="tpu_custom_call" | custom-call | flops 21474836480 | bytes 50331648 | tf_op jit(solution)/shard_map/layer_bwd_0/pallas_call | solution.py:637
  426.7 0.0 copy-start.13
  426.7 0.0 copy-start.12
  426.7 0.0 copy-start.8
  426.7 0.0 copy-start.10
  426.7 3.1 pad_maximum_fusion.1
  429.9 0.0 copy-done.13
  429.9 0.0 copy-done.12
  429.9 0.7 select_reduce_fusion
  430.6 0.6 pad_maximum_fusion.5
  431.2 0.0 copy-done.8
  431.2 0.0 copy-done.10
  431.2 0.0 copy-start.6
  431.3 1.1 pad_maximum_fusion.3
  432.3 0.0 copy-done.7
  432.3 0.0 copy-done.9
  432.3 1.1 pad_maximum_fusion.4
  433.4 0.0 copy-done.3
  433.4 0.2 copy-done.6
  433.6 1.8 pad_maximum_fusion
  435.4 0.0 copy-done.1
  435.4 1.0 copy-done.2
  436.4 0.4 copy-done.4
  436.8 0.4 copy-done.5
  437.3 2.8 maximum_bitcast_fusion
  440.0 0.0 copy-done
  440.1 1.3 copy.25
  (13 shorter events, 0.1 us)
Async XLA Ops:
  0.7 0.6 copy-start.11
  426.7 3.2 copy-start.13
  426.7 3.2 copy-start.12
  426.7 4.5 %copy-start.8 = (bf16[4,256,256]{2,1,0:T(8,128)(2,1)S(1)}, bf16[4,256,256]{2,1,0:T(8,128)(2,1)}, u32[]{:S(2)}) copy-start(bf16[4,256,256]{2,1,0:T(8,128)(2,1)} %get-tuple-element.58) | copy-start | bytes 1572868
  426.7 4.5 %copy-start.10 = (bf16[4,256,256]{2,1,0:T(8,128)(2,1)S(1)}, bf16[4,256,256]{2,1,0:T(8,128)(2,1)}, u32[]{:S(2)}) copy-start(bf16[4,256,256]{2,1,0:T(8,128)(2,1)} %get-tuple-element.57) | copy-start | bytes 1572868
  429.9 2.5 copy-start.7
  429.9 2.5 copy-start.9
  431.2 2.1 copy-start.3
  431.2 2.3 copy-start.6
  433.6 1.8 copy-start.1
  433.6 2.8 copy-start.2
  433.6 3.3 copy-start.4
  433.6 3.7 copy-start.5
  437.3 2.8 copy-start
